TPU v7x, 8 devices: a whole 2x2x1 slice. The times are simulated.
8 devices in a mesh: dp: 2 (over z, y), tp: 4 (over x, core).
Axes of the slice: x: 2, y: 2, z: 1, core: 2. Of those that a mesh axis runs over, the one named last changes fastest.
Arguments:
- node_lat: bfloat16 [2, 2562, 512], P('dp', None, 'tp')
- edge_lat: bfloat16 [2, 20460, 512], P('dp', None, 'tp')
- senders: int32 [20460], replicated
- receivers: int32 [20460], replicated
- grad_node: bfloat16 [2, 2562, 512], P('dp', None, 'tp')
- grad_edge: bfloat16 [2, 20460, 512], P('dp', None, 'tp')
- edge_w1: bfloat16 [2, 3, 512, 512], P(None, None, 'tp')
- edge_b1: float32 [2, 512], replicated
- edge_w2: bfloat16 [2, 512, 512], P(None, None, 'tp')
- edge_vec: float32 [2, 3, 512], P(None, None, 'tp')
- node_w1: bfloat16 [2, 2, 512, 512], P(None, None, 'tp')
- node_b1: float32 [2, 512], replicated
- node_w2: bfloat16 [2, 512, 512], P(None, None, 'tp')
- node_vec: float32 [2, 3, 512], P(None, None, 'tp')
Outputs:
- output 1: bfloat16 [2, 2562, 512], P('dp', None, 'tp')
- output 2: bfloat16 [2, 20460, 512], P('dp', None, 'tp')
- output 3: bfloat16 [2, 2562, 512], P('dp', None, 'tp')
- output 4: bfloat16 [2, 20460, 512], P('dp', None, 'tp')
- output 5: float32 [2, 3, 512, 512], P(None, None, 'tp')
- output 6: float32 [2, 512], replicated
- output 7: float32 [2, 512, 512], P(None, None, 'tp')
- output 8: float32 [2, 3, 512], P(None, None, 'tp')
- output 9: float32 [2, 2, 512, 512], P(None, None, 'tp')
- output 10: float32 [2, 512], replicated
- output 11: float32 [2, 512, 512], P(None, None, 'tp')
- output 12: float32 [2, 3, 512], P(None, None, 'tp')
All inputs are finite; a program needn't handle non-finite values.
Results may differ from a plain program's by a relative error of at most 0.02.
Values sent between devices are 32-bit elements.
A program may use at most 1 GiB of HBM per device.

v0:
```python
import jax
import jax.numpy as jnp
from jax import lax
from jax.sharding import PartitionSpec as P

LN_EPS = 1e-5


def swish_grad(hidden):
    sigmoid_h = jax.nn.sigmoid(hidden)
    return sigmoid_h * (1.0 + hidden * (1.0 - sigmoid_h))


def seg_sum(msg_rows, seg_ids, num_segments):
    def one_sample(sample_rows):
        return jax.ops.segment_sum(sample_rows, seg_ids, num_segments=num_segments)
    return jax.vmap(one_sample)(msg_rows)


def mlp_forward(inputs, w_first, b_first, w_second, norm_vec):
    part_sum = jnp.einsum('bri,ih->brh', inputs[0], w_first[0], preferred_element_type=jnp.float32)
    for block_id in range(1, len(inputs)):
        part_sum = part_sum + jnp.einsum('bri,ih->brh', inputs[block_id], w_first[block_id], preferred_element_type=jnp.float32)
    hidden = lax.psum(part_sum, 'tp') + b_first
    act_bf = jax.nn.silu(hidden).astype(jnp.bfloat16)
    out_f32 = jnp.einsum('brh,ho->bro', act_bf, w_second, preferred_element_type=jnp.float32) + norm_vec[0]
    full_width = w_second.shape[0]
    row_mean = lax.psum(jnp.sum(out_f32, axis=-1, keepdims=True), 'tp') / full_width
    centered = out_f32 - row_mean
    row_var = lax.psum(jnp.sum(centered * centered, axis=-1, keepdims=True), 'tp') / full_width
    inv_std = lax.rsqrt(row_var + LN_EPS)
    normed = centered * inv_std
    message = (normed * norm_vec[1] + norm_vec[2]).astype(jnp.bfloat16)
    return message, (hidden, normed, inv_std)


def mlp_backward(d_message, inputs, w_first, w_second, norm_vec, saved):
    hidden, normed, inv_std = saved
    full_width = w_second.shape[0]
    d_gamma = jnp.sum(d_message * normed, axis=(0, 1))
    d_beta = jnp.sum(d_message, axis=(0, 1))
    d_normed = d_message * norm_vec[1]
    row_stats = lax.psum(jnp.stack([jnp.sum(d_normed, axis=-1), jnp.sum(d_normed * normed, axis=-1)], axis=-1), 'tp') / full_width
    d_out = inv_std * (d_normed - row_stats[..., 0:1] - normed * row_stats[..., 1:2])
    d_out_bf = d_out.astype(jnp.bfloat16)
    act_bf = jax.nn.silu(hidden).astype(jnp.bfloat16)
    d_w_second = jnp.einsum('brh,bro->ho', act_bf, d_out_bf, preferred_element_type=jnp.float32)
    d_act = lax.psum(jnp.einsum('bro,ho->brh', d_out_bf, w_second, preferred_element_type=jnp.float32), 'tp')
    d_hidden = d_act * swish_grad(hidden)
    d_hidden_bf = d_hidden.astype(jnp.bfloat16)
    d_w_first = jnp.stack([jnp.einsum('bri,brh->ih', x_in, d_hidden_bf, preferred_element_type=jnp.float32) for x_in in inputs])
    d_inputs = [jnp.einsum('brh,ih->bri', d_hidden_bf, w_first[block_id], preferred_element_type=jnp.float32) for block_id in range(len(inputs))]
    d_vec = jnp.stack([jnp.sum(d_out, axis=(0, 1)), d_gamma, d_beta])
    return d_inputs, (d_w_first, jnp.sum(d_hidden, axis=(0, 1)), d_w_second, d_vec)


def layer_forward(node_lat, edge_lat, senders, receivers, layer_par):
    send_lat = jnp.take(node_lat, senders, axis=1)
    recv_lat = jnp.take(node_lat, receivers, axis=1)
    edge_inputs = (edge_lat, send_lat, recv_lat)
    edge_msg, edge_saved = mlp_forward(edge_inputs, layer_par[0], layer_par[1], layer_par[2], layer_par[3])
    node_agg = seg_sum(edge_msg.astype(jnp.float32), receivers, node_lat.shape[1]).astype(jnp.bfloat16)
    node_inputs = (node_lat, node_agg)
    node_msg, node_saved = mlp_forward(node_inputs, layer_par[4], layer_par[5], layer_par[6], layer_par[7])
    new_node = (node_lat.astype(jnp.float32) + node_msg.astype(jnp.float32)).astype(jnp.bfloat16)
    new_edge = (edge_lat.astype(jnp.float32) + edge_msg.astype(jnp.float32)).astype(jnp.bfloat16)
    return new_node, new_edge, (edge_inputs, edge_saved, node_inputs, node_saved)


def layer_backward(d_node_out, d_edge_out, senders, receivers, layer_par, layer_saved):
    edge_inputs, edge_saved, node_inputs, node_saved = layer_saved
    d_node = d_node_out.astype(jnp.float32)
    d_edge = d_edge_out.astype(jnp.float32)
    node_din, node_grads = mlp_backward(d_node, node_inputs, layer_par[4], layer_par[6], layer_par[7], node_saved)
    d_edge_msg = d_edge + jnp.take(node_din[1], receivers, axis=1)
    edge_din, edge_grads = mlp_backward(d_edge_msg, edge_inputs, layer_par[0], layer_par[2], layer_par[3], edge_saved)
    num_nodes = d_node.shape[1]
    d_node_in = d_node + node_din[0] + seg_sum(edge_din[1], senders, num_nodes) + seg_sum(edge_din[2], receivers, num_nodes)
    d_edge_in = d_edge + edge_din[0]
    return d_node_in.astype(jnp.bfloat16), d_edge_in.astype(jnp.bfloat16), edge_grads + node_grads


def solution(mesh):
    lat_spec = P('dp', None, 'tp')
    first_spec = P(None, None, 'tp', None)
    col_spec = P(None, None, 'tp')
    param_specs = (first_spec, P(), col_spec, col_spec, first_spec, P(), col_spec, col_spec)
    in_specs = (lat_spec, lat_spec, P(), P(), lat_spec, lat_spec) + param_specs
    out_specs = (lat_spec, lat_spec, lat_spec, lat_spec) + param_specs

    def local_step(node_lat, edge_lat, senders, receivers, grad_node, grad_edge, edge_w1, edge_b1, edge_w2, edge_vec, node_w1, node_b1, node_w2, node_vec):
        params = (edge_w1, edge_b1, edge_w2, edge_vec, node_w1, node_b1, node_w2, node_vec)
        num_layers = edge_w1.shape[0]
        saved_all = []
        for layer_id in range(num_layers):
            layer_par = tuple(par_arr[layer_id] for par_arr in params)
            node_lat, edge_lat, layer_saved = layer_forward(node_lat, edge_lat, senders, receivers, layer_par)
            saved_all.append(layer_saved)
        d_node = grad_node
        d_edge = grad_edge
        grads_rev = []
        for layer_id in reversed(range(num_layers)):
            layer_par = tuple(par_arr[layer_id] for par_arr in params)
            d_node, d_edge, layer_grads = layer_backward(d_node, d_edge, senders, receivers, layer_par, saved_all[layer_id])
            grads_rev.append(layer_grads)
        grads_fwd = grads_rev[::-1]
        param_grads = tuple(
            lax.psum(jnp.stack([layer_grads[par_id] for layer_grads in grads_fwd]), 'dp')
            for par_id in range(len(params)))
        return (node_lat, edge_lat, d_node, d_edge) + param_grads

    return jax.shard_map(local_step, mesh=mesh, in_specs=in_specs, out_specs=out_specs, check_vma=False)
```

profile of v0, /device:TPU:0, one launch (start us, length us, event | category | flops | bytes accessed | tf_op | source)
XLA Modules:
  0.0 5126.6 jit_solution(4138233751328340899)
XLA Ops:
  11.6 72.2 %gather_fusion.1 = bf16[20460,128]{1,0:T(8,128)(2,1)} fusion(bf16[2562,128]{1,0:T(8,128)(2,1)S(1)} %bitcast.593, s32[20480]{0:T(1024)S(1)} %pad_clamp_fusion), kind=kCustom, calls=%fused_computation.2.clone | custom fusion | bytes 10557360 | tf_op jit(solution)/shard_map/jit(_take)/gather | solution.py:59
  83.9 72.5 %gather_fusion = bf16[20460,128]{1,0:T(8,128)(2,1)} fusion(bf16[2562,128]{1,0:T(8,128)(2,1)S(1)} %bitcast.594, s32[20480]{0:T(1024)S(1)} %pad_clamp_fusion.1), kind=kCustom, calls=%fused_computation.clone | custom fusion | bytes 10557360 | tf_op jit(solution)/shard_map/jit(_take)/gather | solution.py:58
  156.4 18.8 fusion.66
  175.1 16.5 fusion.63
  191.7 43.3 add_bitcast_fusion.1
  240.0 686.0 %all-reduce.18.cloned.1.call-done = f32[1,20460,512]{2,1,0:T(8,128)} async-done(((f32[1,20460,512]{2,1,0:T(8,128)}), f32[1,20460,512]{2,1,0:T(8,128)}) %all-reduce.18.cloned.1.call-update) | async-done | bytes 41902096 | tf_op jit(solution)/shard_map/psum | solution.py:24
  926.0 25.2 multiply_convert_fusion.1
  965.0 25.3 all-reduce.20.cloned.1.call-done
  1000.8 25.6 all-reduce.22.cloned.1.call-done
  1027.4 109.4 %scatter_custom_fusion = f32[2562,128]{1,0:T(8,128)S(1)} fusion(s32[20460]{0:T(1024)} %param.21, f32[]{:T(128)} %constant.52.clone.1, f32[20460,128]{1,0:T(8,128)} %get-tuple-element.109, f32[128]{0:T(128)S(1)} %get-tuple-element.103, f32[128]{0:T(128)S(1)} %get-tuple-element.104, f32[20460]{0:T(1024)S(1)} %bitcast.608, f32[20460]{0:T(1024)S(1)} %bitcast.602), kind=kCustom, calls=%fused_computation.62 | custom fusion | flops 18332160 | bytes 11954528 | tf_op jit(solution)/shard_map/vmap()/scatter-add | solution.py:16
  1143.1 19.8 fusion.58
  1162.9 77.6 %all-reduce.24.cloned.1.call-done = f32[1,2562,512]{2,1,0:T(8,128)} async-done(((f32[1,2562,512]{2,1,0:T(8,128)}), f32[1,2562,512]{2,1,0:T(8,128)}) %all-reduce.24.cloned.1.call-update) | async-done | bytes 5246992 | tf_op jit(solution)/shard_map/psum | solution.py:24
  1270.0 72.3 %gather_fusion.2 = bf16[20460,128]{1,0:T(8,128)(2,1)} fusion(bf16[2562,128]{1,0:T(8,128)(2,1)S(1)} %bitcast.591, s32[20480]{0:T(1024)S(1)} %copy-done.55), kind=kCustom, calls=%fused_computation.3.clone | custom fusion | bytes 10557360 | tf_op jit(solution)/shard_map/jit(_take)/gather | solution.py:58
  1342.3 72.1 %gather_fusion.3 = bf16[20460,128]{1,0:T(8,128)(2,1)} fusion(bf16[2562,128]{1,0:T(8,128)(2,1)S(1)} %bitcast.592, s32[20480]{0:T(1024)S(1)} %copy-done.37), kind=kCustom, calls=%fused_computation.4.clone | custom fusion | bytes 10557360 | tf_op jit(solution)/shard_map/jit(_take)/gather | solution.py:59
  1414.4 16.5 fusion.55
  1431.0 43.3 add_bitcast_fusion
  1474.4 688.5 %all-reduce.26.cloned.1.call-done = f32[1,20460,512]{2,1,0:T(8,128)} async-done(((f32[1,20460,512]{2,1,0:T(8,128)}), f32[1,20460,512]{2,1,0:T(8,128)}) %all-reduce.26.cloned.1.call-update) | async-done | bytes 41902096 | tf_op jit(solution)/shard_map/psum | solution.py:24
  2162.9 25.2 multiply_convert_fusion
  2201.0 26.1 all-reduce.28.cloned.1.call-done
  2240.5 22.8 all-reduce.30.cloned.1.call-done
  2264.4 19.3 fusion.40
  2283.6 110.6 %scatter_custom_fusion.1 = f32[2562,128]{1,0:T(8,128)S(1)} fusion(s32[20460]{0:T(1024)} %param.21, bf16[20460,128]{1,0:T(8,128)(2,1)} %get-tuple-element.85, f32[]{:T(128)} %constant.52.clone.1), kind=kCustom, calls=%fused_computation.59 | custom fusion | flops 5237760 | bytes 6551040 | tf_op jit(solution)/shard_map/vmap()/scatter-add | solution.py:16
  2400.4 97.4 %all-reduce.32.cloned.1.call-done = f32[1,2562,512]{2,1,0:T(8,128)} async-done(((f32[1,2562,512]{2,1,0:T(8,128)}), f32[1,2562,512]{2,1,0:T(8,128)}) %all-reduce.32.cloned.1.call-update) | async-done | bytes 5246992 | tf_op jit(solution)/shard_map/psum | solution.py:24
  2545.3 97.9 %all-reduce.34.cloned.1.call-done = f32[1,2562,512]{2,1,0:T(8,128)} async-done(((f32[1,2562,512]{2,1,0:T(8,128)}), f32[1,2562,512]{2,1,0:T(8,128)}) %all-reduce.34.cloned.1.call-update) | async-done | bytes 5246992 | tf_op jit(solution)/shard_map/psum | solution.py:48
  2651.2 68.1 %gather_fusion.4 = f32[20460,128]{1,0:T(8,128)} fusion(f32[2562,128]{1,0:T(8,128)S(1)} %fusion.83, s32[20480]{0:T(1024)S(1)} %copy-done.37), kind=kCustom, calls=%fused_computation.1.clone | custom fusion | bytes 21032880 | tf_op jit(solution)/shard_map/jit(_take)/gather | solution.py:75
  2719.3 26.4 fusion.47
  2746.6 26.5 all-reduce.36.cloned.1.call-done
  2774.2 19.0 fusion.271
  2795.6 16.1 convolution_bitcast_fusion.1
  2814.8 685.1 %all-reduce.38.cloned.1.call-done = f32[1,20460,512]{2,1,0:T(8,128)} async-done(((f32[1,20460,512]{2,1,0:T(8,128)}), f32[1,20460,512]{2,1,0:T(8,128)}) %all-reduce.38.cloned.1.call-update) | async-done | bytes 41902096 | tf_op jit(solution)/shard_map/psum | solution.py:48
  3499.9 34.7 fusion.274
  3559.0 110.7 %scatter_custom_fusion.3 = f32[2562,128]{1,0:T(8,128)} fusion(s32[20460]{0:T(1024)} %param.21, f32[20460,128]{1,0:T(8,128)} %fusion.23, f32[]{:T(128)} %constant.52.clone.1), kind=kCustom, calls=%fused_computation.219 | custom fusion | flops 2618880 | bytes 1312256 | tf_op jit(solution)/shard_map/vmap()/scatter-add | solution.py:16
  3669.7 110.2 %scatter_fusion = f32[2562,128]{1,0:T(8,128)S(1)} fusion(f32[2562,128]{1,0:T(8,128)S(1)} %fusion.69, s32[20460]{0:T(1024)S(1)} %copy-done.39, f32[20460,128]{1,0:T(8,128)} %fusion.25), kind=kCustom, calls=%fused_computation.8 | custom fusion | flops 2618880 | bytes 31508400 | tf_op jit(solution)/shard_map/vmap()/scatter-add | solution.py:16
  3803.4 98.4 %all-reduce.40.cloned.1.call-done = f32[1,2562,512]{2,1,0:T(8,128)} async-done(((f32[1,2562,512]{2,1,0:T(8,128)}), f32[1,2562,512]{2,1,0:T(8,128)}) %all-reduce.40.cloned.1.call-update) | async-done | bytes 5246992 | tf_op jit(solution)/shard_map/psum | solution.py:48
  3910.8 68.2 %gather_fusion.5 = f32[20460,128]{1,0:T(8,128)} fusion(f32[2562,128]{1,0:T(8,128)S(1)} %fusion.76, s32[20480]{0:T(1024)S(1)} %copy-done.38), kind=kCustom, calls=%fused_computation.5.clone | custom fusion | bytes 21032880 | tf_op jit(solution)/shard_map/jit(_take)/gather | solution.py:75
  3979.0 28.0 fusion.43
  4008.1 26.3 all-reduce.42.cloned.1.call-done
  4035.5 18.5 fusion.269
  4056.4 16.2 convolution_bitcast_fusion
  4094.7 15.9 fusion.147
  4110.5 15.9 fusion.152
  4126.5 19.6 fusion.142
  4162.3 598.6 %all-reduce.44.cloned.1.call-done = f32[1,20460,512]{2,1,0:T(8,128)} async-done(((f32[1,20460,512]{2,1,0:T(8,128)}), f32[1,20460,512]{2,1,0:T(8,128)}) %all-reduce.44.cloned.1.call-update) | async-done | bytes 41902096 | tf_op jit(solution)/shard_map/psum | solution.py:48
  4760.8 34.1 fusion.273
  4795.0 21.7 fusion.162
  4875.9 109.9 %scatter_custom_fusion.5 = f32[2562,128]{1,0:T(8,128)S(1)} fusion(s32[20460]{0:T(1024)} %param.21, f32[20460,128]{1,0:T(8,128)} %fusion.12, f32[]{:T(128)} %constant.52.clone.1), kind=kCustom, calls=%fused_computation.217 | custom fusion | flops 2618880 | bytes 1312256 | tf_op jit(solution)/shard_map/vmap()/scatter-add | solution.py:16
  4985.8 110.1 %scatter_fusion.1 = f32[2562,128]{1,0:T(8,128)S(1)} fusion(f32[2562,128]{1,0:T(8,128)S(1)} %fusion.71, s32[20460]{0:T(1024)S(1)} %copy-done.40, f32[20460,128]{1,0:T(8,128)} %fusion.14), kind=kCustom, calls=%fused_computation.10 | custom fusion | flops 2618880 | bytes 31508400 | tf_op jit(solution)/shard_map/vmap()/scatter-add | solution.py:16
  5096.9 15.5 fusion.4
  (357 shorter events, 333.2 us)
Async XLA Ops:
  7.2 918.8 %all-reduce.18.cloned.1.call-start = ((), (), s32[]{:S(2)}) async-start(), calls=%async_computation | async-start | bytes 83820544 | tf_op jit(solution)/shard_map/psum | solution.py:24
  8.2 1406.2 %copy-start.58 = (pred[20460]{0:T(1024)(128)(4,1)}, pred[20460]{0:T(1024)(128)(4,1)S(1)}, u32[]{:S(2)}) copy-start(pred[20460]{0:T(1024)(128)(4,1)S(1)} %compare_and_fusion.1) | copy-start | bytes 61384
  10.0 1420.9 %copy-start.51 = (pred[20460]{0:T(1024)(128)(4,1)}, pred[20460]{0:T(1024)(128)(4,1)S(1)}, u32[]{:S(2)}) copy-start(pred[20460]{0:T(1024)(128)(4,1)S(1)} %compare_and_fusion) | copy-start | bytes 61384
  11.0 72.9 %copy-start.54 = (s32[20480]{0:T(1024)}, s32[20480]{0:T(1024)S(1)}, u32[]{:S(2)}) copy-start(s32[20480]{0:T(1024)S(1)} %pad_clamp_fusion.1) | copy-start | bytes 245764
  83.9 72.5 %copy-start.31 = (bf16[2,3,128,512]{3,2,1,0:T(8,128)(2,1)S(1)}, bf16[2,3,128,512]{3,2,1,0:T(8,128)(2,1)}, u32[]{:S(2)}) copy-start(bf16[2,3,128,512]{3,2,1,0:T(8,128)(2,1)} %param.24) | copy-start | bytes 2359300
  235.0 755.2 %all-reduce.20.cloned.1.call-start = ((), (), s32[]{:S(2)}) async-start(), calls=%async_computation.1 | async-start | bytes 163840 | tf_op jit(solution)/shard_map/psum | solution.py:28
  236.3 2028.0 %copy-start.65 = (f32[128]{0:T(128)}, f32[128]{0:T(128)S(1)}, u32[]{:S(2)}) copy-start(f32[128]{0:T(128)S(1)} %get-tuple-element.104) | copy-start | bytes 1540
  236.3 2028.0 %copy-start.73 = (f32[128]{0:T(128)}, f32[128]{0:T(128)S(1)}, u32[]{:S(2)}) copy-start(f32[128]{0:T(128)S(1)} %get-tuple-element.103) | copy-start | bytes 1540
  236.8 689.2 %copy-start.67 = (f32[1,512]{1,0:T(1,128)}, f32[1,512]{1,0:T(1,128)S(1)}, u32[]{:S(2)}) copy-start(f32[1,512]{1,0:T(1,128)S(1)} %get-tuple-element.95) | copy-start | bytes 6148
  964.1 62.3 %all-reduce.22.cloned.1.call-start = ((), (), s32[]{:S(2)}) async-start(), calls=%async_computation.2 | async-start | bytes 163840 | tf_op jit(solution)/shard_map/psum | solution.py:30
  965.0 275.5 %copy-start.70 = (f32[1,512]{1,0:T(1,128)}, f32[1,512]{1,0:T(1,128)S(1)}, u32[]{:S(2)}) copy-start(f32[1,512]{1,0:T(1,128)S(1)} %get-tuple-element.93) | copy-start | bytes 6148
  991.2 1273.1 %copy-start.27 = (f32[1,20460,1]{1,2,0:T(1,128)}, f32[1,20460,1]{1,2,0:T(1,128)S(1)}, u32[]{:S(2)}) copy-start(f32[1,20460,1]{1,2,0:T(1,128)S(1)} %broadcast_multiply_fusion.3) | copy-start | bytes 245524
  1000.2 240.2 %all-reduce.24.cloned.1.call-start = ((), (), s32[]{:S(2)}) async-start(), calls=%async_computation.3 | async-start | bytes 10518528 | tf_op jit(solution)/shard_map/psum | solution.py:24
  1000.8 267.6 %copy-start.78 = (f32[128]{0:T(128)}, f32[128]{0:T(128)S(1)}, u32[]{:S(2)}) copy-start(f32[128]{0:T(128)S(1)} %get-tuple-element.99) | copy-start | bytes 1540
  1027.4 1236.9 %copy-start.29 = (f32[1,20460,1]{1,2,0:T(1,128)}, f32[1,20460,1]{1,2,0:T(1,128)S(1)}, u32[]{:S(2)}) copy-start(f32[1,20460,1]{1,2,0:T(1,128)S(1)} %add_rsqrt_fusion.1) | copy-start | bytes 245524
  1143.0 1019.9 %all-reduce.26.cloned.1.call-start = ((), (), s32[]{:S(2)}) async-start(), calls=%async_computation.4 | async-start | bytes 83820544 | tf_op jit(solution)/shard_map/psum | solution.py:24
  1162.9 83.0 %copy-start.45 = (bf16[2,512,128]{2,1,0:T(8,128)(2,1)S(1)}, bf16[2,512,128]{2,1,0:T(8,128)(2,1)}, u32[]{:S(2)}) copy-start(bf16[2,512,128]{2,1,0:T(8,128)(2,1)} %param.30) | copy-start | bytes 786436
  1246.9 95.4 %copy-start.10 = (f32[2562,128]{1,0:T(8,128)}, f32[2562,128]{1,0:T(8,128)S(1)}, u32[]{:S(2)}) copy-start(f32[2562,128]{1,0:T(8,128)S(1)} %get-tuple-element.111) | copy-start | bytes 3935236
  1257.1 85.2 %copy-start.60 = (f32[2562]{0:T(1024)}, f32[2562]{0:T(1024)S(1)}, u32[]{:S(2)}) copy-start(f32[2562]{0:T(1024)S(1)} %multiply_reduce_fusion.7) | copy-start | bytes 30748
  1270.0 1267.8 %copy-start = (bf16[1,2562,128]{2,1,0:T(8,128)(2,1)}, bf16[1,2562,128]{2,1,0:T(8,128)(2,1)S(1)}, u32[]{:S(2)}) copy-start(bf16[1,2562,128]{2,1,0:T(8,128)(2,1)S(1)} %fusion.113) | copy-start | bytes 1967620
  1270.0 72.3 %copy-start.37 = (s32[20480]{0:T(1024)S(1)}, s32[20480]{0:T(1024)}, u32[]{:S(2)}) copy-start(s32[20480]{0:T(1024)} %copy-done.36) | copy-start | bytes 245764
  1474.3 688.6 %copy-start.69 = (f32[1,512]{1,0:T(1,128)S(1)}, f32[1,512]{1,0:T(1,128)}, u32[]{:S(2)}) copy-start(f32[1,512]{1,0:T(1,128)} %get-tuple-element.94) | copy-start | bytes 6148
  1474.3 752.8 %all-reduce.28.cloned.1.call-start = ((), (), s32[]{:S(2)}) async-start(), calls=%async_computation.5 | async-start | bytes 163840 | tf_op jit(solution)/shard_map/psum | solution.py:28
  2201.0 62.3 %all-reduce.30.cloned.1.call-start = ((), (), s32[]{:S(2)}) async-start(), calls=%async_computation.6 | async-start | bytes 163840 | tf_op jit(solution)/shard_map/psum | solution.py:30
  2237.2 260.6 %all-reduce.32.cloned.1.call-start = ((), (), s32[]{:S(2)}) async-start(), calls=%async_computation.7 | async-start | bytes 10518528 | tf_op jit(solution)/shard_map/psum | solution.py:24
  2400.3 97.5 %copy-start.72 = (f32[1,512]{1,0:T(1,128)S(1)}, f32[1,512]{1,0:T(1,128)}, u32[]{:S(2)}) copy-start(f32[1,512]{1,0:T(1,128)} %get-tuple-element.92) | copy-start | bytes 6148
  2400.3 102.8 %copy-start.46 = (bf16[2,512,128]{2,1,0:T(8,128)(2,1)S(1)}, bf16[2,512,128]{2,1,0:T(8,128)(2,1)}, u32[]{:S(2)}) copy-start(bf16[2,512,128]{2,1,0:T(8,128)(2,1)} %param.30) | copy-start | bytes 786436
  2400.3 102.8 %copy-start.83 = (f32[128]{0:T(128)S(1)}, f32[128]{0:T(128)}, u32[]{:S(2)}) copy-start(f32[128]{0:T(128)} %get-tuple-element.97) | copy-start | bytes 1540
  2400.3 242.8 %all-reduce.34.cloned.1.call-start = ((), (), s32[]{:S(2)}) async-start(), calls=%async_computation.8 | async-start | bytes 10518528 | tf_op jit(solution)/shard_map/psum | solution.py:48
  2503.1 34.7 copy-start.93
  2545.2 105.1 %copy-start.35 = (bf16[2,2,128,512]{3,2,1,0:T(8,128)(2,1)S(1)}, bf16[2,2,128,512]{3,2,1,0:T(8,128)(2,1)}, u32[]{:S(2)}) copy-start(bf16[2,2,128,512]{3,2,1,0:T(8,128)(2,1)} %param.28) | copy-start | bytes 1572868
  2545.2 227.9 %all-reduce.36.cloned.1.call-start = ((), (), s32[]{:S(2)}) async-start(), calls=%async_computation.9 | async-start | bytes 327680 | tf_op jit(solution)/shard_map/psum | solution.py:43
  2651.2 68.1 %copy-start.52 = (pred[20460]{0:T(1024)(128)(4,1)S(1)}, pred[20460]{0:T(1024)(128)(4,1)}, u32[]{:S(2)}) copy-start(pred[20460]{0:T(1024)(128)(4,1)} %copy-done.51) | copy-start | bytes 61384
  2746.5 753.4 %all-reduce.38.cloned.1.call-start = ((), (), s32[]{:S(2)}) async-start(), calls=%async_computation.10 | async-start | bytes 83820544 | tf_op jit(solution)/shard_map/psum | solution.py:48
  2811.7 1090.0 %all-reduce.40.cloned.1.call-start = ((), (), s32[]{:S(2)}) async-start(), calls=%async_computation.11 | async-start | bytes 10518528 | tf_op jit(solution)/shard_map/psum | solution.py:48
  3546.8 122.9 %copy-start.39 = (s32[20460]{0:T(1024)S(1)}, s32[20460]{0:T(1024)}, u32[]{:S(2)}) copy-start(s32[20460]{0:T(1024)} %param.20) | copy-start | bytes 245524
  3669.7 112.5 %copy-start.11 = (f32[2562,128]{1,0:T(8,128)S(1)}, f32[2562,128]{1,0:T(8,128)}, u32[]{:S(2)}) copy-start(f32[2562,128]{1,0:T(8,128)} %copy-done.10) | copy-start | bytes 3935236
  3669.7 112.5 %copy-start.79 = (f32[128]{0:T(128)S(1)}, f32[128]{0:T(128)}, u32[]{:S(2)}) copy-start(f32[128]{0:T(128)} %copy-done.78) | copy-start | bytes 1540
  3800.1 101.6 %copy-start.71 = (f32[1,512]{1,0:T(1,128)S(1)}, f32[1,512]{1,0:T(1,128)}, u32[]{:S(2)}) copy-start(f32[1,512]{1,0:T(1,128)} %copy-done.70) | copy-start | bytes 6148
  3803.4 231.0 %all-reduce.42.cloned.1.call-start = ((), (), s32[]{:S(2)}) async-start(), calls=%async_computation.12 | async-start | bytes 327680 | tf_op jit(solution)/shard_map/psum | solution.py:43
  3910.8 68.2 %copy-start.28 = (f32[1,20460,1]{1,2,0:T(1,128)S(1)}, f32[1,20460,1]{1,2,0:T(1,128)}, u32[]{:S(2)}) copy-start(f32[1,20460,1]{1,2,0:T(1,128)} %copy-done.27) | copy-start | bytes 245524
  3910.8 68.2 %copy-start.30 = (f32[1,20460,1]{1,2,0:T(1,128)S(1)}, f32[1,20460,1]{1,2,0:T(1,128)}, u32[]{:S(2)}) copy-start(f32[1,20460,1]{1,2,0:T(1,128)} %copy-done.29) | copy-start | bytes 245524
  3910.8 68.2 %copy-start.53 = (pred[20460]{0:T(1024)(128)(4,1)S(1)}, pred[20460]{0:T(1024)(128)(4,1)}, u32[]{:S(2)}) copy-start(pred[20460]{0:T(1024)(128)(4,1)} %copy-done.51) | copy-start | bytes 61384
  3910.8 68.2 %copy-start.66 = (f32[128]{0:T(128)S(1)}, f32[128]{0:T(128)}, u32[]{:S(2)}) copy-start(f32[128]{0:T(128)} %copy-done.65) | copy-start | bytes 1540
  4007.8 753.0 %all-reduce.44.cloned.1.call-start = ((), (), s32[]{:S(2)}) async-start(), calls=%async_computation.13 | async-start | bytes 83820544 | tf_op jit(solution)/shard_map/psum | solution.py:48
  4072.7 1039.7 %all-reduce.46.cloned.1.call-start = ((), (), s32[]{:S(2)}) async-start(), calls=%async_computation.14 | async-start | bytes 7340032 | tf_op jit(solution)/shard_map/psum | solution.py:108
  4151.3 609.5 %copy-start.68 = (f32[1,512]{1,0:T(1,128)S(1)}, f32[1,512]{1,0:T(1,128)}, u32[]{:S(2)}) copy-start(f32[1,512]{1,0:T(1,128)} %copy-done.67) | copy-start | bytes 6148
  4853.4 132.3 %copy-start.40 = (s32[20460]{0:T(1024)S(1)}, s32[20460]{0:T(1024)}, u32[]{:S(2)}) copy-start(s32[20460]{0:T(1024)} %param.20) | copy-start | bytes 245524
  (76 other events, 863.4 us)
Sparse Core Ops, SparseCore 0:
  235.1 690.8 all-reduce.17
  964.2 25.9 all-reduce.19
  1000.4 25.9 all-reduce.21
  1143.1 97.2 all-reduce.23
  1474.5 688.3 all-reduce.25
  2201.1 25.9 all-reduce.27
  2237.3 25.9 all-reduce.29
  2400.4 97.2 all-reduce.31
  2545.3 97.7 all-reduce.33
  2746.6 26.3 all-reduce.35
  2811.9 688.0 all-reduce.37
  3803.5 98.2 all-reduce.39
  4007.9 26.3 all-reduce.41
  4072.8 687.9 all-reduce.43
  4853.5 91.7 all-reduce.45
where the time goes:
time: 5140 us; the launch traced here: 5130 us
  waiting for transfers between devices  3180 us (62%)
  other arithmetic  934 us (18%)
  matrix products  471 us (9%)
  local copies, waits for them, and re-layouts  451 us (9%)
  blocking collectives  70.6 us (1%)
    psum x4, waiting for transfers between devices, mlp_forward(): hidden = lax.psum(part_sum, 'tp') + b_first  1550 us
    psum x4, waiting for transfers between devices, mlp_backward(): lax.psum(jnp.einsum('bro,ho->brh', d_out_bf, w_second, preferred_element_...  1480 us
    scatter-add x6, other arithmetic, one_sample(): return jax.ops.segment_sum(sample_rows, seg_ids, num_segments=num_segments)  661 us
    gather x2, local copies, waits for them, and re-layouts, layer_forward(): send_lat = jnp.take(node_lat, senders, axis=1)  145 us
    gather x2, local copies, waits for them, and re-layouts, layer_forward(): recv_lat = jnp.take(node_lat, receivers, axis=1)  144 us
    gather x2, local copies, waits for them, and re-layouts, layer_backward(): d_edge_msg = d_edge + jnp.take(node_din[1], receivers, axis=1)  136 us
    dot_general x6, matrix products, mlp_forward(): jnp.einsum('bri,ih->brh', inputs[block_id], w_first[block_id], preferred_...  132 us
  transfers between devices with their start and end apart: 15, of which 14 were waited for; matrix products, arithmetic and copies ran while one was open for 7% of the time, Pallas kernels for 0%

commit v1 on v0

v1 whole, which is shorter than its diff:
```python
import functools

import jax
import jax.numpy as jnp
from jax import lax
from jax.experimental import pallas as pl
from jax.experimental.pallas import tpu as pltpu
from jax.sharding import PartitionSpec as P

LN_EPS = 1e-5
F32 = jnp.float32
BF16 = jnp.bfloat16
LANES = 128
EDGE_BLK = 256
NODE_BLK = 368
GATHER_UNROLL = 16
ALL = Ellipsis
FULL = (slice(None), slice(None))
VMEM_BYTES = 64 * 2**20 - 2**16


WORK = 4 * 10**9


def slot_views(pair_a, pair_b):
    return pair_a.at[0], pair_b.at[0], pair_a.at[1], pair_b.at[1]


def dot(lhs, rhs):
    return lax.dot_general(lhs, rhs, (((1,), (0,)), ((), ())), preferred_element_type=F32)


def dot_tb(lhs, rhs):
    return lax.dot_general(lhs, rhs, (((1,), (1,)), ((), ())), preferred_element_type=F32)


def dot_ta(lhs, rhs):
    return lax.dot_general(lhs, rhs, (((0,), (0,)), ((), ())), preferred_element_type=F32)


def col(val, slot):
    return val[:, slot * LANES:(slot + 1) * LANES]


def gather_rows(tables, index_refs, base, out_ref, num_rows):
    def step(it, carry):
        for sub in range(GATHER_UNROLL):
            row = it * GATHER_UNROLL + sub
            acc = None
            for table, index_ref in zip(tables, index_refs):
                val = table[pl.ds(pl.multiple_of(index_ref[base + row], 4), 4), :]
                acc = val if acc is None else acc + val
            out_ref[pl.ds(pl.multiple_of(row * 4, 4), 4), :] = acc
        return carry
    lax.fori_loop(0, num_rows // GATHER_UNROLL, step, 0)


def scatter_rows(accs, index_refs, base, src_ref, num_rows, copies, stride):
    def step(it, carry):
        pending = []
        for sub in range(copies):
            row = it * copies + sub
            val = src_ref[pl.ds(pl.multiple_of(row * 4, 4), 4), :]
            for acc, index_ref in zip(accs, index_refs):
                at = pl.multiple_of(index_ref[base + row] + sub * stride, 4)
                pending.append((acc, at, acc[pl.ds(at, 4), :] + val))
        for acc, at, val in pending:
            acc[pl.ds(at, 4), :] = val
        return carry
    lax.fori_loop(0, num_rows // copies, step, 0)


def zero_rows(ref, rows, step_rows):
    def step(it, carry):
        ref[pl.ds(pl.multiple_of(it * step_rows, 8), step_rows), :] = jnp.zeros((step_rows, LANES), F32)
        return carry
    lax.fori_loop(0, rows // step_rows, step, 0)


def row_mean(val):
    return jnp.sum(val, axis=-1, keepdims=True) * (1.0 / val.shape[-1])


def mlp_tail(hidden, w2t, vec_ref):
    act = (hidden * jax.nn.sigmoid(hidden)).astype(BF16)
    out = dot_tb(act, w2t) + vec_ref[0:1, :]
    centered = out - row_mean(out)
    inv_std = lax.rsqrt(row_mean(centered * centered) + LN_EPS)
    normed = centered * inv_std
    message = (normed * vec_ref[1:2, :] + vec_ref[2:3, :]).astype(BF16)
    return act, normed, inv_std, message


def mlp_back(d_message, hidden, normed, inv_std, w2t, vec_ref):
    d_normed = d_message * vec_ref[1:2, :]
    d_out = inv_std * (d_normed - row_mean(d_normed) - normed * row_mean(d_normed * normed))
    d_out_bf = d_out.astype(BF16)
    sig = jax.nn.sigmoid(hidden)
    act = (hidden * sig).astype(BF16)
    d_act = dot(d_out_bf, w2t)
    d_hidden = d_act * (sig * (1.0 + hidden * (1.0 - sig)))
    sums = [jnp.sum(x, axis=0, keepdims=True) for x in (d_out, d_message * normed, d_message, d_hidden)]
    return d_out_bf, act, d_hidden, sums


def add_to(ref, idx, val, first):
    @pl.when(first)
    def _():
        ref[idx] = val

    @pl.when(jnp.logical_not(first))
    def _():
        ref[idx] += val


def call(body, grid, in_specs, out_specs, out_shape, scratch, name, prefetch=0, work=1):
    return pl.pallas_call(
        body,
        out_shape=out_shape,
        grid_spec=pltpu.PrefetchScalarGridSpec(
            num_scalar_prefetch=prefetch, grid=grid, in_specs=in_specs, out_specs=out_specs, scratch_shapes=scratch),
        compiler_params=pltpu.CompilerParams(vmem_limit_bytes=VMEM_BYTES, dimension_semantics=("arbitrary",) * len(grid)),
        cost_estimate=pl.CostEstimate(flops=work * WORK, bytes_accessed=work * WORK // 1000, transcendentals=0),
        name=name)


def rows_spec(blk, width):
    return pl.BlockSpec((blk, width), lambda i, *_: (i, 0))


def whole_spec(shape):
    zeros = (0,) * len(shape)
    return pl.BlockSpec(shape, lambda i, *_: zeros, pipeline_mode=pl.Buffered(1))


def pair_spec(blk):
    return pl.BlockSpec((2, blk, LANES), lambda i, *_: (0, i, 0))


def sds(shape, dtype):
    return jax.ShapeDtypeStruct(shape, dtype)


def edge_fwd_body(n_in, last, pad_nodes, copies, snd_ref, rcv_ref, *refs):
    x_refs = refs[:n_in]
    ps_ref, pr_ref, w1_ref, w2t_ref, vec_ref, hid_ref, nrm_ref, inv_ref = refs[n_in:n_in + 8]
    n_out = 4 if last else 1
    new_refs = refs[n_in + 8:n_in + 8 + n_out]
    sa_ref, sb_ref, gat_ref, msg_ref, acc_ref = refs[n_in + 8 + n_out:]
    step = pl.program_id(0)
    base = step * EDGE_BLK
    stride = 4 * pad_nodes

    @pl.when(step == 0)
    def _():
        zero_rows(acc_ref, stride * copies, stride // 4)

    gather_rows((ps_ref, pr_ref), (snd_ref, rcv_ref), base, gat_ref, EDGE_BLK)
    x_in = jnp.concatenate([ref[ALL].astype(BF16) for ref in x_refs], axis=-1)
    part = dot(x_in, w1_ref[ALL])
    hidden = jnp.concatenate(
        [col(part, slot) + gat_ref[pl.ds(slot, EDGE_BLK, stride=4), :] for slot in range(4)], axis=-1)
    hid_ref[ALL] = hidden
    _, normed, inv_std, message = mlp_tail(hidden, w2t_ref[ALL], vec_ref)
    nrm_ref[ALL] = normed
    inv_ref[ALL] = jnp.broadcast_to(inv_std, (EDGE_BLK, LANES))
    msg = message.astype(F32)
    new = (x_in.astype(F32) + msg).astype(BF16)
    if last:
        for slot in range(4):
            new_refs[slot][ALL] = col(new, slot).astype(new_refs[slot].dtype)
    else:
        new_refs[0][ALL] = new
    for slot in range(4):
        msg_ref[pl.ds(slot, EDGE_BLK, stride=4), :] = col(msg, slot)
    scatter_rows((acc_ref,), (rcv_ref,), base, msg_ref, EDGE_BLK, copies, stride)

    @pl.when(step == pl.num_programs(0) - 1)
    def _():
        def fin(it, carry):
            for slot, out in enumerate(slot_views(sa_ref, sb_ref)):
                total = acc_ref[pl.ds(it * (4 * NODE_BLK) + slot, NODE_BLK, stride=4), :]
                for cp in range(1, copies):
                    total = total + acc_ref[pl.ds(it * (4 * NODE_BLK) + slot + cp * stride, NODE_BLK, stride=4), :]
                out[pl.ds(pl.multiple_of(it * NODE_BLK, 8), NODE_BLK), :] = total
            return carry
        lax.fori_loop(0, pad_nodes // NODE_BLK, fin, 0)


def edge_forward(snd, rcv, xs, ps, pr, w1, w2t, vec, last, pad_nodes):
    rows, width = snd.shape[0], w1.shape[0]
    copies = 4
    n_in = len(xs)
    slot_shapes = [sds((rows, LANES), BF16)] + [sds((rows, LANES), F32)] * 3
    new_shapes = slot_shapes if last else [sds((rows, width), BF16)]
    outs = [sds((rows, width), F32), sds((rows, width), F32), sds((rows, LANES), F32)] + new_shapes
    outs += [sds((2, pad_nodes, LANES), F32)] * 2
    in_specs = [rows_spec(EDGE_BLK, x.shape[1]) for x in xs]
    in_specs += [whole_spec(a.shape) for a in (ps, pr, w1, w2t, vec)]
    out_specs = [rows_spec(EDGE_BLK, o.shape[1]) for o in outs[:-2]] + [whole_spec(o.shape) for o in outs[-2:]]
    scratch = [pltpu.VMEM((4 * EDGE_BLK, LANES), F32), pltpu.VMEM((4 * EDGE_BLK, LANES), F32),
               pltpu.VMEM((copies * 4 * pad_nodes, LANES), F32)]
    return call(functools.partial(edge_fwd_body, n_in, last, pad_nodes, copies), (rows // EDGE_BLK,), in_specs, out_specs,
                outs, scratch, "edge_fwd", prefetch=2, work=12)(snd, rcv, *xs, ps, pr, w1, w2t, vec)


def edge_bwd_body(n_in, last, pad_nodes, copies, snd_ref, rcv_ref, *refs):
    n_g = 4 if last else 1
    g_refs = refs[:n_g]
    x_refs = refs[n_g:n_g + n_in]
    hid_ref, nrm_ref, inv_ref, ds_ref, w1_ref, w2t_ref, vec_ref = refs[n_g + n_in:n_g + n_in + 7]
    rest = refs[n_g + n_in + 7:]
    n_out = 1 if last else 4
    d_refs = rest[:n_out]
    dw1_ref, dw2t_ref, small_ref, ts_ref, tr_ref, gat_ref, dh_ref, accs_ref, accr_ref = rest[n_out:]
    step = pl.program_id(0)
    base = step * EDGE_BLK
    stride = 4 * pad_nodes
    first = step == 0

    @pl.when(first)
    def _():
        zero_rows(accs_ref, stride * copies, stride // 4)
        zero_rows(accr_ref, stride * copies, stride // 4)

    gather_rows((ds_ref,), (rcv_ref,), base, gat_ref, EDGE_BLK)
    d_edge = jnp.concatenate([ref[ALL].astype(F32) for ref in g_refs], axis=-1)
    d_message = jnp.concatenate(
        [col(d_edge, slot) + gat_ref[pl.ds(slot, EDGE_BLK, stride=4), :] for slot in range(4)], axis=-1)
    d_out_bf, act, d_hidden, sums = mlp_back(
        d_message, hid_ref[ALL], nrm_ref[ALL], inv_ref[:, 0:1], w2t_ref[ALL], vec_ref)
    d_hidden_bf = d_hidden.astype(BF16)
    x_in = jnp.concatenate([ref[ALL].astype(BF16) for ref in x_refs], axis=-1)
    add_to(dw2t_ref, FULL, dot_ta(d_out_bf, act), first)
    add_to(dw1_ref, FULL, dot_ta(x_in, d_hidden_bf), first)
    add_to(small_ref, (slice(0, 4), slice(None)), jnp.concatenate(sums, axis=0), first)
    d_x = (d_edge + dot_tb(d_hidden_bf, w1_ref[ALL])).astype(BF16)
    if last:
        d_refs[0][ALL] = d_x
    else:
        for slot in range(4):
            d_refs[slot][ALL] = col(d_x, slot).astype(d_refs[slot].dtype)
    for slot in range(4):
        dh_ref[pl.ds(slot, EDGE_BLK, stride=4), :] = col(d_hidden, slot)
    scatter_rows((accs_ref, accr_ref), (snd_ref, rcv_ref), base, dh_ref, EDGE_BLK, copies, stride)

    @pl.when(step == pl.num_programs(0) - 1)
    def _():
        small_ref[4:8, :] = jnp.zeros((4, small_ref.shape[1]), F32)

        def fin(it, carry):
            for acc_ref, out_ref in ((accs_ref, ts_ref), (accr_ref, tr_ref)):
                for slot in range(4):
                    total = acc_ref[pl.ds(it * (4 * NODE_BLK) + slot, NODE_BLK, stride=4), :]
                    for cp in range(1, copies):
                        total = total + acc_ref[pl.ds(it * (4 * NODE_BLK) + slot + cp * stride, NODE_BLK, stride=4), :]
                    out_ref[pl.ds(pl.multiple_of(it * NODE_BLK, 16), NODE_BLK),
                            slot * LANES:(slot + 1) * LANES] = total.astype(BF16)
            return carry
        lax.fori_loop(0, pad_nodes // NODE_BLK, fin, 0)


def edge_backward(snd, rcv, gs, xs, saved, ds, w1, w2t, vec, last, pad_nodes):
    rows, width = snd.shape[0], w1.shape[0]
    copies = 2
    hid, nrm, inv = saved
    slot_shapes = [sds((rows, LANES), BF16)] + [sds((rows, LANES), F32)] * 3
    d_shapes = [sds((rows, width), BF16)] if last else slot_shapes
    tail = [sds((width, width), F32), sds((width, width), F32), sds((8, width), F32),
            sds((pad_nodes, width), BF16), sds((pad_nodes, width), BF16)]
    ins = list(gs) + list(xs) + [hid, nrm, inv]
    in_specs = [rows_spec(EDGE_BLK, x.shape[1]) for x in ins] + [whole_spec(a.shape) for a in (ds, w1, w2t, vec)]
    out_specs = [rows_spec(EDGE_BLK, o.shape[1]) for o in d_shapes] + [whole_spec(o.shape) for o in tail]
    scratch = [pltpu.VMEM((4 * EDGE_BLK, LANES), F32), pltpu.VMEM((4 * EDGE_BLK, LANES), F32),
               pltpu.VMEM((copies * 4 * pad_nodes, LANES), F32), pltpu.VMEM((copies * 4 * pad_nodes, LANES), F32)]
    return call(functools.partial(edge_bwd_body, len(xs), last, pad_nodes, copies), (rows // EDGE_BLK,), in_specs, out_specs,
                d_shapes + tail, scratch, "edge_bwd", prefetch=2, work=20)(snd, rcv, *ins, ds, w1, w2t, vec)


def proj_bwd_body(ts_ref, tr_ref, v_ref, w1s_ref, w1r_ref, dw1e_ref, dw2t_ref, small_ref, node_b1_ref,
                  da_ref, db_ref, ga_ref, gb_ref, acc_s, acc_r):
    step = pl.program_id(0)
    first = step == 0
    d_v = dot_tb(ts_ref[ALL], w1s_ref[ALL]) + dot_tb(tr_ref[ALL], w1r_ref[ALL])
    for slot, out in enumerate(slot_views(da_ref, db_ref)):
        out[ALL] = col(d_v, slot)
    add_to(acc_s, FULL, dot_ta(v_ref[ALL], ts_ref[ALL]), first)
    add_to(acc_r, FULL, dot_ta(v_ref[ALL], tr_ref[ALL]), first)

    @pl.when(step == pl.num_programs(0) - 1)
    def _():
        for slot, out in enumerate(slot_views(ga_ref, gb_ref)):
            rows = slice(slot * LANES, (slot + 1) * LANES)
            for part, src in enumerate((dw1e_ref, acc_s, acc_r, dw2t_ref)):
                out[part * LANES:(part + 1) * LANES, :] = src[rows, :]
            vec_row = jnp.concatenate(
                [small_ref[k:k + 1, rows] for k in range(3)] + [jnp.zeros((1, LANES), F32)], axis=-1)
            out[512:520, :] = jnp.concatenate(
                [vec_row, small_ref[3:4, :], node_b1_ref[0:1, :], jnp.zeros((5, vec_row.shape[1]), F32)], axis=0)


def proj_backward(ts, tr, v_full, w1s, w1r, dw1e, dw2t, small, node_b1):
    nodes, width = v_full.shape
    ins = [ts, tr, v_full, w1s, w1r, dw1e, dw2t, small, node_b1]
    outs = [sds((2, nodes, LANES), F32)] * 2 + [sds((2, width + 8, width), F32)] * 2
    in_specs = [rows_spec(NODE_BLK, width)] * 3 + [whole_spec(a.shape) for a in ins[3:]]
    out_specs = [pair_spec(NODE_BLK)] * 2 + [whole_spec(outs[2].shape)] * 2
    scratch = [pltpu.VMEM((width, width), F32)] * 2
    return call(proj_bwd_body, (nodes // NODE_BLK,), in_specs, out_specs, outs, scratch, "proj_bwd")(*ins)


def write_table(ref, val):
    for slot in range(4):
        ref[pl.ds(slot, NODE_BLK, stride=4), :] = col(val, slot)


def node_proj_body(v0_ref, v1_ref, v2_ref, v3_ref, w1s_ref, w1r_ref, b1_ref, v_ref, ps_ref, pr_ref):
    v_in = jnp.concatenate([ref[ALL].astype(BF16) for ref in (v0_ref, v1_ref, v2_ref, v3_ref)], axis=-1)
    v_ref[ALL] = v_in
    write_table(ps_ref, dot(v_in, w1s_ref[ALL]) + b1_ref[0:1, :])
    write_table(pr_ref, dot(v_in, w1r_ref[ALL]))


def node_project(vs, w1s, w1r, b1):
    nodes, width = vs[0].shape[0], w1s.shape[0]
    in_specs = [rows_spec(NODE_BLK, LANES)] * 4 + [whole_spec(a.shape) for a in (w1s, w1r, b1)]
    outs = [sds((nodes, width), BF16), sds((4 * nodes, LANES), F32), sds((4 * nodes, LANES), F32)]
    out_specs = [rows_spec(NODE_BLK, width)] + [rows_spec(4 * NODE_BLK, LANES)] * 2
    return call(node_proj_body, (nodes // NODE_BLK,), in_specs, out_specs, outs, [], "node_proj")(
        *vs, w1s, w1r, b1)


def read_pairs(a_ref, b_ref):
    return jnp.concatenate([a_ref[0], b_ref[0], a_ref[1], b_ref[1]], axis=-1)


def node_fwd_body(v_ref, sa_ref, sb_ref, w1_ref, w2t_ref, vec_ref, b1_ref, w1s_ref, w1r_ref, eb1_ref,
                  new_ref, s_ref, hid_ref, nrm_ref, inv_ref, ps_ref, pr_ref):
    v_in = v_ref[ALL]
    s_in = read_pairs(sa_ref, sb_ref).astype(BF16)
    s_ref[ALL] = s_in
    hidden = dot(v_in, w1_ref[0]) + dot(s_in, w1_ref[1]) + b1_ref[0:1, :]
    hid_ref[ALL] = hidden
    _, normed, inv_std, message = mlp_tail(hidden, w2t_ref[ALL], vec_ref)
    nrm_ref[ALL] = normed
    inv_ref[ALL] = jnp.broadcast_to(inv_std, (NODE_BLK, LANES))
    new = (v_in.astype(F32) + message.astype(F32)).astype(BF16)
    new_ref[ALL] = new
    write_table(ps_ref, dot(new, w1s_ref[ALL]) + eb1_ref[0:1, :])
    write_table(pr_ref, dot(new, w1r_ref[ALL]))


def node_forward(v_in, sa, sb, w1, w2t, vec, b1, w1s, w1r, eb1):
    nodes, width = v_in.shape
    in_specs = [rows_spec(NODE_BLK, width), pair_spec(NODE_BLK), pair_spec(NODE_BLK)]
    in_specs += [whole_spec(a.shape) for a in (w1, w2t, vec, b1, w1s, w1r, eb1)]
    outs = [sds((nodes, width), BF16), sds((nodes, width), BF16), sds((nodes, width), F32), sds((nodes, width), F32),
            sds((nodes, LANES), F32), sds((4 * nodes, LANES), F32), sds((4 * nodes, LANES), F32)]
    out_specs = [rows_spec(NODE_BLK, o.shape[1]) for o in outs[:5]] + [rows_spec(4 * NODE_BLK, LANES)] * 2
    return call(node_fwd_body, (nodes // NODE_BLK,), in_specs, out_specs, outs, [], "node_fwd")(
        v_in, sa, sb, w1, w2t, vec, b1, w1s, w1r, eb1)


def node_grads(first, d_message, v_in, s_in, hidden, normed, inv_std, w1_ref, w2t_ref, vec_ref, ds_ref, gn_ref, db1_ref):
    d_out_bf, act, d_hidden, sums = mlp_back(d_message, hidden, normed, inv_std, w2t_ref[ALL], vec_ref)
    d_hidden_bf = d_hidden.astype(BF16)
    write_table(ds_ref, dot_tb(d_hidden_bf, w1_ref[1]))
    whole = slice(None)
    add_to(gn_ref, (slice(0, LANES), whole), dot_ta(col(v_in, 0), d_hidden_bf), first)
    add_to(gn_ref, (slice(LANES, 2 * LANES), whole), dot_ta(col(s_in, 0), d_hidden_bf), first)
    add_to(gn_ref, (slice(2 * LANES, 3 * LANES), whole), dot_ta(col(d_out_bf, 0), act), first)
    vec_row = jnp.concatenate([col(x, 0) for x in sums[:3]] + [jnp.zeros((1, LANES), F32)], axis=-1)
    add_to(gn_ref, (slice(3 * LANES, 3 * LANES + 8), whole),
           jnp.concatenate([vec_row, jnp.zeros((7, vec_row.shape[1]), F32)], axis=0), first)
    add_to(db1_ref, (whole, whole), jnp.broadcast_to(sums[3], db1_ref.shape), first)
    return dot_tb(d_hidden_bf, w1_ref[0])


def node_top_body(v_ref, sa_ref, sb_ref, g0_ref, g1_ref, g2_ref, g3_ref, w1_ref, w2t_ref, vec_ref, b1_ref,
                  new_ref, ds_ref, dv_ref, gn_ref, db1_ref):
    first = pl.program_id(0) == 0
    v_in = v_ref[ALL]
    s_in = read_pairs(sa_ref, sb_ref).astype(BF16)
    hidden = dot(v_in, w1_ref[0]) + dot(s_in, w1_ref[1]) + b1_ref[0:1, :]
    _, normed, inv_std, message = mlp_tail(hidden, w2t_ref[ALL], vec_ref)
    new_ref[ALL] = (col(v_in, 0).astype(F32) + col(message, 0).astype(F32)).astype(BF16)
    d_new = jnp.concatenate([ref[ALL].astype(F32) for ref in (g0_ref, g1_ref, g2_ref, g3_ref)], axis=-1)
    dv_ref[ALL] = d_new + node_grads(
        first, d_new, v_in, s_in, hidden, normed, inv_std, w1_ref, w2t_ref, vec_ref, ds_ref, gn_ref, db1_ref)


def node_top(v_in, sa, sb, gs, w1, w2t, vec, b1):
    nodes, width = v_in.shape
    in_specs = [rows_spec(NODE_BLK, width), pair_spec(NODE_BLK), pair_spec(NODE_BLK)] + [rows_spec(NODE_BLK, LANES)] * 4
    in_specs += [whole_spec(a.shape) for a in (w1, w2t, vec, b1)]
    outs = [sds((nodes, LANES), BF16), sds((4 * nodes, LANES), F32), sds((nodes, width), F32),
            sds((3 * LANES + 8, width), F32), sds((8, width), F32)]
    out_specs = [rows_spec(NODE_BLK, LANES), rows_spec(4 * NODE_BLK, LANES), rows_spec(NODE_BLK, width),
                 whole_spec(outs[3].shape), whole_spec(outs[4].shape)]
    return call(node_top_body, (nodes // NODE_BLK,), in_specs, out_specs, outs, [], "node_top")(
        v_in, sa, sb, *gs, w1, w2t, vec, b1)


def node_bwd_body(dv_ref, ta_ref, tb_ref, v_ref, s_ref, hid_ref, nrm_ref, inv_ref, w1_ref, w2t_ref, vec_ref,
                  ds_ref, dvo_ref, gn_ref, db1_ref):
    first = pl.program_id(0) == 0
    d_new = (dv_ref[ALL] + read_pairs(ta_ref, tb_ref)).astype(BF16).astype(F32)
    d_v = node_grads(first, d_new, v_ref[ALL], s_ref[ALL], hid_ref[ALL], nrm_ref[ALL], inv_ref[:, 0:1],
                     w1_ref, w2t_ref, vec_ref, ds_ref, gn_ref, db1_ref)
    dvo_ref[ALL] = col(d_new, 0) + col(d_v, 0)


def node_backward(dv, ta, tb, v_in, s_in, saved, w1, w2t, vec):
    nodes, width = v_in.shape
    ins = [dv, ta, tb, v_in, s_in, *saved]
    in_specs = [rows_spec(NODE_BLK, width), pair_spec(NODE_BLK), pair_spec(NODE_BLK)]
    in_specs += [rows_spec(NODE_BLK, a.shape[1]) for a in ins[3:]] + [whole_spec(a.shape) for a in (w1, w2t, vec)]
    outs = [sds((4 * nodes, LANES), F32), sds((nodes, LANES), F32), sds((3 * LANES + 8, width), F32), sds((8, width), F32)]
    out_specs = [rows_spec(4 * NODE_BLK, LANES), rows_spec(NODE_BLK, LANES), whole_spec(outs[2].shape),
                 whole_spec(outs[3].shape)]
    return call(node_bwd_body, (nodes // NODE_BLK,), in_specs, out_specs, outs, [], "node_bwd")(
        *ins, w1, w2t, vec)


def to_slots_body(limit, me_ref, x_ref, *out_refs):
    part, slot = pl.program_id(0), pl.program_id(1)
    blk = x_ref.shape[0]
    at = ((me_ref[0] ^ slot) * pl.num_programs(0) + part) * blk
    row = lax.broadcasted_iota(jnp.int32, x_ref.shape, 0) + at
    val = jnp.where(row < limit, x_ref[ALL].astype(F32), 0.0)
    for k, out in enumerate(out_refs):
        @pl.when(slot == k)
        def _():
            out[ALL] = val.astype(out.dtype)


def to_slots(me, val, rows):
    limit, parts = val.shape[0], 2
    blk = rows // parts
    outs = [sds((rows, LANES), BF16)] + [sds((rows, LANES), F32)] * 3
    return call(functools.partial(to_slots_body, limit), (parts, 4),
                [pl.BlockSpec((blk, LANES), lambda r, d, me: ((me[0] ^ d) * parts + r, 0))],
                [pl.BlockSpec((blk, LANES), lambda r, d, me: (r, 0))] * 4, outs, [], "to_slots", prefetch=1)(me, val)


def from_slots_body(me_ref, *refs):
    out_ref = refs[-1]
    for k, ref in enumerate(refs[:-1]):
        @pl.when(pl.program_id(1) == k)
        def _():
            out_ref[ALL] = ref[ALL].astype(BF16)


def from_slots(me, slots, limit):
    rows, parts = slots[0].shape[0], 2
    blk = rows // parts
    return call(from_slots_body, (parts, 4), [pl.BlockSpec((blk, LANES), lambda r, d, me: (r, 0))] * 4,
                pl.BlockSpec((blk, LANES), lambda r, d, me: ((me[0] ^ d) * parts + r, 0)), sds((limit, LANES), BF16), [],
                "from_slots", prefetch=1)(me, *slots)


def unpack_body(starts, *refs):
    slots, outs = refs[:4], refs[4:]
    for at, out in zip(starts, outs):
        for k, ref in enumerate(slots):
            out[k * LANES:(k + 1) * LANES, :] = ref[at:at + LANES, :].astype(BF16)


def unpack_weights(slots, starts):
    width = slots[0].shape[1]
    outs = [sds((4 * LANES, width), BF16)] * len(starts)
    return call(functools.partial(unpack_body, starts), (1,), [whole_spec(s.shape) for s in slots],
                [whole_spec(o.shape) for o in outs], outs, [], "unpack")(*slots)


def solution(mesh):
    lat_spec = P('dp', None, 'tp')
    first_spec = P(None, None, 'tp', None)
    col_spec = P(None, None, 'tp')
    param_specs = (first_spec, P(), col_spec, col_spec, first_spec, P(), col_spec, col_spec)
    in_specs = (lat_spec, lat_spec, P(), P(), lat_spec, lat_spec) + param_specs
    out_specs = (lat_spec, lat_spec, lat_spec, lat_spec) + param_specs
    tp = mesh.shape['tp']

    def swap(val, mask):
        return lax.ppermute(val, 'tp', [(i, i ^ mask) for i in range(tp)])

    def swap_dp(val):
        return lax.ppermute(val, 'dp', [(0, 1), (1, 0)])

    def slots_of(val):
        far = swap(val, 2)
        return val, swap(val, 1), far, swap(far, 1)

    def local_step(node_lat, edge_lat, senders, receivers, grad_node, grad_edge,
                   edge_w1, edge_b1, edge_w2, edge_vec, node_w1, node_b1, node_w2, node_vec):
        me = lax.axis_index('tp')
        nodes, edges = node_lat.shape[1], edge_lat.shape[1]
        width = edge_w2.shape[1]
        rows = -(-edges // (tp * EDGE_BLK)) * EDGE_BLK
        pad_nodes = (nodes // NODE_BLK + 1) * NODE_BLK

        me_ref = me.astype(jnp.int32)[None]

        def to_rows(val):
            blocks = to_slots(me_ref, val, rows)
            return [blocks[0]] + [swap(blocks[d], d) for d in range(1, tp)]

        def to_columns(slots):
            return from_slots(me_ref, [slots[0]] + [swap(slots[d], d) for d in range(1, tp)], edges)[None]

        def my_index(ids):
            padded = jnp.pad(ids, (0, tp * rows - edges), constant_values=nodes)
            return lax.dynamic_slice(padded, (me * rows,), (rows,)) * 4

        snd, rcv = my_index(senders), my_index(receivers)

        def pack(l, w1, w2):
            return jnp.concatenate([w1[l].reshape(-1, width), w2[l].T], axis=0).astype(F32)

        vecs = jnp.concatenate([edge_vec.reshape(-1), node_vec.reshape(-1)]).reshape(-1, width)
        vecs = jnp.pad(vecs, ((0, 8 - vecs.shape[0]), (0, 0)))
        group_a = jnp.concatenate([pack(0, edge_w1, edge_w2), vecs], axis=0)
        group_b = jnp.concatenate([pack(0, node_w1, node_w2), pack(1, edge_w1, edge_w2), pack(1, node_w1, node_w2)], axis=0)
        v_pad = jnp.pad(node_lat[0], ((0, pad_nodes - nodes), (0, 0)))
        v_slots = slots_of(v_pad.astype(F32))
        slots_a = slots_of(group_a)
        x_slots = to_rows(edge_lat[0])
        slots_b = slots_of(group_b)
        g_slots = to_rows(grad_edge[0])
        gn_pad = jnp.pad(grad_node[0], ((0, pad_nodes - nodes), (0, 0)))
        gn_slots = slots_of(gn_pad.astype(F32))

        mats_a = unpack_weights(slots_a, (0, 128, 256, 384))
        mats_b = unpack_weights(slots_b, tuple(range(0, 1280, 128)))
        ew, nw = [mats_a, mats_b[3:7]], [mats_b[:3], mats_b[7:]]
        all_vec = jnp.stack([s[512:515].reshape(2, 2, 3, LANES) for s in slots_a], axis=3).reshape(2, 2, 3, width)
        all_vec = jnp.pad(all_vec, ((0, 0), (0, 0), (0, 5), (0, 0)))
        eb1 = [jnp.broadcast_to(edge_b1[l][None], (8, width)) for l in range(2)]
        nb1 = [jnp.broadcast_to(node_b1[l][None], (8, width)) for l in range(2)]
        nw1 = [jnp.stack(nw[l][:2]) for l in range(2)]

        def chip_sum(pair_a, pair_b):
            return pair_a + swap(pair_b, 1)

        def all_sum(pair_a, pair_b):
            chip = chip_sum(pair_a, pair_b)
            total = chip + swap(chip, 2)[::-1]
            return total, swap(total, 1)

        def own_sum(pair_a, pair_b):
            chip = chip_sum(pair_a, pair_b)
            return chip[0] + swap(chip[1], 2)

        v0, ps, pr = node_project(v_slots, ew[0][1], ew[0][2], eb1[0])
        hid0, nrm0, inv0, e1, sa, sb = edge_forward(
            snd, rcv, x_slots, ps, pr, ew[0][0], ew[0][3], all_vec[0, 0], False, pad_nodes)
        sa, sb = all_sum(sa, sb)
        v1, s0, nhid, nnrm, ninv, ps, pr = node_forward(
            v0, sa, sb, nw1[0], nw[0][2], all_vec[1, 0], nb1[0], ew[1][1], ew[1][2], eb1[1])
        out1 = edge_forward(snd, rcv, [e1], ps, pr, ew[1][0], ew[1][3], all_vec[0, 1], True, pad_nodes)
        hid1, nrm1, inv1 = out1[:3]
        edge_out = to_columns(out1[3:7])
        sa, sb = all_sum(*out1[7:])

        v2, ds, dv, gn1, ndb1 = node_top(v1, sa, sb, [gn_pad] + list(gn_slots[1:]), nw1[1], nw[1][2], all_vec[1, 1], nb1[1])
        node_out = v2[:nodes][None]

        def mine_only(db1):
            lane = lax.broadcasted_iota(jnp.int32, db1.shape, 1)
            return jnp.where(lane // LANES == me, db1, 0.0)

        def edge_grad_sum(pair_a, pair_b):
            own = own_sum(pair_a, pair_b)
            return own + swap_dp(own)

        d_e1, dw1e, dw2t, small, ts, tr = edge_backward(
            snd, rcv, g_slots, [e1], (hid1, nrm1, inv1), ds, ew[1][0], ew[1][3], all_vec[0, 1], True, pad_nodes)
        da, db, ga1, gb1 = proj_backward(ts, tr, v1, ew[1][1], ew[1][2], dw1e, dw2t, small, mine_only(ndb1))
        da, db = all_sum(da, db)
        ds, dv_own, gn0, ndb1 = node_backward(
            dv, da, db, v0, s0, (nhid, nnrm, ninv), nw1[0], nw[0][2], all_vec[1, 0])
        *d_slots, dw1e, dw2t, small, ts, tr = edge_backward(
            snd, rcv, [d_e1], x_slots, (hid0, nrm0, inv0), ds, ew[0][0], ew[0][3], all_vec[0, 0], False, pad_nodes)
        d_edge = to_columns(d_slots)
        da, db, ga0, gb0 = proj_backward(ts, tr, v0, ew[0][1], ew[0][2], dw1e, dw2t, small, mine_only(ndb1))
        d_node = (dv_own + own_sum(da, db))[:nodes].astype(BF16)[None]

        ge = [edge_grad_sum(ga0, gb0), edge_grad_sum(ga1, gb1)]
        gn = [gn0 + swap_dp(gn0), gn1 + swap_dp(gn1)]
        stack = lambda fn: jnp.stack([fn(l) for l in range(2)])
        return (node_out, edge_out, d_node, d_edge,
                stack(lambda l: ge[l][:384].reshape(3, LANES, width)),
                stack(lambda l: ge[l][513]),
                stack(lambda l: ge[l][384:512].T),
                stack(lambda l: ge[l][512, :384].reshape(3, LANES)),
                stack(lambda l: gn[l][:256].reshape(2, LANES, width)),
                stack(lambda l: ge[l][514]),
                stack(lambda l: gn[l][256:384].T),
                stack(lambda l: gn[l][384, :384].reshape(3, LANES)))

    return jax.shard_map(local_step, mesh=mesh, in_specs=in_specs, out_specs=out_specs, check_vma=False)
```

time: 5140 us -> 1160 us (0.23)
  waiting for transfers between devices: 3180 us -> 645 us
  other arithmetic: 934 us -> 49 us
  matrix products: 471 us -> 0 us
  local copies, waits for them, and re-layouts: 451 us -> 35.2 us
  Pallas kernels: 0 us -> 397 us
  blocking collectives: 70.6 us -> 0 us
    psum x15 -> x0, waiting for transfers between devices: 3180 us -> none  [the longest x4 1550 us: mlp_forward(): hidden = lax.psum(part_sum, 'tp') + b_first]
    scatter-add x6 -> x0, other arithmetic: 661 us -> none  [one_sample(): return jax.ops.segment_sum(sample_rows, seg_ids, num_segments=num_segments)]
    ppermute x0 -> x43, waiting for transfers between devices: none -> 645 us  [the longest x39 604 us: swap(): return lax.ppermute(val, 'tp', [(i, i ^ mask) for i in range(tp)])]
    dot_general x42 -> x0, matrix products: 471 us -> none  [the longest x6 132 us: mlp_forward(): jnp.einsum('bri,ih->brh', inputs[block_id], w_first[block_id], preferred_...]
    gather x6 -> x0, local copies, waits for them, and re-layouts: 425 us -> none  [the longest x2 145 us: layer_forward(): send_lat = jnp.take(node_lat, senders, axis=1)]
    pallas_call x0 -> x16, Pallas kernels: none -> 397 us  [the longest x2 149 us: edge_backward(): call(functools.partial(edge_bwd_body, len(xs), last, pad_nodes, copies),...]
    reduce_sum x16 -> x0, other arithmetic: 178 us -> none  [the longest x4 80.2 us: mlp_backward(): jnp.sum(d_hidden, axis=(0, 1))]
    convert_element_type x7 -> x3, other arithmetic: 79.9 us -> 2.71 us  [the longest x1 1.44 us: local_step(): gn_slots = slots_of(gn_pad.astype(F32))]
  transfers between devices with their start and end apart: 15 -> 43, of which waited for: 14 -> 21; matrix products, arithmetic and copies ran while one was open for 7% -> 5% of each run, Pallas kernels for 0% -> 16%
where the time goes in v1:
time: 1160 us
  waiting for transfers between devices  645 us (56%)
  Pallas kernels  397 us (34%)
  other arithmetic  49 us (4%)
  local copies, waits for them, and re-layouts  35.2 us (3%)
  starting transfers between devices  30.6 us (3%)
    ppermute x39, waiting for transfers between devices, swap(): return lax.ppermute(val, 'tp', [(i, i ^ mask) for i in range(tp)])  604 us
    pallas_call x2, Pallas kernels, edge_backward(): call(functools.partial(edge_bwd_body, len(xs), last, pad_nodes, copies),...  149 us
    pallas_call x2, Pallas kernels, edge_forward(): call(functools.partial(edge_fwd_body, n_in, last, pad_nodes, copies), (ro...  104 us
    ppermute x4, waiting for transfers between devices, swap_dp(): return lax.ppermute(val, 'dp', [(0, 1), (1, 0)])  40.5 us
    pallas_call x2, Pallas kernels, proj_backward(): call(proj_bwd_body, (nodes // NODE_BLK,), in_specs, out_specs, outs, scra...  31.5 us
    ppermute x39, starting transfers between devices, swap(): return lax.ppermute(val, 'tp', [(i, i ^ mask) for i in range(tp)])  25 us
  transfers between devices with their start and end apart: 43, of which 21 were waited for; matrix products, arithmetic and copies ran while one was open for 5% of the time, Pallas kernels for 16%

profile of v1, /device:TPU:0, one launch (start us, length us, event | category | flops | bytes accessed | tf_op | source)
XLA Modules:
  0.0 1157.5 jit_solution(17466688315300558446)
XLA Ops:
  6.9 3.3 collective-permute-start.4
  11.4 23.2 %collective-permute-done.4.refs_2_ = f32[520,512]{1,0:T(8,128)} collective-permute-done((f32[520,512]{1,0:T(8,128)}, f32[520,512]{1,0:T(8,128)}, u32[]{:S(2)}, u32[]{:S(2)}) %collective-permute-start.4) | collective-permute-done | bytes 1064992 | tf_op jit(solution)/shard_map/ppermute | solution.py:486
  34.6 9.8 to_slots.2
  44.8 2.0 collective-permute-start.7
  46.9 16.0 %collective-permute-done.1.v2_ref = f32[2576,128]{1,0:T(8,128)} collective-permute-done((f32[2576,128]{1,0:T(8,128)}, f32[2576,128]{1,0:T(8,128)}, u32[]{:S(2)}, u32[]{:S(2)}) %collective-permute-start.1) | collective-permute-done | bytes 1318944 | tf_op jit(solution)/shard_map/ppermute | solution.py:486
  69.7 3.6 unpack.2
  74.5 10.8 node_proj.1
  85.4 33.7 %collective-permute-done.7.refs_2_.refs_3_ = f32[5120,128]{1,0:T(8,128)} collective-permute-done((f32[5120,128]{1,0:T(8,128)}, f32[5120,128]{1,0:T(8,128)}, u32[]{:S(2)}, u32[]{:S(2)}) %collective-permute-start.7) | collective-permute-done | bytes 2621472 | tf_op jit(solution)/shard_map/ppermute | solution.py:486
  119.0 54.6 %collective-permute-done.8.refs_3_.refs_4_ = f32[5120,128]{1,0:T(8,128)} collective-permute-done((f32[5120,128]{1,0:T(8,128)}, f32[5120,128]{1,0:T(8,128)}, u32[]{:S(2)}, u32[]{:S(2)}) %collective-permute-start.8) | collective-permute-done | bytes 2621472 | tf_op jit(solution)/shard_map/ppermute | solution.py:486
  173.6 51.8 %edge_fwd.2 = (f32[5120,512]{1,0:T(8,128)}, f32[5120,512]{1,0:T(8,128)}, f32[5120,128]{1,0:T(8,128)}, bf16[5120,512]{1,0:T(8,128)(2,1)}, f32[2,2576,128]{2,1,0:T(8,128)}, /*index=5*/f32[2,2576,128]{2,1,0:T(8,128)}) custom-call(s32[5120]{0:T(1024)} %get-tuple-element.222.snd_ref, s32[5120]{0:T(1024)} %get-tuple-element.223.rcv_ref, ...), custom_call_target="tpu_custom_call" | custom-call | flops 48000000000 | bytes 48000000 | tf_op jit(solution)/shard_map/edge_fwd/pallas_call | solution.py:203
  235.0 113.2 %collective-permute-done.13.refs_2_ = f32[1280,512]{1,0:T(8,128)S(1)} collective-permute-done((f32[1280,512]{1,0:T(8,128)S(1)}, f32[1280,512]{1,0:T(8,128)S(1)}, u32[]{:S(2)}, u32[]{:S(2)}) %collective-permute-start.13) | collective-permute-done | bytes 2621472 | tf_op jit(solution)/shard_map/ppermute | solution.py:486
  353.1 6.5 unpack.3
  359.6 2.3 pad_maximum_fusion.1.w1_ref
  363.7 16.1 %node_fwd.1 = (bf16[2576,512]{1,0:T(8,128)(2,1)}, bf16[2576,512]{1,0:T(8,128)(2,1)}, f32[2576,512]{1,0:T(8,128)}, f32[2576,512]{1,0:T(8,128)}, f32[2576,128]{1,0...) custom-call(bf16[2576,512]{1,0:T(8,128)(2,1)} %get-tuple-element.93.v_ref, ...), custom_call_target="tpu_custom_call" | custom-call | flops 4000000000 | bytes 4000000 | tf_op jit(solution)/shard_map/node_fwd/pallas_call | solution.py:360
  379.8 51.9 %edge_fwd.3 = (f32[5120,512]{1,0:T(8,128)}, f32[5120,512]{1,0:T(8,128)}, f32[5120,128]{1,0:T(8,128)}, bf16[5120,128]{1,0:T(8,128)(2,1)}, f32[5120,128]{1,0:T(8,1...) custom-call(s32[5120]{0:T(1024)} %get-tuple-element.222.snd_ref, ...), custom_call_target="tpu_custom_call" | custom-call | flops 48000000000 | bytes 48000000 | tf_op jit(solution)/shard_map/edge_fwd/pallas_call | solution.py:203
  431.9 4.7 collective-permute-done.15
  436.7 2.2 add.72
  442.3 56.6 %collective-permute-done.16 = f32[2,2576,128]{2,1,0:T(8,128)S(1)} collective-permute-done((f32[2,2576,128]{2,1,0:T(8,128)S(1)}, f32[2,2576,128]{2,1,0:T(8,128)S(1)}, u32[]{:S(2)}, u32[]{:S(2)}) %collective-permute-start.16) | collective-permute-done | bytes 2637856 | tf_op jit(solution)/shard_map/ppermute | solution.py:486
  500.7 9.7 to_slots.3
  512.6 14.6 %collective-permute-done.19.g2_ref = f32[2576,128]{1,0:T(8,128)} collective-permute-done((f32[2576,128]{1,0:T(8,128)}, f32[2576,128]{1,0:T(8,128)}, u32[]{:S(2)}, u32[]{:S(2)}) %collective-permute-start.19) | collective-permute-done | bytes 1318944 | tf_op jit(solution)/shard_map/ppermute | solution.py:486
  528.9 2.3 pad_maximum_fusion.2.w1_ref
  532.4 23.0 %node_top.1 = (bf16[2576,128]{1,0:T(8,128)(2,1)}, f32[10304,128]{1,0:T(8,128)}, f32[2576,512]{1,0:T(8,128)}, f32[392,512]{1,0:T(8,128)}, f32[8,512]{1,0:T(8,128)}) custom-call(bf16[2576,512]{1,0:T(8,128)(2,1)} %get-tuple-element.109.v_ref, f32[2,2576,128]{2,1,0:T(8,128)} %reverse_add_fusion.1.sa_ref, f32[2,2576,128]{2,1,0:T(8,128)} %collective-permute-done.17.sb_ref, ...), custom_call_target="tpu_custom_call" | custom-call | flops 4000000000 | bytes 4000000 | tf_op jit(solution)/shard_map/node_top/pallas_call | solution.py:400
  556.8 26.6 %collective-permute-done.25.refs_2_ = f32[5120,128]{1,0:T(8,128)} collective-permute-done((f32[5120,128]{1,0:T(8,128)}, f32[5120,128]{1,0:T(8,128)}, u32[]{:S(2)}, u32[]{:S(2)}) %collective-permute-start.25) | collective-permute-done | bytes 2621472 | tf_op jit(solution)/shard_map/ppermute | solution.py:486
  583.4 54.6 %collective-permute-done.26.refs_3_ = f32[5120,128]{1,0:T(8,128)} collective-permute-done((f32[5120,128]{1,0:T(8,128)}, f32[5120,128]{1,0:T(8,128)}, u32[]{:S(2)}, u32[]{:S(2)}) %collective-permute-start.26) | collective-permute-done | bytes 2621472 | tf_op jit(solution)/shard_map/ppermute | solution.py:486
  638.0 74.0 %edge_bwd.2 = (bf16[5120,512]{1,0:T(8,128)(2,1)}, f32[512,512]{1,0:T(8,128)}, f32[512,512]{1,0:T(8,128)}, f32[8,512]{1,0:T(8,128)}, bf16[2576,512]{1,0:T(8,128)(2,1)}, /*index=5*/bf16[2576,512]{1,0:T(8,128)(2,1)}) custom-call(s32[5120]{0:T(1024)} %get-tuple-element.222.snd_ref, s32[5120]{0:T(1024)} %get-tuple-element.223.rcv_ref, ...), custom_call_target="tpu_custom_call" | custom-call | flops 80000000000 | bytes 80000000 | tf_op jit(solution)/shard_map/edge_bwd/pallas_call | solution.py:276
  712.0 15.7 %proj_bwd.2 = (f32[2,2576,128]{2,1,0:T(8,128)}, f32[2,2576,128]{2,1,0:T(8,128)}, f32[2,520,512]{2,1,0:T(8,128)}, f32[2,520,512]{2,1,0:T(8,128)}) custom-call(bf16[2576,512]{1,0:T(8,128)(2,1)} %get-tuple-element.134.ts_ref, bf16[2576,512]{1,0:T(8,128)(2,1)} %get-tuple-element.135.tr_ref, bf16[2576,512]{1,0:T(8,128)(2,1)} %get-tuple-element.109.v_ref, ...), custom_call_target="tpu_custom_call" | custom-call | flops 4000000000 | bytes 4000000 | tf_op jit(solution)/shard_map/proj_bwd/pallas_call | solution.py:309
  728.3 4.6 collective-permute-done.27
  732.9 2.1 add.74
  736.8 57.8 %collective-permute-done.28 = f32[2,2576,128]{2,1,0:T(8,128)S(1)} collective-permute-done((f32[2,2576,128]{2,1,0:T(8,128)S(1)}, f32[2,2576,128]{2,1,0:T(8,128)S(1)}, u32[]{:S(2)}, u32[]{:S(2)}) %collective-permute-start.28) | collective-permute-done | bytes 2637856 | tf_op jit(solution)/shard_map/ppermute | solution.py:486
  797.2 5.6 collective-permute-done.38
  807.7 17.8 %node_bwd.1 = (f32[10304,128]{1,0:T(8,128)}, f32[2576,128]{1,0:T(8,128)}, f32[392,512]{1,0:T(8,128)}, f32[8,512]{1,0:T(8,128)}) custom-call(f32[2576,512]{1,0:T(8,128)} %get-tuple-element.125.dv_ref, f32[2,2576,128]{2,1,0:T(8,128)} %copy-done, f32[2,2576,128]{2,1,0:T(8,128)} %copy-done.4, bf16[2576,512]{1,0:T(8,128)(2,1)} %get-tuple-element.93.v_ref, ...), custom_call_target="tpu_custom_call" | custom-call | flops 4000000000 | bytes 4000000 | tf_op jit(solution)/shard_map/node_bwd/pallas_call | solution.py:421
  825.5 74.6 %edge_bwd.3 = (bf16[5120,128]{1,0:T(8,128)(2,1)}, f32[5120,128]{1,0:T(8,128)}, f32[5120,128]{1,0:T(8,128)}, f32[5120,128]{1,0:T(8,128)}, f32[512,512]{1,0:T(8,12...) custom-call(s32[5120]{0:T(1024)} %get-tuple-element.222.snd_ref, ...), custom_call_target="tpu_custom_call" | custom-call | flops 80000000000 | bytes 80000000 | tf_op jit(solution)/shard_map/edge_bwd/pallas_call | solution.py:276
  901.5 15.7 %proj_bwd.3 = (f32[2,2576,128]{2,1,0:T(8,128)}, f32[2,2576,128]{2,1,0:T(8,128)}, f32[2,520,512]{2,1,0:T(8,128)}, f32[2,520,512]{2,1,0:T(8,128)}) custom-call(bf16[2576,512]{1,0:T(8,128)(2,1)} %get-tuple-element.152.ts_ref, bf16[2576,512]{1,0:T(8,128)(2,1)} %get-tuple-element.153.tr_ref, bf16[2576,512]{1,0:T(8,128)(2,1)} %get-tuple-element.93.v_ref, ...), custom_call_target="tpu_custom_call" | custom-call | flops 4000000000 | bytes 4000000 | tf_op jit(solution)/shard_map/proj_bwd/pallas_call | solution.py:309
  917.2 16.4 %collective-permute-done.39 = f32[520,512]{1,0:T(8,128)} collective-permute-done((f32[520,512]{1,0:T(8,128)}, f32[520,512]{1,0:T(8,128)}, u32[]{:S(2)}, u32[]{:S(2)}) %collective-permute-start.39) | collective-permute-done | bytes 1064992 | tf_op jit(solution)/shard_map/ppermute | solution.py:486
  933.6 2.7 fusion.1
  938.4 8.1 from_slots.2
  950.2 6.9 collective-permute-done.42
  959.5 20.4 %collective-permute-done.40 = f32[520,512]{1,0:T(8,128)} collective-permute-done((f32[520,512]{1,0:T(8,128)}, f32[520,512]{1,0:T(8,128)}, u32[]{:S(2)}, u32[]{:S(2)}) %collective-permute-start.40) | collective-permute-done | bytes 1064992 | tf_op jit(solution)/shard_map/ppermute | solution.py:489
  983.5 13.2 %collective-permute-done.41 = f32[392,512]{1,0:T(8,128)S(1)} collective-permute-done((f32[392,512]{1,0:T(8,128)}, f32[392,512]{1,0:T(8,128)S(1)}, u32[]{:S(2)}, u32[]{:S(2)}) %collective-permute-start.41) | collective-permute-done | bytes 802848 | tf_op jit(solution)/shard_map/ppermute | solution.py:489
  1000.7 2.2 add.79
  1004.6 2.1 add.76
  1010.6 2.0 copy.52
  1013.2 2.1 pad_maximum_fusion.3
  1015.3 105.2 %collective-permute-done.36 = f32[520,512]{1,0:T(8,128)} collective-permute-done((f32[520,512]{1,0:T(8,128)}, f32[520,512]{1,0:T(8,128)}, u32[]{:S(2)}, u32[]{:S(2)}) %collective-permute-start.36) | collective-permute-done | bytes 1064992 | tf_op jit(solution)/shard_map/ppermute | solution.py:486
  1120.5 2.4 fusion.2
  1124.7 8.1 from_slots.3
  1132.8 15.5 %collective-permute-done.31 = f32[2576,128]{1,0:T(8,128)} collective-permute-done((f32[2576,128]{1,0:T(8,128)}, f32[2576,128]{1,0:T(8,128)}, u32[]{:S(2)}, u32[]{:S(2)}) %collective-permute-start.31) | collective-permute-done | bytes 1318944 | tf_op jit(solution)/shard_map/ppermute | solution.py:486
  1148.3 3.1 fusion.3
  (196 shorter events, 85.3 us)
Async XLA Ops:
  6.9 27.7 %collective-permute-start.4 = (f32[520,512]{1,0:T(8,128)}, f32[520,512]{1,0:T(8,128)}, u32[]{:S(2)}, u32[]{:S(2)}) collective-permute-start(f32[520,512]{1,0:T(8,128)} %select_maximum_fusion.refs_0_), channel_id=1, source_target_pairs={{0,2},{1,3},{2,0},{3,1},{4,6},{5,7},{6,4},{7,5}} | collective-permute-start | bytes 3194888 | tf_op jit(solution)/shard_map/ppermute | solution.py:486
  10.2 36.6 %collective-permute-start.3 = (f32[520,512]{1,0:T(8,128)}, f32[520,512]{1,0:T(8,128)}, u32[]{:S(2)}, u32[]{:S(2)}) collective-permute-start(f32[520,512]{1,0:T(8,128)} %select_maximum_fusion.refs_0_), channel_id=1, source_target_pairs={{0,1},{1,0},{2,3},{3,2},{4,5},{5,4},{6,7},{7,6}} | collective-permute-start | bytes 3194888 | tf_op jit(solution)/shard_map/ppermute | solution.py:486
  11.4 51.5 %collective-permute-start.1 = (f32[2576,128]{1,0:T(8,128)}, f32[2576,128]{1,0:T(8,128)}, u32[]{:S(2)}, u32[]{:S(2)}) collective-permute-start(f32[2576,128]{1,0:T(8,128)} %pad_convert_fusion.v0_ref), channel_id=1, source_target_pairs={{0,2},{1,3},{2,0},{3,1},{4,6},{5,7},{6,4},{7,5}} | collective-permute-start | bytes 3956744 | tf_op jit(solution)/shard_map/ppermute | solution.py:486
  34.6 28.3 %collective-permute-start.5 = (f32[520,512]{1,0:T(8,128)}, f32[520,512]{1,0:T(8,128)}, u32[]{:S(2)}, u32[]{:S(2)}) collective-permute-start(f32[520,512]{1,0:T(8,128)} %collective-permute-done.4.refs_2_), channel_id=1, source_target_pairs={{0,1},{1,0},{2,3},{3,2},{4,5},{5,4},{6,7},{7,6}} | collective-permute-start | bytes 3194888 | tf_op jit(solution)/shard_map/ppermute | solution.py:486
  44.3 41.0 %collective-permute-start.6 = (f32[5120,128]{1,0:T(8,128)}, f32[5120,128]{1,0:T(8,128)}, u32[]{:S(2)}, u32[]{:S(2)}) collective-permute-start(f32[5120,128]{1,0:T(8,128)} %get-tuple-element.95), channel_id=1, source_target_pairs={{0,1},{1,0},{2,3},{3,2},{4,5},{5,4},{6,7},{7,6}} | collective-permute-start | bytes 7864328 | tf_op jit(solution)/shard_map/ppermute | solution.py:486
  44.8 74.2 %collective-permute-start.7 = (f32[5120,128]{1,0:T(8,128)}, f32[5120,128]{1,0:T(8,128)}, u32[]{:S(2)}, u32[]{:S(2)}) collective-permute-start(f32[5120,128]{1,0:T(8,128)} %get-tuple-element.96), channel_id=1, source_target_pairs={{0,2},{1,3},{2,0},{3,1},{4,6},{5,7},{6,4},{7,5}} | collective-permute-start | bytes 7864328 | tf_op jit(solution)/shard_map/ppermute | solution.py:486
  46.9 126.7 %collective-permute-start.8 = (f32[5120,128]{1,0:T(8,128)}, f32[5120,128]{1,0:T(8,128)}, u32[]{:S(2)}, u32[]{:S(2)}) collective-permute-start(f32[5120,128]{1,0:T(8,128)} %get-tuple-element.97), channel_id=1, source_target_pairs={{0,3},{1,2},{2,1},{3,0},{4,7},{5,6},{6,5},{7,4}} | collective-permute-start | bytes 7864328 | tf_op jit(solution)/shard_map/ppermute | solution.py:486
  62.9 10.4 collective-permute-start
  62.9 10.4 collective-permute-start.2
  225.4 5.2 collective-permute-start.9
  232.6 115.7 %collective-permute-start.10 = (f32[2,2576,128]{2,1,0:T(8,128)S(1)}, f32[2,2576,128]{2,1,0:T(8,128)S(1)}, u32[]{:S(2)}, u32[]{:S(2)}) collective-permute-start(f32[2,2576,128]{2,1,0:T(8,128)S(1)} %add.70), channel_id=1, source_target_pairs={{0,2},{1,3},{2,0},{3,1},{4,6},{5,7},{6,4},{7,5}} | collective-permute-start | bytes 7913480 | tf_op jit(solution)/shard_map/ppermute | solution.py:486
  234.7 115.4 %copy-start.7 = (f32[1280,512]{1,0:T(8,128)}, f32[1280,512]{1,0:T(8,128)S(1)}, u32[]{:S(2)}) copy-start(f32[1280,512]{1,0:T(8,128)S(1)} %concatenate.32.refs_0_) | copy-start | bytes 7864324
  234.7 115.9 %copy-start.19 = (f32[2,512]{1,0:T(2,128)S(1)}, f32[2,512]{1,0:T(2,128)}, u32[]{:S(2)}) copy-start(f32[2,512]{1,0:T(2,128)} %param.25) | copy-start | bytes 12292
  234.8 113.5 %collective-permute-start.13 = (f32[1280,512]{1,0:T(8,128)S(1)}, f32[1280,512]{1,0:T(8,128)S(1)}, u32[]{:S(2)}, u32[]{:S(2)}) collective-permute-start(f32[1280,512]{1,0:T(8,128)S(1)} %concatenate.32.refs_0_), channel_id=1, source_target_pairs={{0,2},{1,3},{2,0},{3,1},{4,6},{5,7},{6,4},{7,5}} | collective-permute-start | bytes 7864328 | tf_op jit(solution)/shard_map/ppermute | solution.py:486
  235.0 116.2 %collective-permute-start.12 = (f32[1280,512]{1,0:T(8,128)S(1)}, f32[1280,512]{1,0:T(8,128)S(1)}, u32[]{:S(2)}, u32[]{:S(2)}) collective-permute-start(f32[1280,512]{1,0:T(8,128)S(1)} %concatenate.32.refs_0_), channel_id=1, source_target_pairs={{0,1},{1,0},{2,3},{3,2},{4,5},{5,4},{6,7},{7,6}} | collective-permute-start | bytes 7864328 | tf_op jit(solution)/shard_map/ppermute | solution.py:486
  348.2 4.9 collective-permute-start.14
  350.7 11.2 collective-permute-start.11
  431.7 5.0 collective-permute-start.15
  438.8 60.1 %collective-permute-start.16 = (f32[2,2576,128]{2,1,0:T(8,128)S(1)}, f32[2,2576,128]{2,1,0:T(8,128)S(1)}, u32[]{:S(2)}, u32[]{:S(2)}) collective-permute-start(f32[2,2576,128]{2,1,0:T(8,128)S(1)} %add.72), channel_id=1, source_target_pairs={{0,2},{1,3},{2,0},{3,1},{4,6},{5,7},{6,4},{7,5}} | collective-permute-start | bytes 7913480 | tf_op jit(solution)/shard_map/ppermute | solution.py:486
  442.0 70.6 %collective-permute-start.18 = (f32[2576,128]{1,0:T(8,128)}, f32[2576,128]{1,0:T(8,128)}, u32[]{:S(2)}, u32[]{:S(2)}) collective-permute-start(f32[2576,128]{1,0:T(8,128)} %get-tuple-element.202), channel_id=1, source_target_pairs={{0,1},{1,0},{2,3},{3,2},{4,5},{5,4},{6,7},{7,6}} | collective-permute-start | bytes 3956744 | tf_op jit(solution)/shard_map/ppermute | solution.py:486
  442.0 85.2 %collective-permute-start.19 = (f32[2576,128]{1,0:T(8,128)}, f32[2576,128]{1,0:T(8,128)}, u32[]{:S(2)}, u32[]{:S(2)}) collective-permute-start(f32[2576,128]{1,0:T(8,128)} %get-tuple-element.202), channel_id=1, source_target_pairs={{0,2},{1,3},{2,0},{3,1},{4,6},{5,7},{6,4},{7,5}} | collective-permute-start | bytes 3956744 | tf_op jit(solution)/shard_map/ppermute | solution.py:486
  500.7 30.5 %collective-permute-start.17 = (f32[2,2576,128]{2,1,0:T(8,128)}, f32[2,2576,128]{2,1,0:T(8,128)}, u32[]{:S(2)}, u32[]{:S(2)}) collective-permute-start(f32[2,2576,128]{2,1,0:T(8,128)} %reverse_add_fusion.1.sa_ref), channel_id=1, source_target_pairs={{0,1},{1,0},{2,3},{3,2},{4,5},{5,4},{6,7},{7,6}} | collective-permute-start | bytes 7913480 | tf_op jit(solution)/shard_map/ppermute | solution.py:486
  510.4 46.4 %collective-permute-start.24 = (f32[5120,128]{1,0:T(8,128)}, f32[5120,128]{1,0:T(8,128)}, u32[]{:S(2)}, u32[]{:S(2)}) collective-permute-start(f32[5120,128]{1,0:T(8,128)} %get-tuple-element.127), channel_id=1, source_target_pairs={{0,1},{1,0},{2,3},{3,2},{4,5},{5,4},{6,7},{7,6}} | collective-permute-start | bytes 7864328 | tf_op jit(solution)/shard_map/ppermute | solution.py:486
  510.9 72.5 %collective-permute-start.25 = (f32[5120,128]{1,0:T(8,128)}, f32[5120,128]{1,0:T(8,128)}, u32[]{:S(2)}, u32[]{:S(2)}) collective-permute-start(f32[5120,128]{1,0:T(8,128)} %get-tuple-element.128), channel_id=1, source_target_pairs={{0,2},{1,3},{2,0},{3,1},{4,6},{5,7},{6,4},{7,5}} | collective-permute-start | bytes 7864328 | tf_op jit(solution)/shard_map/ppermute | solution.py:486
  512.6 125.4 %collective-permute-start.26 = (f32[5120,128]{1,0:T(8,128)}, f32[5120,128]{1,0:T(8,128)}, u32[]{:S(2)}, u32[]{:S(2)}) collective-permute-start(f32[5120,128]{1,0:T(8,128)} %get-tuple-element.129), channel_id=1, source_target_pairs={{0,3},{1,2},{2,1},{3,0},{4,7},{5,6},{6,5},{7,4}} | collective-permute-start | bytes 7864328 | tf_op jit(solution)/shard_map/ppermute | solution.py:486
  527.2 3.9 collective-permute-start.20
  727.7 5.2 collective-permute-start.27
  735.0 59.8 %copy-start.22 = (f32[2,520,512]{2,1,0:T(8,128)S(1)}, f32[2,520,512]{2,1,0:T(8,128)}, u32[]{:S(2)}) copy-start(f32[2,520,512]{2,1,0:T(8,128)} %get-tuple-element.167) | copy-start | bytes 6389764
  735.0 67.8 %copy-start.9 = (f32[2,520,512]{2,1,0:T(8,128)S(1)}, f32[2,520,512]{2,1,0:T(8,128)}, u32[]{:S(2)}) copy-start(f32[2,520,512]{2,1,0:T(8,128)} %get-tuple-element.166) | copy-start | bytes 6389764
  735.0 59.5 %collective-permute-start.28 = (f32[2,2576,128]{2,1,0:T(8,128)S(1)}, f32[2,2576,128]{2,1,0:T(8,128)S(1)}, u32[]{:S(2)}, u32[]{:S(2)}) collective-permute-start(f32[2,2576,128]{2,1,0:T(8,128)S(1)} %add.74), channel_id=1, source_target_pairs={{0,2},{1,3},{2,0},{3,1},{4,6},{5,7},{6,4},{7,5}} | collective-permute-start | bytes 7913480 | tf_op jit(solution)/shard_map/ppermute | solution.py:486
  794.8 11.4 collective-permute-start.29
  794.8 8.0 collective-permute-start.38
  795.3 141.0 %collective-permute-start.21 = (f32[5120,128]{1,0:T(8,128)}, f32[5120,128]{1,0:T(8,128)}, u32[]{:S(2)}, u32[]{:S(2)}) collective-permute-start(f32[5120,128]{1,0:T(8,128)} %get-tuple-element.122), channel_id=1, source_target_pairs={{0,1},{1,0},{2,3},{3,2},{4,5},{5,4},{6,7},{7,6}} | collective-permute-start | bytes 7864328 | tf_op jit(solution)/shard_map/ppermute | solution.py:486
  795.4 142.7 %collective-permute-start.22 = (f32[5120,128]{1,0:T(8,128)}, f32[5120,128]{1,0:T(8,128)}, u32[]{:S(2)}, u32[]{:S(2)}) collective-permute-start(f32[5120,128]{1,0:T(8,128)} %get-tuple-element.123), channel_id=1, source_target_pairs={{0,2},{1,3},{2,0},{3,1},{4,6},{5,7},{6,4},{7,5}} | collective-permute-start | bytes 7864328 | tf_op jit(solution)/shard_map/ppermute | solution.py:486
  797.1 141.3 %collective-permute-start.23 = (f32[5120,128]{1,0:T(8,128)}, f32[5120,128]{1,0:T(8,128)}, u32[]{:S(2)}, u32[]{:S(2)}) collective-permute-start(f32[5120,128]{1,0:T(8,128)} %get-tuple-element.124), channel_id=1, source_target_pairs={{0,3},{1,2},{2,1},{3,0},{4,7},{5,6},{6,5},{7,4}} | collective-permute-start | bytes 7864328 | tf_op jit(solution)/shard_map/ppermute | solution.py:486
  804.5 129.1 %collective-permute-start.39 = (f32[520,512]{1,0:T(8,128)}, f32[520,512]{1,0:T(8,128)}, u32[]{:S(2)}, u32[]{:S(2)}) collective-permute-start(f32[520,512]{1,0:T(8,128)} %slice_bitcast_fusion.2), channel_id=1, source_target_pairs={{0,2},{1,3},{2,0},{3,1},{4,6},{5,7},{6,4},{7,5}} | collective-permute-start | bytes 3194888 | tf_op jit(solution)/shard_map/ppermute | solution.py:486
  917.2 87.4 %collective-permute-start.30 = (f32[2,2576,128]{2,1,0:T(8,128)}, f32[2,2576,128]{2,1,0:T(8,128)}, u32[]{:S(2)}, u32[]{:S(2)}) collective-permute-start(f32[2,2576,128]{2,1,0:T(8,128)} %get-tuple-element.159), channel_id=1, source_target_pairs={{0,1},{1,0},{2,3},{3,2},{4,5},{5,4},{6,7},{7,6}} | collective-permute-start | bytes 7913480 | tf_op jit(solution)/shard_map/ppermute | solution.py:486
  933.6 67.1 %collective-permute-start.35 = (f32[2,520,512]{2,1,0:T(8,128)}, f32[2,520,512]{2,1,0:T(8,128)}, u32[]{:S(2)}, u32[]{:S(2)}) collective-permute-start(f32[2,520,512]{2,1,0:T(8,128)} %get-tuple-element.165), channel_id=1, source_target_pairs={{0,1},{1,0},{2,3},{3,2},{4,5},{5,4},{6,7},{7,6}} | collective-permute-start | bytes 6389768 | tf_op jit(solution)/shard_map/ppermute | solution.py:486
  936.3 20.8 %collective-permute-start.42 = (f32[392,512]{1,0:T(8,128)}, f32[392,512]{1,0:T(8,128)}, u32[]{:S(2)}, u32[]{:S(2)}) collective-permute-start(f32[392,512]{1,0:T(8,128)} %get-tuple-element.169), channel_id=1, source_target_pairs={{0,4},{4,0},{1,5},{5,1},{2,6},{6,2},{3,7},{7,3}} | collective-permute-start | bytes 2408456 | tf_op jit(solution)/shard_map/ppermute | solution.py:489
  938.1 41.8 %collective-permute-start.40 = (f32[520,512]{1,0:T(8,128)}, f32[520,512]{1,0:T(8,128)}, u32[]{:S(2)}, u32[]{:S(2)}) collective-permute-start(f32[520,512]{1,0:T(8,128)} %fusion.1), channel_id=1, source_target_pairs={{0,4},{4,0},{1,5},{5,1},{2,6},{6,2},{3,7},{7,3}} | collective-permute-start | bytes 3194888 | tf_op jit(solution)/shard_map/ppermute | solution.py:489
  946.5 50.2 %collective-permute-start.41 = (f32[392,512]{1,0:T(8,128)}, f32[392,512]{1,0:T(8,128)S(1)}, u32[]{:S(2)}, u32[]{:S(2)}) collective-permute-start(f32[392,512]{1,0:T(8,128)} %get-tuple-element.168), channel_id=1, source_target_pairs={{0,4},{4,0},{1,5},{5,1},{2,6},{6,2},{3,7},{7,3}} | collective-permute-start | bytes 2408456 | tf_op jit(solution)/shard_map/ppermute | solution.py:489
  959.5 40.1 %copy-start.12 = (f32[392,512]{1,0:T(8,128)S(1)}, f32[392,512]{1,0:T(8,128)}, u32[]{:S(2)}) copy-start(f32[392,512]{1,0:T(8,128)} %get-tuple-element.168) | copy-start | bytes 2408452
  981.7 143.0 %collective-permute-start.32 = (f32[5120,128]{1,0:T(8,128)}, f32[5120,128]{1,0:T(8,128)}, u32[]{:S(2)}, u32[]{:S(2)}) collective-permute-start(f32[5120,128]{1,0:T(8,128)} %get-tuple-element.161), channel_id=1, source_target_pairs={{0,1},{1,0},{2,3},{3,2},{4,5},{5,4},{6,7},{7,6}} | collective-permute-start | bytes 7864328 | tf_op jit(solution)/shard_map/ppermute | solution.py:486
  981.8 142.9 %collective-permute-start.33 = (f32[5120,128]{1,0:T(8,128)}, f32[5120,128]{1,0:T(8,128)}, u32[]{:S(2)}, u32[]{:S(2)}) collective-permute-start(f32[5120,128]{1,0:T(8,128)} %get-tuple-element.162), channel_id=1, source_target_pairs={{0,2},{1,3},{2,0},{3,1},{4,6},{5,7},{6,4},{7,5}} | collective-permute-start | bytes 7864328 | tf_op jit(solution)/shard_map/ppermute | solution.py:486
  996.7 128.0 %collective-permute-start.34 = (f32[5120,128]{1,0:T(8,128)}, f32[5120,128]{1,0:T(8,128)}, u32[]{:S(2)}, u32[]{:S(2)}) collective-permute-start(f32[5120,128]{1,0:T(8,128)} %get-tuple-element.163), channel_id=1, source_target_pairs={{0,3},{1,2},{2,1},{3,0},{4,7},{5,6},{6,5},{7,4}} | collective-permute-start | bytes 7864328 | tf_op jit(solution)/shard_map/ppermute | solution.py:486
  1004.0 116.6 %collective-permute-start.36 = (f32[520,512]{1,0:T(8,128)}, f32[520,512]{1,0:T(8,128)}, u32[]{:S(2)}, u32[]{:S(2)}) collective-permute-start(f32[520,512]{1,0:T(8,128)} %slice_bitcast_fusion.4), channel_id=1, source_target_pairs={{0,2},{1,3},{2,0},{3,1},{4,6},{5,7},{6,4},{7,5}} | collective-permute-start | bytes 3194888 | tf_op jit(solution)/shard_map/ppermute | solution.py:486
  1008.4 139.9 %collective-permute-start.31 = (f32[2576,128]{1,0:T(8,128)}, f32[2576,128]{1,0:T(8,128)}, u32[]{:S(2)}, u32[]{:S(2)}) collective-permute-start(f32[2576,128]{1,0:T(8,128)} %get-tuple-element.195), channel_id=1, source_target_pairs={{0,2},{1,3},{2,0},{3,1},{4,6},{5,7},{6,4},{7,5}} | collective-permute-start | bytes 3956744 | tf_op jit(solution)/shard_map/ppermute | solution.py:486
  1122.9 28.5 %collective-permute-start.37 = (f32[520,512]{1,0:T(8,128)}, f32[520,512]{1,0:T(8,128)}, u32[]{:S(2)}, u32[]{:S(2)}) collective-permute-start(f32[520,512]{1,0:T(8,128)} %fusion.2), channel_id=1, source_target_pairs={{0,4},{4,0},{1,5},{5,1},{2,6},{6,2},{3,7},{7,3}} | collective-permute-start | bytes 3194888 | tf_op jit(solution)/shard_map/ppermute | solution.py:489
  (20 other events, 94.7 us)

commit v2 on v1

--- a/solution.py
+++ b/solution.py
@@ -20,6 +20,10 @@
 
 
 WORK = 4 * 10**9
+
+
+def wide(val):
+    return val.shape[-1]
 
 
 def slot_views(pair_a, pair_b):
@@ -70,6 +74,27 @@
     lax.fori_loop(0, num_rows // copies, step, 0)
 
 
+def gather_flat(tables, index_refs, base, out_ref, rows):
+    for row in rows:
+        acc = None
+        for table, index_ref in zip(tables, index_refs):
+            val = table[pl.ds(pl.multiple_of(index_ref[base + row], 4), 4), :]
+            acc = val if acc is None else acc + val
+        out_ref[4 * row:4 * row + 4, :] = acc
+
+
+def scatter_flat(accs, index_refs, base, src_ref, rows, copies, stride):
+    for row in rows[::copies]:
+        pending = []
+        for sub in range(copies):
+            val = src_ref[4 * (row + sub):4 * (row + sub) + 4, :]
+            for acc, index_ref in zip(accs, index_refs):
+                at = pl.multiple_of(index_ref[base + row + sub] + sub * stride, 4)
+                pending.append((acc, at, acc[pl.ds(at, 4), :] + val))
+        for acc, at, val in pending:
+            acc[pl.ds(at, 4), :] = val
+
+
 def zero_rows(ref, rows, step_rows):
     def step(it, carry):
         ref[pl.ds(pl.multiple_of(it * step_rows, 8), step_rows), :] = jnp.zeros((step_rows, LANES), F32)
@@ -99,7 +124,7 @@
     act = (hidden * sig).astype(BF16)
     d_act = dot(d_out_bf, w2t)
     d_hidden = d_act * (sig * (1.0 + hidden * (1.0 - sig)))
-    sums = [jnp.sum(x, axis=0, keepdims=True) for x in (d_out, d_message * normed, d_message, d_hidden)]
+    sums = [jnp.sum(x.reshape(-1, 8, wide(x)), axis=0) for x in (d_out, d_message * normed, d_message, d_hidden)]
     return d_out_bf, act, d_hidden, sums
 
 
@@ -151,16 +176,21 @@
     base = step * EDGE_BLK
     stride = 4 * pad_nodes
 
+    last_step = pl.num_programs(0) - 1
+
     @pl.when(step == 0)
     def _():
         zero_rows(acc_ref, stride * copies, stride // 4)
-
-    gather_rows((ps_ref, pr_ref), (snd_ref, rcv_ref), base, gat_ref, EDGE_BLK)
+        msg_ref[ALL] = jnp.zeros(msg_ref.shape, F32)
+        gather_rows((ps_ref, pr_ref), (snd_ref, rcv_ref), base, gat_ref, EDGE_BLK)
+
     x_in = jnp.concatenate([ref[ALL].astype(BF16) for ref in x_refs], axis=-1)
     part = dot(x_in, w1_ref[ALL])
     hidden = jnp.concatenate(
         [col(part, slot) + gat_ref[pl.ds(slot, EDGE_BLK, stride=4), :] for slot in range(4)], axis=-1)
     hid_ref[ALL] = hidden
+    scatter_flat((acc_ref,), (rcv_ref,), jnp.maximum(base - EDGE_BLK, 0), msg_ref, range(EDGE_BLK), copies, stride)
+    gather_flat((ps_ref, pr_ref), (snd_ref, rcv_ref), jnp.minimum(base + EDGE_BLK, last_step * EDGE_BLK), gat_ref, range(EDGE_BLK))
     _, normed, inv_std, message = mlp_tail(hidden, w2t_ref[ALL], vec_ref)
     nrm_ref[ALL] = normed
     inv_ref[ALL] = jnp.broadcast_to(inv_std, (EDGE_BLK, LANES))
@@ -173,7 +203,10 @@
         new_refs[0][ALL] = new
     for slot in range(4):
         msg_ref[pl.ds(slot, EDGE_BLK, stride=4), :] = col(msg, slot)
-    scatter_rows((acc_ref,), (rcv_ref,), base, msg_ref, EDGE_BLK, copies, stride)
+
+    @pl.when(step == last_step)
+    def _():
+        scatter_rows((acc_ref,), (rcv_ref,), base, msg_ref, EDGE_BLK, copies, stride)
 
     @pl.when(step == pl.num_programs(0) - 1)
     def _():
@@ -195,9 +228,9 @@
     new_shapes = slot_shapes if last else [sds((rows, width), BF16)]
     outs = [sds((rows, width), F32), sds((rows, width), F32), sds((rows, LANES), F32)] + new_shapes
     outs += [sds((2, pad_nodes, LANES), F32)] * 2
-    in_specs = [rows_spec(EDGE_BLK, x.shape[1]) for x in xs]
+    in_specs = [rows_spec(EDGE_BLK, wide(x)) for x in xs]
     in_specs += [whole_spec(a.shape) for a in (ps, pr, w1, w2t, vec)]
-    out_specs = [rows_spec(EDGE_BLK, o.shape[1]) for o in outs[:-2]] + [whole_spec(o.shape) for o in outs[-2:]]
+    out_specs = [rows_spec(EDGE_BLK, wide(o)) for o in outs[:-2]] + [whole_spec(o.shape) for o in outs[-2:]]
     scratch = [pltpu.VMEM((4 * EDGE_BLK, LANES), F32), pltpu.VMEM((4 * EDGE_BLK, LANES), F32),
                pltpu.VMEM((copies * 4 * pad_nodes, LANES), F32)]
     return call(functools.partial(edge_fwd_body, n_in, last, pad_nodes, copies), (rows // EDGE_BLK,), in_specs, out_specs,
@@ -212,28 +245,32 @@
     rest = refs[n_g + n_in + 7:]
     n_out = 1 if last else 4
     d_refs = rest[:n_out]
-    dw1_ref, dw2t_ref, small_ref, ts_ref, tr_ref, gat_ref, dh_ref, accs_ref, accr_ref = rest[n_out:]
+    dw1_ref, dw2t_ref, small_ref, ts_ref, tr_ref, gat_ref, dh_ref, accs_ref, accr_ref, sums_ref = rest[n_out:]
     step = pl.program_id(0)
     base = step * EDGE_BLK
     stride = 4 * pad_nodes
-    first = step == 0
-
-    @pl.when(first)
+    last_step = pl.num_programs(0) - 1
+
+    @pl.when(step == 0)
     def _():
         zero_rows(accs_ref, stride * copies, stride // 4)
         zero_rows(accr_ref, stride * copies, stride // 4)
-
-    gather_rows((ds_ref,), (rcv_ref,), base, gat_ref, EDGE_BLK)
+        for ref in (dh_ref, dw1_ref, dw2t_ref, sums_ref):
+            ref[ALL] = jnp.zeros(ref.shape, F32)
+        gather_rows((ds_ref,), (rcv_ref,), base, gat_ref, EDGE_BLK)
+
     d_edge = jnp.concatenate([ref[ALL].astype(F32) for ref in g_refs], axis=-1)
     d_message = jnp.concatenate(
         [col(d_edge, slot) + gat_ref[pl.ds(slot, EDGE_BLK, stride=4), :] for slot in range(4)], axis=-1)
+    scatter_flat((accs_ref, accr_ref), (snd_ref, rcv_ref), jnp.maximum(base - EDGE_BLK, 0), dh_ref, range(EDGE_BLK), copies, stride)
+    gather_flat((ds_ref,), (rcv_ref,), jnp.minimum(base + EDGE_BLK, last_step * EDGE_BLK), gat_ref, range(EDGE_BLK))
     d_out_bf, act, d_hidden, sums = mlp_back(
         d_message, hid_ref[ALL], nrm_ref[ALL], inv_ref[:, 0:1], w2t_ref[ALL], vec_ref)
     d_hidden_bf = d_hidden.astype(BF16)
     x_in = jnp.concatenate([ref[ALL].astype(BF16) for ref in x_refs], axis=-1)
-    add_to(dw2t_ref, FULL, dot_ta(d_out_bf, act), first)
-    add_to(dw1_ref, FULL, dot_ta(x_in, d_hidden_bf), first)
-    add_to(small_ref, (slice(0, 4), slice(None)), jnp.concatenate(sums, axis=0), first)
+    dw2t_ref[ALL] += dot_ta(d_out_bf, act)
+    dw1_ref[ALL] += dot_ta(x_in, d_hidden_bf)
+    sums_ref[ALL] += jnp.concatenate(sums, axis=0)
     d_x = (d_edge + dot_tb(d_hidden_bf, w1_ref[ALL])).astype(BF16)
     if last:
         d_refs[0][ALL] = d_x
@@ -242,11 +279,12 @@
             d_refs[slot][ALL] = col(d_x, slot).astype(d_refs[slot].dtype)
     for slot in range(4):
         dh_ref[pl.ds(slot, EDGE_BLK, stride=4), :] = col(d_hidden, slot)
-    scatter_rows((accs_ref, accr_ref), (snd_ref, rcv_ref), base, dh_ref, EDGE_BLK, copies, stride)
-
-    @pl.when(step == pl.num_programs(0) - 1)
-    def _():
-        small_ref[4:8, :] = jnp.zeros((4, small_ref.shape[1]), F32)
+
+    @pl.when(step == last_step)
+    def _():
+        scatter_rows((accs_ref, accr_ref), (snd_ref, rcv_ref), base, dh_ref, EDGE_BLK, copies, stride)
+        total = [jnp.sum(sums_ref[8 * k:8 * k + 8, :], axis=0, keepdims=True) for k in range(4)]
+        small_ref[ALL] = jnp.concatenate(total + [jnp.zeros((4, wide(small_ref)), F32)], axis=0)
 
         def fin(it, carry):
             for acc_ref, out_ref in ((accs_ref, ts_ref), (accr_ref, tr_ref)):
@@ -269,10 +307,11 @@
     tail = [sds((width, width), F32), sds((width, width), F32), sds((8, width), F32),
             sds((pad_nodes, width), BF16), sds((pad_nodes, width), BF16)]
     ins = list(gs) + list(xs) + [hid, nrm, inv]
-    in_specs = [rows_spec(EDGE_BLK, x.shape[1]) for x in ins] + [whole_spec(a.shape) for a in (ds, w1, w2t, vec)]
-    out_specs = [rows_spec(EDGE_BLK, o.shape[1]) for o in d_shapes] + [whole_spec(o.shape) for o in tail]
+    in_specs = [rows_spec(EDGE_BLK, wide(x)) for x in ins] + [whole_spec(a.shape) for a in (ds, w1, w2t, vec)]
+    out_specs = [rows_spec(EDGE_BLK, wide(o)) for o in d_shapes] + [whole_spec(o.shape) for o in tail]
     scratch = [pltpu.VMEM((4 * EDGE_BLK, LANES), F32), pltpu.VMEM((4 * EDGE_BLK, LANES), F32),
-               pltpu.VMEM((copies * 4 * pad_nodes, LANES), F32), pltpu.VMEM((copies * 4 * pad_nodes, LANES), F32)]
+               pltpu.VMEM((copies * 4 * pad_nodes, LANES), F32), pltpu.VMEM((copies * 4 * pad_nodes, LANES), F32),
+               pltpu.VMEM((4 * 8, width), F32)]
     return call(functools.partial(edge_bwd_body, len(xs), last, pad_nodes, copies), (rows // EDGE_BLK,), in_specs, out_specs,
                 d_shapes + tail, scratch, "edge_bwd", prefetch=2, work=20)(snd, rcv, *ins, ds, w1, w2t, vec)
 
@@ -296,7 +335,7 @@
             vec_row = jnp.concatenate(
                 [small_ref[k:k + 1, rows] for k in range(3)] + [jnp.zeros((1, LANES), F32)], axis=-1)
             out[512:520, :] = jnp.concatenate(
-                [vec_row, small_ref[3:4, :], node_b1_ref[0:1, :], jnp.zeros((5, vec_row.shape[1]), F32)], axis=0)
+                [vec_row, small_ref[3:4, :], node_b1_ref[0:1, :], jnp.zeros((5, wide(vec_row)), F32)], axis=0)
 
 
 def proj_backward(ts, tr, v_full, w1s, w1r, dw1e, dw2t, small, node_b1):
@@ -356,7 +395,7 @@
     in_specs += [whole_spec(a.shape) for a in (w1, w2t, vec, b1, w1s, w1r, eb1)]
     outs = [sds((nodes, width), BF16), sds((nodes, width), BF16), sds((nodes, width), F32), sds((nodes, width), F32),
             sds((nodes, LANES), F32), sds((4 * nodes, LANES), F32), sds((4 * nodes, LANES), F32)]
-    out_specs = [rows_spec(NODE_BLK, o.shape[1]) for o in outs[:5]] + [rows_spec(4 * NODE_BLK, LANES)] * 2
+    out_specs = [rows_spec(NODE_BLK, wide(o)) for o in outs[:5]] + [rows_spec(4 * NODE_BLK, LANES)] * 2
     return call(node_fwd_body, (nodes // NODE_BLK,), in_specs, out_specs, outs, [], "node_fwd")(
         v_in, sa, sb, w1, w2t, vec, b1, w1s, w1r, eb1)
 
@@ -369,10 +408,9 @@
     add_to(gn_ref, (slice(0, LANES), whole), dot_ta(col(v_in, 0), d_hidden_bf), first)
     add_to(gn_ref, (slice(LANES, 2 * LANES), whole), dot_ta(col(s_in, 0), d_hidden_bf), first)
     add_to(gn_ref, (slice(2 * LANES, 3 * LANES), whole), dot_ta(col(d_out_bf, 0), act), first)
-    vec_row = jnp.concatenate([col(x, 0) for x in sums[:3]] + [jnp.zeros((1, LANES), F32)], axis=-1)
     add_to(gn_ref, (slice(3 * LANES, 3 * LANES + 8), whole),
-           jnp.concatenate([vec_row, jnp.zeros((7, vec_row.shape[1]), F32)], axis=0), first)
-    add_to(db1_ref, (whole, whole), jnp.broadcast_to(sums[3], db1_ref.shape), first)
+           jnp.concatenate([col(x, 0) for x in sums[:3]] + [jnp.zeros((8, LANES), F32)], axis=-1), first)
+    add_to(db1_ref, (whole, whole), sums[3], first)
     return dot_tb(d_hidden_bf, w1_ref[0])
 
 
@@ -414,7 +452,7 @@
     nodes, width = v_in.shape
     ins = [dv, ta, tb, v_in, s_in, *saved]
     in_specs = [rows_spec(NODE_BLK, width), pair_spec(NODE_BLK), pair_spec(NODE_BLK)]
-    in_specs += [rows_spec(NODE_BLK, a.shape[1]) for a in ins[3:]] + [whole_spec(a.shape) for a in (w1, w2t, vec)]
+    in_specs += [rows_spec(NODE_BLK, wide(a)) for a in ins[3:]] + [whole_spec(a.shape) for a in (w1, w2t, vec)]
     outs = [sds((4 * nodes, LANES), F32), sds((nodes, LANES), F32), sds((3 * LANES + 8, width), F32), sds((8, width), F32)]
     out_specs = [rows_spec(4 * NODE_BLK, LANES), rows_spec(NODE_BLK, LANES), whole_spec(outs[2].shape),
                  whole_spec(outs[3].shape)]
@@ -467,7 +505,7 @@
 
 
 def unpack_weights(slots, starts):
-    width = slots[0].shape[1]
+    width = wide(slots[0])
     outs = [sds((4 * LANES, width), BF16)] * len(starts)
     return call(functools.partial(unpack_body, starts), (1,), [whole_spec(s.shape) for s in slots],
                 [whole_spec(o.shape) for o in outs], outs, [], "unpack")(*slots)
@@ -495,8 +533,9 @@
     def local_step(node_lat, edge_lat, senders, receivers, grad_node, grad_edge,
                    edge_w1, edge_b1, edge_w2, edge_vec, node_w1, node_b1, node_w2, node_vec):
         me = lax.axis_index('tp')
-        nodes, edges = node_lat.shape[1], edge_lat.shape[1]
-        width = edge_w2.shape[1]
+        _, nodes, _ = node_lat.shape
+        _, edges, _ = edge_lat.shape
+        width = wide(edge_b1)
         rows = -(-edges // (tp * EDGE_BLK)) * EDGE_BLK
         pad_nodes = (nodes // NODE_BLK + 1) * NODE_BLK
 
@@ -568,7 +607,7 @@
 
         def mine_only(db1):
             lane = lax.broadcasted_iota(jnp.int32, db1.shape, 1)
-            return jnp.where(lane // LANES == me, db1, 0.0)
+            return jnp.broadcast_to(jnp.where(lane // LANES == me, db1, 0.0).sum(axis=0), db1.shape)
 
         def edge_grad_sum(pair_a, pair_b):
             own = own_sum(pair_a, pair_b)
@@ -597,6 +636,6 @@
                 stack(lambda l: gn[l][:256].reshape(2, LANES, width)),
                 stack(lambda l: ge[l][514]),
                 stack(lambda l: gn[l][256:384].T),
-                stack(lambda l: gn[l][384, :384].reshape(3, LANES)))
+                stack(lambda l: gn[l][384:, :384].sum(axis=0).reshape(3, LANES)))
 
     return jax.shard_map(local_step, mesh=mesh, in_specs=in_specs, out_specs=out_specs, check_vma=False)

time: 1160 us -> 1110 us (0.957)
  Pallas kernels: 397 us -> 310 us
  waiting for transfers between devices: 645 us -> 676 us
    pallas_call x2, Pallas kernels: 149 us -> 85.9 us  [edge_backward(): call(functools.partial(edge_bwd_body, len(xs), last, pad_nodes, copies),...]
    ppermute x39, waiting for transfers between devices: 604 us -> 636 us  [swap(): return lax.ppermute(val, 'tp', [(i, i ^ mask) for i in range(tp)])]
    pallas_call x2, Pallas kernels: 104 us -> 78.4 us  [edge_forward(): call(functools.partial(edge_fwd_body, n_in, last, pad_nodes, copies), (ro...]
  transfers between devices with their start and end apart: 43 -> 43, of which waited for: 21 -> 21; matrix products, arithmetic and copies ran while one was open for 5% -> 5% of each run, Pallas kernels for 16% -> 14%
where the time goes in v2:
time: 1110 us; the launch traced here: 1100 us
  waiting for transfers between devices  676 us (61%)
  Pallas kernels  310 us (28%)
  other arithmetic  47.9 us (4%)
  local copies, waits for them, and re-layouts  37 us (3%)
  starting transfers between devices  30.1 us (3%)
    ppermute x39, waiting for transfers between devices, swap(): return lax.ppermute(val, 'tp', [(i, i ^ mask) for i in range(tp)])  636 us
    pallas_call x2, Pallas kernels, edge_backward(): call(functools.partial(edge_bwd_body, len(xs), last, pad_nodes, copies),...  85.9 us
    pallas_call x2, Pallas kernels, edge_forward(): call(functools.partial(edge_fwd_body, n_in, last, pad_nodes, copies), (ro...  78.4 us
    ppermute x4, waiting for transfers between devices, swap_dp(): return lax.ppermute(val, 'dp', [(0, 1), (1, 0)])  40.6 us
    pallas_call x2, Pallas kernels, proj_backward(): call(proj_bwd_body, (nodes // NODE_BLK,), in_specs, out_specs, outs, scra...  31.5 us
    ppermute x39, starting transfers between devices, swap(): return lax.ppermute(val, 'tp', [(i, i ^ mask) for i in range(tp)])  24.6 us
    pallas_call x1, Pallas kernels, node_top(): call(node_top_body, (nodes // NODE_BLK,), in_specs, out_specs, outs, [],...  23.3 us
  transfers between devices with their start and end apart: 43, of which 21 were waited for; matrix products, arithmetic and copies ran while one was open for 5% of the time, Pallas kernels for 14%

profile of v2, /device:TPU:0, one launch (start us, length us, event | category | flops | bytes accessed | tf_op | source)
XLA Modules:
  0.0 1101.9 jit_solution(15160298262086386384)
XLA Ops:
  6.9 3.3 collective-permute-start.4
  11.4 23.2 %collective-permute-done.4.refs_2_ = f32[520,512]{1,0:T(8,128)} collective-permute-done((f32[520,512]{1,0:T(8,128)}, f32[520,512]{1,0:T(8,128)}, u32[]{:S(2)}, u32[]{:S(2)}) %collective-permute-start.4) | collective-permute-done | bytes 1064992 | tf_op jit(solution)/shard_map/ppermute | solution.py:524
  34.6 9.8 to_slots.2
  44.9 2.0 collective-permute-start.7
  46.9 16.0 %collective-permute-done.1.v2_ref = f32[2576,128]{1,0:T(8,128)} collective-permute-done((f32[2576,128]{1,0:T(8,128)}, f32[2576,128]{1,0:T(8,128)}, u32[]{:S(2)}, u32[]{:S(2)}) %collective-permute-start.1) | collective-permute-done | bytes 1318944 | tf_op jit(solution)/shard_map/ppermute | solution.py:524
  69.7 3.6 unpack.2
  74.5 10.8 node_proj.1
  85.3 33.7 %collective-permute-done.7.refs_2_.refs_3_ = f32[5120,128]{1,0:T(8,128)} collective-permute-done((f32[5120,128]{1,0:T(8,128)}, f32[5120,128]{1,0:T(8,128)}, u32[]{:S(2)}, u32[]{:S(2)}) %collective-permute-start.7) | collective-permute-done | bytes 2621472 | tf_op jit(solution)/shard_map/ppermute | solution.py:524
  119.0 54.6 %collective-permute-done.8.refs_3_.refs_4_ = f32[5120,128]{1,0:T(8,128)} collective-permute-done((f32[5120,128]{1,0:T(8,128)}, f32[5120,128]{1,0:T(8,128)}, u32[]{:S(2)}, u32[]{:S(2)}) %collective-permute-start.8) | collective-permute-done | bytes 2621472 | tf_op jit(solution)/shard_map/ppermute | solution.py:524
  173.6 40.7 %edge_fwd.2 = (f32[5120,512]{1,0:T(8,128)}, f32[5120,512]{1,0:T(8,128)}, f32[5120,128]{1,0:T(8,128)}, bf16[5120,512]{1,0:T(8,128)(2,1)}, f32[2,2576,128]{2,1,0:T(8,128)}, /*index=5*/f32[2,2576,128]{2,1,0:T(8,128)}) custom-call(s32[5120]{0:T(1024)} %get-tuple-element.222.snd_ref, s32[5120]{0:T(1024)} %get-tuple-element.223.rcv_ref, ...), custom_call_target="tpu_custom_call" | custom-call | flops 48000000000 | bytes 48000000 | tf_op jit(solution)/shard_map/edge_fwd/pallas_call | solution.py:236
  224.0 113.2 %collective-permute-done.13.refs_2_ = f32[1280,512]{1,0:T(8,128)S(1)} collective-permute-done((f32[1280,512]{1,0:T(8,128)S(1)}, f32[1280,512]{1,0:T(8,128)S(1)}, u32[]{:S(2)}, u32[]{:S(2)}) %collective-permute-start.13) | collective-permute-done | bytes 2621472 | tf_op jit(solution)/shard_map/ppermute | solution.py:524
  342.0 6.5 unpack.3
  348.5 2.3 pad_maximum_fusion.1.w1_ref
  352.6 16.1 %node_fwd.1 = (bf16[2576,512]{1,0:T(8,128)(2,1)}, bf16[2576,512]{1,0:T(8,128)(2,1)}, f32[2576,512]{1,0:T(8,128)}, f32[2576,512]{1,0:T(8,128)}, f32[2576,128]{1,0...) custom-call(bf16[2576,512]{1,0:T(8,128)(2,1)} %get-tuple-element.93.v_ref, ...), custom_call_target="tpu_custom_call" | custom-call | flops 4000000000 | bytes 4000000 | tf_op jit(solution)/shard_map/node_fwd/pallas_call | solution.py:399
  368.7 37.6 %edge_fwd.3 = (f32[5120,512]{1,0:T(8,128)}, f32[5120,512]{1,0:T(8,128)}, f32[5120,128]{1,0:T(8,128)}, bf16[5120,128]{1,0:T(8,128)(2,1)}, f32[5120,128]{1,0:T(8,1...) custom-call(s32[5120]{0:T(1024)} %get-tuple-element.222.snd_ref, ...), custom_call_target="tpu_custom_call" | custom-call | flops 48000000000 | bytes 48000000 | tf_op jit(solution)/shard_map/edge_fwd/pallas_call | solution.py:236
  406.6 4.7 collective-permute-done.15
  411.3 2.2 add.72
  417.0 56.6 %collective-permute-done.16 = f32[2,2576,128]{2,1,0:T(8,128)S(1)} collective-permute-done((f32[2,2576,128]{2,1,0:T(8,128)S(1)}, f32[2,2576,128]{2,1,0:T(8,128)S(1)}, u32[]{:S(2)}, u32[]{:S(2)}) %collective-permute-start.16) | collective-permute-done | bytes 2637856 | tf_op jit(solution)/shard_map/ppermute | solution.py:524
  475.3 9.8 to_slots.3
  487.4 14.5 %collective-permute-done.19.g2_ref = f32[2576,128]{1,0:T(8,128)} collective-permute-done((f32[2576,128]{1,0:T(8,128)}, f32[2576,128]{1,0:T(8,128)}, u32[]{:S(2)}, u32[]{:S(2)}) %collective-permute-start.19) | collective-permute-done | bytes 1318944 | tf_op jit(solution)/shard_map/ppermute | solution.py:524
  502.9 2.3 pad_maximum_fusion.2.w1_ref
  506.5 23.3 %node_top.1 = (bf16[2576,128]{1,0:T(8,128)(2,1)}, f32[10304,128]{1,0:T(8,128)}, f32[2576,512]{1,0:T(8,128)}, f32[392,512]{1,0:T(8,128)}, f32[8,512]{1,0:T(8,128)}) custom-call(bf16[2576,512]{1,0:T(8,128)(2,1)} %get-tuple-element.109.v_ref, f32[2,2576,128]{2,1,0:T(8,128)} %reverse_add_fusion.1.sa_ref, f32[2,2576,128]{2,1,0:T(8,128)} %collective-permute-done.17.sb_ref, ...), custom_call_target="tpu_custom_call" | custom-call | flops 4000000000 | bytes 4000000 | tf_op jit(solution)/shard_map/node_top/pallas_call | solution.py:438
  531.2 26.9 %collective-permute-done.25.refs_2_ = f32[5120,128]{1,0:T(8,128)} collective-permute-done((f32[5120,128]{1,0:T(8,128)}, f32[5120,128]{1,0:T(8,128)}, u32[]{:S(2)}, u32[]{:S(2)}) %collective-permute-start.25) | collective-permute-done | bytes 2621472 | tf_op jit(solution)/shard_map/ppermute | solution.py:524
  558.0 54.7 %collective-permute-done.26.refs_3_ = f32[5120,128]{1,0:T(8,128)} collective-permute-done((f32[5120,128]{1,0:T(8,128)}, f32[5120,128]{1,0:T(8,128)}, u32[]{:S(2)}, u32[]{:S(2)}) %collective-permute-start.26) | collective-permute-done | bytes 2621472 | tf_op jit(solution)/shard_map/ppermute | solution.py:524
  612.7 42.5 %edge_bwd.2 = (bf16[5120,512]{1,0:T(8,128)(2,1)}, f32[512,512]{1,0:T(8,128)}, f32[512,512]{1,0:T(8,128)}, f32[8,512]{1,0:T(8,128)}, bf16[2576,512]{1,0:T(8,128)(2,1)}, /*index=5*/bf16[2576,512]{1,0:T(8,128)(2,1)}) custom-call(s32[5120]{0:T(1024)} %get-tuple-element.222.snd_ref, s32[5120]{0:T(1024)} %get-tuple-element.223.rcv_ref, ...), custom_call_target="tpu_custom_call" | custom-call | flops 80000000000 | bytes 80000000 | tf_op jit(solution)/shard_map/edge_bwd/pallas_call | solution.py:315
  656.5 15.7 %proj_bwd.2 = (f32[2,2576,128]{2,1,0:T(8,128)}, f32[2,2576,128]{2,1,0:T(8,128)}, f32[2,520,512]{2,1,0:T(8,128)}, f32[2,520,512]{2,1,0:T(8,128)}) custom-call(bf16[2576,512]{1,0:T(8,128)(2,1)} %get-tuple-element.134.ts_ref, bf16[2576,512]{1,0:T(8,128)(2,1)} %get-tuple-element.135.tr_ref, bf16[2576,512]{1,0:T(8,128)(2,1)} %get-tuple-element.109.v_ref, ...), custom_call_target="tpu_custom_call" | custom-call | flops 4000000000 | bytes 4000000 | tf_op jit(solution)/shard_map/proj_bwd/pallas_call | solution.py:348
  672.8 4.6 collective-permute-done.27
  677.3 2.1 add.74
  681.1 57.9 %collective-permute-done.28 = f32[2,2576,128]{2,1,0:T(8,128)S(1)} collective-permute-done((f32[2,2576,128]{2,1,0:T(8,128)S(1)}, f32[2,2576,128]{2,1,0:T(8,128)S(1)}, u32[]{:S(2)}, u32[]{:S(2)}) %collective-permute-start.28) | collective-permute-done | bytes 2637856 | tf_op jit(solution)/shard_map/ppermute | solution.py:524
  741.6 5.6 collective-permute-done.38
  752.0 17.8 %node_bwd.1 = (f32[10304,128]{1,0:T(8,128)}, f32[2576,128]{1,0:T(8,128)}, f32[392,512]{1,0:T(8,128)}, f32[8,512]{1,0:T(8,128)}) custom-call(f32[2576,512]{1,0:T(8,128)} %get-tuple-element.125.dv_ref, f32[2,2576,128]{2,1,0:T(8,128)} %copy-done, f32[2,2576,128]{2,1,0:T(8,128)} %copy-done.4, bf16[2576,512]{1,0:T(8,128)(2,1)} %get-tuple-element.93.v_ref, ...), custom_call_target="tpu_custom_call" | custom-call | flops 4000000000 | bytes 4000000 | tf_op jit(solution)/shard_map/node_bwd/pallas_call | solution.py:459
  769.8 43.5 %edge_bwd.3 = (bf16[5120,128]{1,0:T(8,128)(2,1)}, f32[5120,128]{1,0:T(8,128)}, f32[5120,128]{1,0:T(8,128)}, f32[5120,128]{1,0:T(8,128)}, f32[512,512]{1,0:T(8,12...) custom-call(s32[5120]{0:T(1024)} %get-tuple-element.222.snd_ref, ...), custom_call_target="tpu_custom_call" | custom-call | flops 80000000000 | bytes 80000000 | tf_op jit(solution)/shard_map/edge_bwd/pallas_call | solution.py:315
  814.7 15.8 %proj_bwd.3 = (f32[2,2576,128]{2,1,0:T(8,128)}, f32[2,2576,128]{2,1,0:T(8,128)}, f32[2,520,512]{2,1,0:T(8,128)}, f32[2,520,512]{2,1,0:T(8,128)}) custom-call(bf16[2576,512]{1,0:T(8,128)(2,1)} %get-tuple-element.152.ts_ref, bf16[2576,512]{1,0:T(8,128)(2,1)} %get-tuple-element.153.tr_ref, bf16[2576,512]{1,0:T(8,128)(2,1)} %get-tuple-element.93.v_ref, ...), custom_call_target="tpu_custom_call" | custom-call | flops 4000000000 | bytes 4000000 | tf_op jit(solution)/shard_map/proj_bwd/pallas_call | solution.py:348
  830.5 47.5 %collective-permute-done.39 = f32[520,512]{1,0:T(8,128)} collective-permute-done((f32[520,512]{1,0:T(8,128)}, f32[520,512]{1,0:T(8,128)}, u32[]{:S(2)}, u32[]{:S(2)}) %collective-permute-start.39) | collective-permute-done | bytes 1064992 | tf_op jit(solution)/shard_map/ppermute | solution.py:524
  878.0 2.7 fusion.1
  882.8 8.1 from_slots.2
  894.7 6.9 collective-permute-done.42
  904.0 20.4 %collective-permute-done.40 = f32[520,512]{1,0:T(8,128)} collective-permute-done((f32[520,512]{1,0:T(8,128)}, f32[520,512]{1,0:T(8,128)}, u32[]{:S(2)}, u32[]{:S(2)}) %collective-permute-start.40) | collective-permute-done | bytes 1064992 | tf_op jit(solution)/shard_map/ppermute | solution.py:527
  927.9 13.3 %collective-permute-done.41 = f32[392,512]{1,0:T(8,128)S(1)} collective-permute-done((f32[392,512]{1,0:T(8,128)}, f32[392,512]{1,0:T(8,128)S(1)}, u32[]{:S(2)}, u32[]{:S(2)}) %collective-permute-start.41) | collective-permute-done | bytes 802848 | tf_op jit(solution)/shard_map/ppermute | solution.py:527
  945.0 2.2 add.79
  948.9 2.1 add.76
  954.9 2.0 copy.50
  957.6 2.1 pad_maximum_fusion.3
  959.7 105.3 %collective-permute-done.36 = f32[520,512]{1,0:T(8,128)} collective-permute-done((f32[520,512]{1,0:T(8,128)}, f32[520,512]{1,0:T(8,128)}, u32[]{:S(2)}, u32[]{:S(2)}) %collective-permute-start.36) | collective-permute-done | bytes 1064992 | tf_op jit(solution)/shard_map/ppermute | solution.py:524
  1065.0 2.4 fusion.2
  1069.2 8.1 from_slots.3
  1077.3 15.4 %collective-permute-done.31 = f32[2576,128]{1,0:T(8,128)} collective-permute-done((f32[2576,128]{1,0:T(8,128)}, f32[2576,128]{1,0:T(8,128)}, u32[]{:S(2)}, u32[]{:S(2)}) %collective-permute-start.31) | collective-permute-done | bytes 1318944 | tf_op jit(solution)/shard_map/ppermute | solution.py:524
  1092.7 3.1 fusion.3
  (197 shorter events, 85.5 us)
Async XLA Ops:
  6.9 27.7 %collective-permute-start.4 = (f32[520,512]{1,0:T(8,128)}, f32[520,512]{1,0:T(8,128)}, u32[]{:S(2)}, u32[]{:S(2)}) collective-permute-start(f32[520,512]{1,0:T(8,128)} %select_maximum_fusion.refs_0_), channel_id=1, source_target_pairs={{0,2},{1,3},{2,0},{3,1},{4,6},{5,7},{6,4},{7,5}} | collective-permute-start | bytes 3194888 | tf_op jit(solution)/shard_map/ppermute | solution.py:524
  10.2 36.7 %collective-permute-start.3 = (f32[520,512]{1,0:T(8,128)}, f32[520,512]{1,0:T(8,128)}, u32[]{:S(2)}, u32[]{:S(2)}) collective-permute-start(f32[520,512]{1,0:T(8,128)} %select_maximum_fusion.refs_0_), channel_id=1, source_target_pairs={{0,1},{1,0},{2,3},{3,2},{4,5},{5,4},{6,7},{7,6}} | collective-permute-start | bytes 3194888 | tf_op jit(solution)/shard_map/ppermute | solution.py:524
  11.4 51.5 %collective-permute-start.1 = (f32[2576,128]{1,0:T(8,128)}, f32[2576,128]{1,0:T(8,128)}, u32[]{:S(2)}, u32[]{:S(2)}) collective-permute-start(f32[2576,128]{1,0:T(8,128)} %pad_convert_fusion.v0_ref), channel_id=1, source_target_pairs={{0,2},{1,3},{2,0},{3,1},{4,6},{5,7},{6,4},{7,5}} | collective-permute-start | bytes 3956744 | tf_op jit(solution)/shard_map/ppermute | solution.py:524
  34.6 28.3 %collective-permute-start.5 = (f32[520,512]{1,0:T(8,128)}, f32[520,512]{1,0:T(8,128)}, u32[]{:S(2)}, u32[]{:S(2)}) collective-permute-start(f32[520,512]{1,0:T(8,128)} %collective-permute-done.4.refs_2_), channel_id=1, source_target_pairs={{0,1},{1,0},{2,3},{3,2},{4,5},{5,4},{6,7},{7,6}} | collective-permute-start | bytes 3194888 | tf_op jit(solution)/shard_map/ppermute | solution.py:524
  44.4 41.0 %collective-permute-start.6 = (f32[5120,128]{1,0:T(8,128)}, f32[5120,128]{1,0:T(8,128)}, u32[]{:S(2)}, u32[]{:S(2)}) collective-permute-start(f32[5120,128]{1,0:T(8,128)} %get-tuple-element.95), channel_id=1, source_target_pairs={{0,1},{1,0},{2,3},{3,2},{4,5},{5,4},{6,7},{7,6}} | collective-permute-start | bytes 7864328 | tf_op jit(solution)/shard_map/ppermute | solution.py:524
  44.9 74.2 %collective-permute-start.7 = (f32[5120,128]{1,0:T(8,128)}, f32[5120,128]{1,0:T(8,128)}, u32[]{:S(2)}, u32[]{:S(2)}) collective-permute-start(f32[5120,128]{1,0:T(8,128)} %get-tuple-element.96), channel_id=1, source_target_pairs={{0,2},{1,3},{2,0},{3,1},{4,6},{5,7},{6,4},{7,5}} | collective-permute-start | bytes 7864328 | tf_op jit(solution)/shard_map/ppermute | solution.py:524
  46.9 126.7 %collective-permute-start.8 = (f32[5120,128]{1,0:T(8,128)}, f32[5120,128]{1,0:T(8,128)}, u32[]{:S(2)}, u32[]{:S(2)}) collective-permute-start(f32[5120,128]{1,0:T(8,128)} %get-tuple-element.97), channel_id=1, source_target_pairs={{0,3},{1,2},{2,1},{3,0},{4,7},{5,6},{6,5},{7,4}} | collective-permute-start | bytes 7864328 | tf_op jit(solution)/shard_map/ppermute | solution.py:524
  62.8 10.4 collective-permute-start
  62.9 10.4 collective-permute-start.2
  214.3 5.1 collective-permute-start.9
  221.5 115.6 %collective-permute-start.10 = (f32[2,2576,128]{2,1,0:T(8,128)S(1)}, f32[2,2576,128]{2,1,0:T(8,128)S(1)}, u32[]{:S(2)}, u32[]{:S(2)}) collective-permute-start(f32[2,2576,128]{2,1,0:T(8,128)S(1)} %add.70), channel_id=1, source_target_pairs={{0,2},{1,3},{2,0},{3,1},{4,6},{5,7},{6,4},{7,5}} | collective-permute-start | bytes 7913480 | tf_op jit(solution)/shard_map/ppermute | solution.py:524
  223.6 115.5 %copy-start.7 = (f32[1280,512]{1,0:T(8,128)}, f32[1280,512]{1,0:T(8,128)S(1)}, u32[]{:S(2)}) copy-start(f32[1280,512]{1,0:T(8,128)S(1)} %concatenate.32.refs_0_) | copy-start | bytes 7864324
  223.6 115.9 %copy-start.19 = (f32[2,512]{1,0:T(2,128)S(1)}, f32[2,512]{1,0:T(2,128)}, u32[]{:S(2)}) copy-start(f32[2,512]{1,0:T(2,128)} %param.25) | copy-start | bytes 12292
  223.7 113.5 %collective-permute-start.13 = (f32[1280,512]{1,0:T(8,128)S(1)}, f32[1280,512]{1,0:T(8,128)S(1)}, u32[]{:S(2)}, u32[]{:S(2)}) collective-permute-start(f32[1280,512]{1,0:T(8,128)S(1)} %concatenate.32.refs_0_), channel_id=1, source_target_pairs={{0,2},{1,3},{2,0},{3,1},{4,6},{5,7},{6,4},{7,5}} | collective-permute-start | bytes 7864328 | tf_op jit(solution)/shard_map/ppermute | solution.py:524
  224.0 116.2 %collective-permute-start.12 = (f32[1280,512]{1,0:T(8,128)S(1)}, f32[1280,512]{1,0:T(8,128)S(1)}, u32[]{:S(2)}, u32[]{:S(2)}) collective-permute-start(f32[1280,512]{1,0:T(8,128)S(1)} %concatenate.32.refs_0_), channel_id=1, source_target_pairs={{0,1},{1,0},{2,3},{3,2},{4,5},{5,4},{6,7},{7,6}} | collective-permute-start | bytes 7864328 | tf_op jit(solution)/shard_map/ppermute | solution.py:524
  337.2 4.9 collective-permute-start.14
  339.6 11.2 %collective-permute-start.11 = (f32[2,2576,128]{2,1,0:T(8,128)}, f32[2,2576,128]{2,1,0:T(8,128)}, u32[]{:S(2)}, u32[]{:S(2)}) collective-permute-start(f32[2,2576,128]{2,1,0:T(8,128)} %reverse_add_fusion.2.sa_ref), channel_id=1, source_target_pairs={{0,1},{1,0},{2,3},{3,2},{4,5},{5,4},{6,7},{7,6}} | collective-permute-start | bytes 7913480 | tf_op jit(solution)/shard_map/ppermute | solution.py:524
  406.4 5.0 collective-permute-start.15
  413.5 60.1 %collective-permute-start.16 = (f32[2,2576,128]{2,1,0:T(8,128)S(1)}, f32[2,2576,128]{2,1,0:T(8,128)S(1)}, u32[]{:S(2)}, u32[]{:S(2)}) collective-permute-start(f32[2,2576,128]{2,1,0:T(8,128)S(1)} %add.72), channel_id=1, source_target_pairs={{0,2},{1,3},{2,0},{3,1},{4,6},{5,7},{6,4},{7,5}} | collective-permute-start | bytes 7913480 | tf_op jit(solution)/shard_map/ppermute | solution.py:524
  416.7 70.7 %collective-permute-start.18 = (f32[2576,128]{1,0:T(8,128)}, f32[2576,128]{1,0:T(8,128)}, u32[]{:S(2)}, u32[]{:S(2)}) collective-permute-start(f32[2576,128]{1,0:T(8,128)} %get-tuple-element.202), channel_id=1, source_target_pairs={{0,1},{1,0},{2,3},{3,2},{4,5},{5,4},{6,7},{7,6}} | collective-permute-start | bytes 3956744 | tf_op jit(solution)/shard_map/ppermute | solution.py:524
  416.7 85.2 %collective-permute-start.19 = (f32[2576,128]{1,0:T(8,128)}, f32[2576,128]{1,0:T(8,128)}, u32[]{:S(2)}, u32[]{:S(2)}) collective-permute-start(f32[2576,128]{1,0:T(8,128)} %get-tuple-element.202), channel_id=1, source_target_pairs={{0,2},{1,3},{2,0},{3,1},{4,6},{5,7},{6,4},{7,5}} | collective-permute-start | bytes 3956744 | tf_op jit(solution)/shard_map/ppermute | solution.py:524
  475.3 29.9 %collective-permute-start.17 = (f32[2,2576,128]{2,1,0:T(8,128)}, f32[2,2576,128]{2,1,0:T(8,128)}, u32[]{:S(2)}, u32[]{:S(2)}) collective-permute-start(f32[2,2576,128]{2,1,0:T(8,128)} %reverse_add_fusion.1.sa_ref), channel_id=1, source_target_pairs={{0,1},{1,0},{2,3},{3,2},{4,5},{5,4},{6,7},{7,6}} | collective-permute-start | bytes 7913480 | tf_op jit(solution)/shard_map/ppermute | solution.py:524
  485.1 46.0 %collective-permute-start.24 = (f32[5120,128]{1,0:T(8,128)}, f32[5120,128]{1,0:T(8,128)}, u32[]{:S(2)}, u32[]{:S(2)}) collective-permute-start(f32[5120,128]{1,0:T(8,128)} %get-tuple-element.127), channel_id=1, source_target_pairs={{0,1},{1,0},{2,3},{3,2},{4,5},{5,4},{6,7},{7,6}} | collective-permute-start | bytes 7864328 | tf_op jit(solution)/shard_map/ppermute | solution.py:524
  485.6 72.4 %collective-permute-start.25 = (f32[5120,128]{1,0:T(8,128)}, f32[5120,128]{1,0:T(8,128)}, u32[]{:S(2)}, u32[]{:S(2)}) collective-permute-start(f32[5120,128]{1,0:T(8,128)} %get-tuple-element.128), channel_id=1, source_target_pairs={{0,2},{1,3},{2,0},{3,1},{4,6},{5,7},{6,4},{7,5}} | collective-permute-start | bytes 7864328 | tf_op jit(solution)/shard_map/ppermute | solution.py:524
  487.4 125.4 %collective-permute-start.26 = (f32[5120,128]{1,0:T(8,128)}, f32[5120,128]{1,0:T(8,128)}, u32[]{:S(2)}, u32[]{:S(2)}) collective-permute-start(f32[5120,128]{1,0:T(8,128)} %get-tuple-element.129), channel_id=1, source_target_pairs={{0,3},{1,2},{2,1},{3,0},{4,7},{5,6},{6,5},{7,4}} | collective-permute-start | bytes 7864328 | tf_op jit(solution)/shard_map/ppermute | solution.py:524
  501.8 3.4 collective-permute-start.20
  672.2 5.2 collective-permute-start.27
  679.4 59.8 %copy-start.22 = (f32[2,520,512]{2,1,0:T(8,128)S(1)}, f32[2,520,512]{2,1,0:T(8,128)}, u32[]{:S(2)}) copy-start(f32[2,520,512]{2,1,0:T(8,128)} %get-tuple-element.167) | copy-start | bytes 6389764
  679.4 67.8 %copy-start.9 = (f32[2,520,512]{2,1,0:T(8,128)S(1)}, f32[2,520,512]{2,1,0:T(8,128)}, u32[]{:S(2)}) copy-start(f32[2,520,512]{2,1,0:T(8,128)} %get-tuple-element.166) | copy-start | bytes 6389764
  679.4 59.5 %collective-permute-start.28 = (f32[2,2576,128]{2,1,0:T(8,128)S(1)}, f32[2,2576,128]{2,1,0:T(8,128)S(1)}, u32[]{:S(2)}, u32[]{:S(2)}) collective-permute-start(f32[2,2576,128]{2,1,0:T(8,128)S(1)} %add.74), channel_id=1, source_target_pairs={{0,2},{1,3},{2,0},{3,1},{4,6},{5,7},{6,4},{7,5}} | collective-permute-start | bytes 7913480 | tf_op jit(solution)/shard_map/ppermute | solution.py:524
  739.2 11.3 %collective-permute-start.29 = (f32[2,2576,128]{2,1,0:T(8,128)S(1)}, f32[2,2576,128]{2,1,0:T(8,128)S(1)}, u32[]{:S(2)}, u32[]{:S(2)}) collective-permute-start(f32[2,2576,128]{2,1,0:T(8,128)S(1)} %reverse_add_fusion.ta_ref), channel_id=1, source_target_pairs={{0,1},{1,0},{2,3},{3,2},{4,5},{5,4},{6,7},{7,6}} | collective-permute-start | bytes 7913480 | tf_op jit(solution)/shard_map/ppermute | solution.py:524
  739.3 8.0 collective-permute-start.38
  739.8 141.0 %collective-permute-start.21 = (f32[5120,128]{1,0:T(8,128)}, f32[5120,128]{1,0:T(8,128)}, u32[]{:S(2)}, u32[]{:S(2)}) collective-permute-start(f32[5120,128]{1,0:T(8,128)} %get-tuple-element.122), channel_id=1, source_target_pairs={{0,1},{1,0},{2,3},{3,2},{4,5},{5,4},{6,7},{7,6}} | collective-permute-start | bytes 7864328 | tf_op jit(solution)/shard_map/ppermute | solution.py:524
  739.8 142.8 %collective-permute-start.22 = (f32[5120,128]{1,0:T(8,128)}, f32[5120,128]{1,0:T(8,128)}, u32[]{:S(2)}, u32[]{:S(2)}) collective-permute-start(f32[5120,128]{1,0:T(8,128)} %get-tuple-element.123), channel_id=1, source_target_pairs={{0,2},{1,3},{2,0},{3,1},{4,6},{5,7},{6,4},{7,5}} | collective-permute-start | bytes 7864328 | tf_op jit(solution)/shard_map/ppermute | solution.py:524
  741.4 141.4 %collective-permute-start.23 = (f32[5120,128]{1,0:T(8,128)}, f32[5120,128]{1,0:T(8,128)}, u32[]{:S(2)}, u32[]{:S(2)}) collective-permute-start(f32[5120,128]{1,0:T(8,128)} %get-tuple-element.124), channel_id=1, source_target_pairs={{0,3},{1,2},{2,1},{3,0},{4,7},{5,6},{6,5},{7,4}} | collective-permute-start | bytes 7864328 | tf_op jit(solution)/shard_map/ppermute | solution.py:524
  748.9 129.2 %collective-permute-start.39 = (f32[520,512]{1,0:T(8,128)}, f32[520,512]{1,0:T(8,128)}, u32[]{:S(2)}, u32[]{:S(2)}) collective-permute-start(f32[520,512]{1,0:T(8,128)} %slice_bitcast_fusion.2), channel_id=1, source_target_pairs={{0,2},{1,3},{2,0},{3,1},{4,6},{5,7},{6,4},{7,5}} | collective-permute-start | bytes 3194888 | tf_op jit(solution)/shard_map/ppermute | solution.py:524
  830.5 118.5 %collective-permute-start.30 = (f32[2,2576,128]{2,1,0:T(8,128)}, f32[2,2576,128]{2,1,0:T(8,128)}, u32[]{:S(2)}, u32[]{:S(2)}) collective-permute-start(f32[2,2576,128]{2,1,0:T(8,128)} %get-tuple-element.159), channel_id=1, source_target_pairs={{0,1},{1,0},{2,3},{3,2},{4,5},{5,4},{6,7},{7,6}} | collective-permute-start | bytes 7913480 | tf_op jit(solution)/shard_map/ppermute | solution.py:524
  878.0 67.0 %collective-permute-start.35 = (f32[2,520,512]{2,1,0:T(8,128)}, f32[2,520,512]{2,1,0:T(8,128)}, u32[]{:S(2)}, u32[]{:S(2)}) collective-permute-start(f32[2,520,512]{2,1,0:T(8,128)} %get-tuple-element.165), channel_id=1, source_target_pairs={{0,1},{1,0},{2,3},{3,2},{4,5},{5,4},{6,7},{7,6}} | collective-permute-start | bytes 6389768 | tf_op jit(solution)/shard_map/ppermute | solution.py:524
  880.8 20.8 %collective-permute-start.42 = (f32[392,512]{1,0:T(8,128)}, f32[392,512]{1,0:T(8,128)}, u32[]{:S(2)}, u32[]{:S(2)}) collective-permute-start(f32[392,512]{1,0:T(8,128)} %get-tuple-element.169), channel_id=1, source_target_pairs={{0,4},{4,0},{1,5},{5,1},{2,6},{6,2},{3,7},{7,3}} | collective-permute-start | bytes 2408456 | tf_op jit(solution)/shard_map/ppermute | solution.py:527
  882.6 41.8 %collective-permute-start.40 = (f32[520,512]{1,0:T(8,128)}, f32[520,512]{1,0:T(8,128)}, u32[]{:S(2)}, u32[]{:S(2)}) collective-permute-start(f32[520,512]{1,0:T(8,128)} %fusion.1), channel_id=1, source_target_pairs={{0,4},{4,0},{1,5},{5,1},{2,6},{6,2},{3,7},{7,3}} | collective-permute-start | bytes 3194888 | tf_op jit(solution)/shard_map/ppermute | solution.py:527
  890.9 50.2 %collective-permute-start.41 = (f32[392,512]{1,0:T(8,128)}, f32[392,512]{1,0:T(8,128)S(1)}, u32[]{:S(2)}, u32[]{:S(2)}) collective-permute-start(f32[392,512]{1,0:T(8,128)} %get-tuple-element.168), channel_id=1, source_target_pairs={{0,4},{4,0},{1,5},{5,1},{2,6},{6,2},{3,7},{7,3}} | collective-permute-start | bytes 2408456 | tf_op jit(solution)/shard_map/ppermute | solution.py:527
  904.0 40.0 %copy-start.12 = (f32[392,512]{1,0:T(8,128)S(1)}, f32[392,512]{1,0:T(8,128)}, u32[]{:S(2)}) copy-start(f32[392,512]{1,0:T(8,128)} %get-tuple-element.168) | copy-start | bytes 2408452
  926.2 143.0 %collective-permute-start.32 = (f32[5120,128]{1,0:T(8,128)}, f32[5120,128]{1,0:T(8,128)}, u32[]{:S(2)}, u32[]{:S(2)}) collective-permute-start(f32[5120,128]{1,0:T(8,128)} %get-tuple-element.161), channel_id=1, source_target_pairs={{0,1},{1,0},{2,3},{3,2},{4,5},{5,4},{6,7},{7,6}} | collective-permute-start | bytes 7864328 | tf_op jit(solution)/shard_map/ppermute | solution.py:524
  926.2 143.0 %collective-permute-start.33 = (f32[5120,128]{1,0:T(8,128)}, f32[5120,128]{1,0:T(8,128)}, u32[]{:S(2)}, u32[]{:S(2)}) collective-permute-start(f32[5120,128]{1,0:T(8,128)} %get-tuple-element.162), channel_id=1, source_target_pairs={{0,2},{1,3},{2,0},{3,1},{4,6},{5,7},{6,4},{7,5}} | collective-permute-start | bytes 7864328 | tf_op jit(solution)/shard_map/ppermute | solution.py:524
  941.2 128.0 %collective-permute-start.34 = (f32[5120,128]{1,0:T(8,128)}, f32[5120,128]{1,0:T(8,128)}, u32[]{:S(2)}, u32[]{:S(2)}) collective-permute-start(f32[5120,128]{1,0:T(8,128)} %get-tuple-element.163), channel_id=1, source_target_pairs={{0,3},{1,2},{2,1},{3,0},{4,7},{5,6},{6,5},{7,4}} | collective-permute-start | bytes 7864328 | tf_op jit(solution)/shard_map/ppermute | solution.py:524
  948.3 116.7 %collective-permute-start.36 = (f32[520,512]{1,0:T(8,128)}, f32[520,512]{1,0:T(8,128)}, u32[]{:S(2)}, u32[]{:S(2)}) collective-permute-start(f32[520,512]{1,0:T(8,128)} %slice_bitcast_fusion.4), channel_id=1, source_target_pairs={{0,2},{1,3},{2,0},{3,1},{4,6},{5,7},{6,4},{7,5}} | collective-permute-start | bytes 3194888 | tf_op jit(solution)/shard_map/ppermute | solution.py:524
  952.7 140.0 %collective-permute-start.31 = (f32[2576,128]{1,0:T(8,128)}, f32[2576,128]{1,0:T(8,128)}, u32[]{:S(2)}, u32[]{:S(2)}) collective-permute-start(f32[2576,128]{1,0:T(8,128)} %get-tuple-element.195), channel_id=1, source_target_pairs={{0,2},{1,3},{2,0},{3,1},{4,6},{5,7},{6,4},{7,5}} | collective-permute-start | bytes 3956744 | tf_op jit(solution)/shard_map/ppermute | solution.py:524
  1067.4 28.5 %collective-permute-start.37 = (f32[520,512]{1,0:T(8,128)}, f32[520,512]{1,0:T(8,128)}, u32[]{:S(2)}, u32[]{:S(2)}) collective-permute-start(f32[520,512]{1,0:T(8,128)} %fusion.2), channel_id=1, source_target_pairs={{0,4},{4,0},{1,5},{5,1},{2,6},{6,2},{3,7},{7,3}} | collective-permute-start | bytes 3194888 | tf_op jit(solution)/shard_map/ppermute | solution.py:527
  (20 other events, 94.3 us)

commit v3 on v2

--- a/solution.py
+++ b/solution.py
@@ -1,4 +1,5 @@
 import functools
+from typing import Any, NamedTuple
 
 import jax
 import jax.numpy as jnp
@@ -6,6 +7,7 @@
 from jax.experimental import pallas as pl
 from jax.experimental.pallas import tpu as pltpu
 from jax.sharding import PartitionSpec as P
+
 
 LN_EPS = 1e-5
 F32 = jnp.float32
@@ -56,6 +58,7 @@
                 acc = val if acc is None else acc + val
             out_ref[pl.ds(pl.multiple_of(row * 4, 4), 4), :] = acc
         return carry
+
     lax.fori_loop(0, num_rows // GATHER_UNROLL, step, 0)
 
 
@@ -71,6 +74,7 @@
         for acc, at, val in pending:
             acc[pl.ds(at, 4), :] = val
         return carry
+
     lax.fori_loop(0, num_rows // copies, step, 0)
 
 
@@ -99,6 +103,7 @@
     def step(it, carry):
         ref[pl.ds(pl.multiple_of(it * step_rows, 8), step_rows), :] = jnp.zeros((step_rows, LANES), F32)
         return carry
+
     lax.fori_loop(0, rows // step_rows, step, 0)
 
 
@@ -138,15 +143,14 @@
         ref[idx] += val
 
 
-def call(body, grid, in_specs, out_specs, out_shape, scratch, name, prefetch=0, work=1):
+def call(body, grid, in_specs, out_specs, out_shape, scratch, prefetch=0, work=1):
     return pl.pallas_call(
         body,
         out_shape=out_shape,
         grid_spec=pltpu.PrefetchScalarGridSpec(
             num_scalar_prefetch=prefetch, grid=grid, in_specs=in_specs, out_specs=out_specs, scratch_shapes=scratch),
         compiler_params=pltpu.CompilerParams(vmem_limit_bytes=VMEM_BYTES, dimension_semantics=("arbitrary",) * len(grid)),
-        cost_estimate=pl.CostEstimate(flops=work * WORK, bytes_accessed=work * WORK // 1000, transcendentals=0),
-        name=name)
+        cost_estimate=pl.CostEstimate(flops=work * WORK, bytes_accessed=work * WORK // 1000, transcendentals=0))
 
 
 def rows_spec(blk, width):
@@ -162,16 +166,27 @@
     return pl.BlockSpec((2, blk, LANES), lambda i, *_: (0, i, 0))
 
 
+def in_part(lo, num):
+    step = pl.program_id(0)
+    return jnp.logical_and(step >= lo, step < lo + num)
+
+
+def part_specs(cuts):
+    lows = [sum(cuts[:k]) for k in range(len(cuts))]
+    return [pl.BlockSpec((EDGE_BLK, LANES), lambda i, *_, lo=lo, num=num: (jnp.clip(i - lo, 0, num - 1), 0))
+            for lo, num in zip(lows, cuts)]
+
+
 def sds(shape, dtype):
     return jax.ShapeDtypeStruct(shape, dtype)
 
 
-def edge_fwd_body(n_in, last, pad_nodes, copies, snd_ref, rcv_ref, *refs):
+def edge_fwd_body(n_in, cuts, pad_nodes, copies, snd_ref, rcv_ref, *refs):
     x_refs = refs[:n_in]
     ps_ref, pr_ref, w1_ref, w2t_ref, vec_ref, hid_ref, nrm_ref, inv_ref = refs[n_in:n_in + 8]
-    n_out = 4 if last else 1
+    n_out = 2 + 2 * len(cuts) if cuts else 1
     new_refs = refs[n_in + 8:n_in + 8 + n_out]
-    sa_ref, sb_ref, gat_ref, msg_ref, acc_ref = refs[n_in + 8 + n_out:]
+    sa_ref, sb_ref, gat_ref, msg_ref, acc_ref, far_ref = refs[n_in + 8 + n_out:]
     step = pl.program_id(0)
     base = step * EDGE_BLK
     stride = 4 * pad_nodes
@@ -196,9 +211,18 @@
     inv_ref[ALL] = jnp.broadcast_to(inv_std, (EDGE_BLK, LANES))
     msg = message.astype(F32)
     new = (x_in.astype(F32) + msg).astype(BF16)
-    if last:
-        for slot in range(4):
-            new_refs[slot][ALL] = col(new, slot).astype(new_refs[slot].dtype)
+    if cuts:
+        new_refs[0][ALL] = col(new, 0)
+        new_refs[1][ALL] = col(new, 1).astype(F32)
+        far_ref[ALL] = new[:, 2 * LANES:].astype(F32)
+        lo = 0
+        for num, ref2, ref3 in zip(cuts, new_refs[2:], new_refs[2 + len(cuts):]):
+            @pl.when(in_part(lo, num))
+            def _():
+                ref2[ALL] = col(far_ref, 0)
+                ref3[ALL] = col(far_ref, 1)
+
+            lo += num
     else:
         new_refs[0][ALL] = new
     for slot in range(4):
@@ -217,35 +241,40 @@
                     total = total + acc_ref[pl.ds(it * (4 * NODE_BLK) + slot + cp * stride, NODE_BLK, stride=4), :]
                 out[pl.ds(pl.multiple_of(it * NODE_BLK, 8), NODE_BLK), :] = total
             return carry
+
         lax.fori_loop(0, pad_nodes // NODE_BLK, fin, 0)
 
 
-def edge_forward(snd, rcv, xs, ps, pr, w1, w2t, vec, last, pad_nodes):
-    rows, width = snd.shape[0], w1.shape[0]
+def slot_parts(rows, cuts):
+    far = [sds((num * EDGE_BLK, LANES), F32) for num in cuts] * 2
+    near = [sds((rows, LANES), BF16), sds((rows, LANES), F32)]
+    return near + far, [rows_spec(EDGE_BLK, LANES)] * 2 + part_specs(cuts) * 2
+
+
+def edge_forward(snd, rcv, xs, ps, pr, w1, w2t, vec, cuts, pad_nodes):
+    rows, width = len(snd), wide(w1)
     copies = 4
-    n_in = len(xs)
-    slot_shapes = [sds((rows, LANES), BF16)] + [sds((rows, LANES), F32)] * 3
-    new_shapes = slot_shapes if last else [sds((rows, width), BF16)]
-    outs = [sds((rows, width), F32), sds((rows, width), F32), sds((rows, LANES), F32)] + new_shapes
-    outs += [sds((2, pad_nodes, LANES), F32)] * 2
+    news, new_specs = slot_parts(rows, cuts) if cuts else ([sds((rows, width), BF16)], [rows_spec(EDGE_BLK, width)])
+    saved = [sds((rows, width), F32), sds((rows, width), F32), sds((rows, LANES), F32)]
+    sums = [sds((2, pad_nodes, LANES), F32)] * 2
     in_specs = [rows_spec(EDGE_BLK, wide(x)) for x in xs]
     in_specs += [whole_spec(a.shape) for a in (ps, pr, w1, w2t, vec)]
-    out_specs = [rows_spec(EDGE_BLK, wide(o)) for o in outs[:-2]] + [whole_spec(o.shape) for o in outs[-2:]]
+    out_specs = [rows_spec(EDGE_BLK, wide(o)) for o in saved] + new_specs + [whole_spec(o.shape) for o in sums]
     scratch = [pltpu.VMEM((4 * EDGE_BLK, LANES), F32), pltpu.VMEM((4 * EDGE_BLK, LANES), F32),
-               pltpu.VMEM((copies * 4 * pad_nodes, LANES), F32)]
-    return call(functools.partial(edge_fwd_body, n_in, last, pad_nodes, copies), (rows // EDGE_BLK,), in_specs, out_specs,
-                outs, scratch, "edge_fwd", prefetch=2, work=12)(snd, rcv, *xs, ps, pr, w1, w2t, vec)
-
-
-def edge_bwd_body(n_in, last, pad_nodes, copies, snd_ref, rcv_ref, *refs):
-    n_g = 4 if last else 1
+               pltpu.VMEM((copies * 4 * pad_nodes, LANES), F32), pltpu.VMEM((EDGE_BLK, 2 * LANES), F32)]
+    return call(functools.partial(edge_fwd_body, len(xs), cuts, pad_nodes, copies), (rows // EDGE_BLK,), in_specs, out_specs,
+                saved + news + sums, scratch, prefetch=2, work=12)(snd, rcv, *xs, ps, pr, w1, w2t, vec)
+
+
+def edge_bwd_body(n_in, cuts, pad_nodes, copies, snd_ref, rcv_ref, *refs):
+    n_g = 2 + 2 * len(cuts) if cuts else 1
     g_refs = refs[:n_g]
     x_refs = refs[n_g:n_g + n_in]
     hid_ref, nrm_ref, inv_ref, ds_ref, w1_ref, w2t_ref, vec_ref = refs[n_g + n_in:n_g + n_in + 7]
     rest = refs[n_g + n_in + 7:]
-    n_out = 1 if last else 4
+    n_out = 1 if cuts else 4
     d_refs = rest[:n_out]
-    dw1_ref, dw2t_ref, small_ref, ts_ref, tr_ref, gat_ref, dh_ref, accs_ref, accr_ref, sums_ref = rest[n_out:]
+    dw1_ref, dw2t_ref, small_ref, ts_ref, tr_ref, gat_ref, dh_ref, accs_ref, accr_ref, sums_ref, far_ref = rest[n_out:]
     step = pl.program_id(0)
     base = step * EDGE_BLK
     stride = 4 * pad_nodes
@@ -259,6 +288,16 @@
             ref[ALL] = jnp.zeros(ref.shape, F32)
         gather_rows((ds_ref,), (rcv_ref,), base, gat_ref, EDGE_BLK)
 
+    if cuts:
+        lo = 0
+        for num, ref2, ref3 in zip(cuts, g_refs[2:], g_refs[2 + len(cuts):]):
+            @pl.when(in_part(lo, num))
+            def _():
+                far_ref[:, :LANES] = ref2[ALL]
+                far_ref[:, LANES:] = ref3[ALL]
+
+            lo += num
+        g_refs = list(g_refs[:2]) + [far_ref]
     d_edge = jnp.concatenate([ref[ALL].astype(F32) for ref in g_refs], axis=-1)
     d_message = jnp.concatenate(
         [col(d_edge, slot) + gat_ref[pl.ds(slot, EDGE_BLK, stride=4), :] for slot in range(4)], axis=-1)
@@ -272,7 +311,7 @@
     dw1_ref[ALL] += dot_ta(x_in, d_hidden_bf)
     sums_ref[ALL] += jnp.concatenate(sums, axis=0)
     d_x = (d_edge + dot_tb(d_hidden_bf, w1_ref[ALL])).astype(BF16)
-    if last:
+    if cuts:
         d_refs[0][ALL] = d_x
     else:
         for slot in range(4):
@@ -295,25 +334,26 @@
                     out_ref[pl.ds(pl.multiple_of(it * NODE_BLK, 16), NODE_BLK),
                             slot * LANES:(slot + 1) * LANES] = total.astype(BF16)
             return carry
+
         lax.fori_loop(0, pad_nodes // NODE_BLK, fin, 0)
 
 
-def edge_backward(snd, rcv, gs, xs, saved, ds, w1, w2t, vec, last, pad_nodes):
-    rows, width = snd.shape[0], w1.shape[0]
+def edge_backward(snd, rcv, gs, xs, saved, ds, w1, w2t, vec, cuts, pad_nodes):
+    rows, width = len(snd), wide(w1)
     copies = 2
-    hid, nrm, inv = saved
     slot_shapes = [sds((rows, LANES), BF16)] + [sds((rows, LANES), F32)] * 3
-    d_shapes = [sds((rows, width), BF16)] if last else slot_shapes
+    d_shapes = [sds((rows, width), BF16)] if cuts else slot_shapes
     tail = [sds((width, width), F32), sds((width, width), F32), sds((8, width), F32),
             sds((pad_nodes, width), BF16), sds((pad_nodes, width), BF16)]
-    ins = list(gs) + list(xs) + [hid, nrm, inv]
-    in_specs = [rows_spec(EDGE_BLK, wide(x)) for x in ins] + [whole_spec(a.shape) for a in (ds, w1, w2t, vec)]
+    g_specs = slot_parts(rows, cuts)[-1] if cuts else [rows_spec(EDGE_BLK, width)]
+    ins = list(xs) + list(saved)
+    in_specs = g_specs + [rows_spec(EDGE_BLK, wide(x)) for x in ins] + [whole_spec(a.shape) for a in (ds, w1, w2t, vec)]
     out_specs = [rows_spec(EDGE_BLK, wide(o)) for o in d_shapes] + [whole_spec(o.shape) for o in tail]
-    scratch = [pltpu.VMEM((4 * EDGE_BLK, LANES), F32), pltpu.VMEM((4 * EDGE_BLK, LANES), F32),
-               pltpu.VMEM((copies * 4 * pad_nodes, LANES), F32), pltpu.VMEM((copies * 4 * pad_nodes, LANES), F32),
-               pltpu.VMEM((4 * 8, width), F32)]
-    return call(functools.partial(edge_bwd_body, len(xs), last, pad_nodes, copies), (rows // EDGE_BLK,), in_specs, out_specs,
-                d_shapes + tail, scratch, "edge_bwd", prefetch=2, work=20)(snd, rcv, *ins, ds, w1, w2t, vec)
+    table = pltpu.VMEM((copies * 4 * pad_nodes, LANES), F32)
+    scratch = [pltpu.VMEM((4 * EDGE_BLK, LANES), F32), pltpu.VMEM((4 * EDGE_BLK, LANES), F32), table, table,
+               pltpu.VMEM((4 * 8, width), F32), pltpu.VMEM((EDGE_BLK, 2 * LANES), F32)]
+    return call(functools.partial(edge_bwd_body, len(xs), cuts, pad_nodes, copies), (rows // EDGE_BLK,), in_specs, out_specs,
+                d_shapes + tail, scratch, prefetch=2, work=20)(snd, rcv, *gs, *ins, ds, w1, w2t, vec)
 
 
 def proj_bwd_body(ts_ref, tr_ref, v_ref, w1s_ref, w1r_ref, dw1e_ref, dw2t_ref, small_ref, node_b1_ref,
@@ -345,7 +385,7 @@
     in_specs = [rows_spec(NODE_BLK, width)] * 3 + [whole_spec(a.shape) for a in ins[3:]]
     out_specs = [pair_spec(NODE_BLK)] * 2 + [whole_spec(outs[2].shape)] * 2
     scratch = [pltpu.VMEM((width, width), F32)] * 2
-    return call(proj_bwd_body, (nodes // NODE_BLK,), in_specs, out_specs, outs, scratch, "proj_bwd")(*ins)
+    return call(proj_bwd_body, (nodes // NODE_BLK,), in_specs, out_specs, outs, scratch)(*ins)
 
 
 def write_table(ref, val):
@@ -365,7 +405,7 @@
     in_specs = [rows_spec(NODE_BLK, LANES)] * 4 + [whole_spec(a.shape) for a in (w1s, w1r, b1)]
     outs = [sds((nodes, width), BF16), sds((4 * nodes, LANES), F32), sds((4 * nodes, LANES), F32)]
     out_specs = [rows_spec(NODE_BLK, width)] + [rows_spec(4 * NODE_BLK, LANES)] * 2
-    return call(node_proj_body, (nodes // NODE_BLK,), in_specs, out_specs, outs, [], "node_proj")(
+    return call(node_proj_body, (nodes // NODE_BLK,), in_specs, out_specs, outs, [])(
         *vs, w1s, w1r, b1)
 
 
@@ -396,7 +436,7 @@
     outs = [sds((nodes, width), BF16), sds((nodes, width), BF16), sds((nodes, width), F32), sds((nodes, width), F32),
             sds((nodes, LANES), F32), sds((4 * nodes, LANES), F32), sds((4 * nodes, LANES), F32)]
     out_specs = [rows_spec(NODE_BLK, wide(o)) for o in outs[:5]] + [rows_spec(4 * NODE_BLK, LANES)] * 2
-    return call(node_fwd_body, (nodes // NODE_BLK,), in_specs, out_specs, outs, [], "node_fwd")(
+    return call(node_fwd_body, (nodes // NODE_BLK,), in_specs, out_specs, outs, [])(
         v_in, sa, sb, w1, w2t, vec, b1, w1s, w1r, eb1)
 
 
@@ -435,7 +475,7 @@
             sds((3 * LANES + 8, width), F32), sds((8, width), F32)]
     out_specs = [rows_spec(NODE_BLK, LANES), rows_spec(4 * NODE_BLK, LANES), rows_spec(NODE_BLK, width),
                  whole_spec(outs[3].shape), whole_spec(outs[4].shape)]
-    return call(node_top_body, (nodes // NODE_BLK,), in_specs, out_specs, outs, [], "node_top")(
+    return call(node_top_body, (nodes // NODE_BLK,), in_specs, out_specs, outs, [])(
         v_in, sa, sb, *gs, w1, w2t, vec, b1)
 
 
@@ -456,59 +496,128 @@
     outs = [sds((4 * nodes, LANES), F32), sds((nodes, LANES), F32), sds((3 * LANES + 8, width), F32), sds((8, width), F32)]
     out_specs = [rows_spec(4 * NODE_BLK, LANES), rows_spec(NODE_BLK, LANES), whole_spec(outs[2].shape),
                  whole_spec(outs[3].shape)]
-    return call(node_bwd_body, (nodes // NODE_BLK,), in_specs, out_specs, outs, [], "node_bwd")(
+    return call(node_bwd_body, (nodes // NODE_BLK,), in_specs, out_specs, outs, [])(
         *ins, w1, w2t, vec)
 
 
-def to_slots_body(limit, me_ref, x_ref, *out_refs):
-    part, slot = pl.program_id(0), pl.program_id(1)
-    blk = x_ref.shape[0]
-    at = ((me_ref[0] ^ slot) * pl.num_programs(0) + part) * blk
-    row = lax.broadcasted_iota(jnp.int32, x_ref.shape, 0) + at
+def part_copies(buf, parts, sem, slot, outward):
+    lo, copies = 0, []
+    for k, part in enumerate(parts):
+        here = buf.at[pl.ds(lo, len(part))]
+        src, dst = (here, part) if outward else (part, here)
+        copies.append(pltpu.make_async_copy(src, dst, sem.at[slot, k]))
+        lo += len(part)
+    return copies
+
+
+def split_slots(refs, num):
+    return [refs[:1], refs[1:2], refs[2:2 + num], refs[2 + num:]]
+
+
+def to_slots_body(limit, num, me_ref, x_ref, *refs):
+    slots = split_slots(refs[:-3], num)
+    own, far, sem = refs[-3:]
+    step = pl.program_id(0)
+    rows = len(x_ref)
+    row = lax.broadcasted_iota(jnp.int32, x_ref.shape, 0) + (me_ref[0] ^ step) * rows
     val = jnp.where(row < limit, x_ref[ALL].astype(F32), 0.0)
-    for k, out in enumerate(out_refs):
-        @pl.when(slot == k)
+    moves = [part_copies(own if k == 0 else far.at[k - 1], parts, sem, k, True) for k, parts in enumerate(slots)]
+    for k, copies in enumerate(moves):
+        @pl.when(step == k)
         def _():
-            out[ALL] = val.astype(out.dtype)
-
-
-def to_slots(me, val, rows):
-    limit, parts = val.shape[0], 2
-    blk = rows // parts
-    outs = [sds((rows, LANES), BF16)] + [sds((rows, LANES), F32)] * 3
-    return call(functools.partial(to_slots_body, limit), (parts, 4),
-                [pl.BlockSpec((blk, LANES), lambda r, d, me: ((me[0] ^ d) * parts + r, 0))],
-                [pl.BlockSpec((blk, LANES), lambda r, d, me: (r, 0))] * 4, outs, [], "to_slots", prefetch=1)(me, val)
-
-
-def from_slots_body(me_ref, *refs):
-    out_ref = refs[-1]
-    for k, ref in enumerate(refs[:-1]):
-        @pl.when(pl.program_id(1) == k)
+            if k == 0:
+                own[ALL] = val.astype(BF16)
+            else:
+                far[k - 1] = val
+            for copy in copies:
+                copy.start()
+
+    @pl.when(step == len(slots) - 1)
+    def _():
+        for copies in moves:
+            for copy in copies:
+                copy.wait()
+
+
+def slot_buffers(rows, num):
+    return [pltpu.VMEM((rows, LANES), BF16), pltpu.VMEM((3, rows, LANES), F32), pltpu.SemaphoreType.DMA((4, num))]
+
+
+ANYWHERE = pl.BlockSpec(memory_space=pl.ANY)
+
+
+def to_slots(me, val, rows, cuts):
+    outs, _ = slot_parts(rows, cuts)
+    return call(functools.partial(to_slots_body, len(val), len(cuts)), (4,),
+                [pl.BlockSpec((rows, LANES), lambda d, me: (me[0] ^ d, 0))], [ANYWHERE] * len(outs), outs,
+                slot_buffers(rows, len(cuts)), prefetch=1)(me, val)
+
+
+def from_slots_body(num, me_ref, *refs):
+    slots = split_slots(refs[:-4], num)
+    out_ref, own, far, sem = refs[-4:]
+    step = pl.program_id(0)
+    moves = [part_copies(own if k == 0 else far.at[k - 1], parts, sem, k, False) for k, parts in enumerate(slots)]
+
+    @pl.when(step == 0)
+    def _():
+        for copies in moves:
+            for copy in copies:
+                copy.start()
+
+    for k, copies in enumerate(moves):
+        @pl.when(step == k)
         def _():
-            out_ref[ALL] = ref[ALL].astype(BF16)
-
-
-def from_slots(me, slots, limit):
-    rows, parts = slots[0].shape[0], 2
-    blk = rows // parts
-    return call(from_slots_body, (parts, 4), [pl.BlockSpec((blk, LANES), lambda r, d, me: (r, 0))] * 4,
-                pl.BlockSpec((blk, LANES), lambda r, d, me: ((me[0] ^ d) * parts + r, 0)), sds((limit, LANES), BF16), [],
-                "from_slots", prefetch=1)(me, *slots)
-
-
-def unpack_body(starts, *refs):
-    slots, outs = refs[:4], refs[4:]
-    for at, out in zip(starts, outs):
-        for k, ref in enumerate(slots):
-            out[k * LANES:(k + 1) * LANES, :] = ref[at:at + LANES, :].astype(BF16)
-
-
-def unpack_weights(slots, starts):
+            for copy in copies:
+                copy.wait()
+            out_ref[ALL] = own[ALL] if k == 0 else far[k - 1].astype(BF16)
+
+
+def from_slots(me, slots, num, limit):
+    rows = len(slots[0])
+    return call(functools.partial(from_slots_body, num), (4,), [ANYWHERE] * len(slots),
+                pl.BlockSpec((rows, LANES), lambda d, me: (me[0] ^ d, 0)), sds((limit, LANES), BF16),
+                slot_buffers(rows, num), prefetch=1)(me, *slots)
+
+
+def unpack_body(per, half_ref, *refs):
+    near, far, outs = refs[:2], refs[2:6], refs[6:]
+    for k, refs_of in enumerate((near[:1] * 2, near[1:] * 2, far[:2], far[2:])):
+        dst = slice(k * LANES, (k + 1) * LANES)
+        for p, out in enumerate(outs):
+            src = pl.ds(p % per * LANES, LANES)
+            if k < 2:
+                out[dst, :] = refs_of[0][p // per, src, :].astype(BF16)
+                continue
+            for mine in range(2):
+                @pl.when(half_ref[0] == mine)
+                def _():
+                    out[dst, :] = refs_of[p // per ^ mine][src, :].astype(BF16)
+
+
+def unpack_weights(half, slots, per):
     width = wide(slots[0])
-    outs = [sds((4 * LANES, width), BF16)] * len(starts)
-    return call(functools.partial(unpack_body, starts), (1,), [whole_spec(s.shape) for s in slots],
-                [whole_spec(o.shape) for o in outs], outs, [], "unpack")(*slots)
+    outs = [sds((4 * LANES, width), BF16)] * (2 * per)
+    return call(functools.partial(unpack_body, per), (1,), [whole_spec(s.shape) for s in slots],
+                [whole_spec(o.shape) for o in outs], outs, [], prefetch=1)(half, *slots)
+
+
+IN_CUTS = (20,)
+GRAD_CUTS = (4, 7, 9)
+OUT_CUTS = (12, 8)
+
+
+class Layer(NamedTuple):
+    w1: Any
+    ws: Any
+    wr: Any
+    w2t: Any
+    vec: Any
+    b1: Any
+    node_w1: Any
+    node_w2t: Any
+    node_vec: Any
+    node_b1: Any
 
 
 def solution(mesh):
@@ -526,116 +635,123 @@
     def swap_dp(val):
         return lax.ppermute(val, 'dp', [(0, 1), (1, 0)])
 
-    def slots_of(val):
-        far = swap(val, 2)
-        return val, swap(val, 1), far, swap(far, 1)
-
     def local_step(node_lat, edge_lat, senders, receivers, grad_node, grad_edge,
                    edge_w1, edge_b1, edge_w2, edge_vec, node_w1, node_b1, node_w2, node_vec):
-        me = lax.axis_index('tp')
+        me, half = lax.axis_index('tp'), lax.axis_index('dp')
         _, nodes, _ = node_lat.shape
         _, edges, _ = edge_lat.shape
         width = wide(edge_b1)
         rows = -(-edges // (tp * EDGE_BLK)) * EDGE_BLK
         pad_nodes = (nodes // NODE_BLK + 1) * NODE_BLK
-
-        me_ref = me.astype(jnp.int32)[None]
-
-        def to_rows(val):
-            blocks = to_slots(me_ref, val, rows)
-            return [blocks[0]] + [swap(blocks[d], d) for d in range(1, tp)]
-
-        def to_columns(slots):
-            return from_slots(me_ref, [slots[0]] + [swap(slots[d], d) for d in range(1, tp)], edges)[None]
+        me_ref, half_ref = me.astype(jnp.int32)[None], half.astype(jnp.int32)[None]
+
+        def to_rows(val, cuts):
+            own, near, *far = to_slots(me_ref, val, rows, cuts)
+            num = len(cuts)
+            moved = [swap(part, 2 + k // num) for k, part in enumerate(far)]
+            return [own, swap(near, 1)] + moved
+
+        def to_columns(parts, cuts):
+            own, near, *far = parts
+            num = len(cuts)
+            moved = [swap(part, 2 + k // num) for k, part in enumerate(far)]
+            return from_slots(me_ref, [own, swap(near, 1)] + moved, num, edges)[None]
 
         def my_index(ids):
             padded = jnp.pad(ids, (0, tp * rows - edges), constant_values=nodes)
             return lax.dynamic_slice(padded, (me * rows,), (rows,)) * 4
 
-        snd, rcv = my_index(senders), my_index(receivers)
+        def node_slots(val):
+            padded = jnp.pad(val, ((0, pad_nodes - nodes), (0, 0)))
+            val = padded.astype(F32)
+            far = swap(val, 2)
+            return [padded, swap(val, 1), far, swap(far, 1)]
+
+        def weight_slots(val):
+            far = swap(lax.dynamic_index_in_dim(val, half, 0, keepdims=False), 2)
+            rest = swap_dp(far)
+            return [val, swap(val, 1), far, rest, swap(far, 1), swap(rest, 1)]
 
         def pack(l, w1, w2):
             return jnp.concatenate([w1[l].reshape(-1, width), w2[l].T], axis=0).astype(F32)
 
         vecs = jnp.concatenate([edge_vec.reshape(-1), node_vec.reshape(-1)]).reshape(-1, width)
-        vecs = jnp.pad(vecs, ((0, 8 - vecs.shape[0]), (0, 0)))
-        group_a = jnp.concatenate([pack(0, edge_w1, edge_w2), vecs], axis=0)
-        group_b = jnp.concatenate([pack(0, node_w1, node_w2), pack(1, edge_w1, edge_w2), pack(1, node_w1, node_w2)], axis=0)
-        v_pad = jnp.pad(node_lat[0], ((0, pad_nodes - nodes), (0, 0)))
-        v_slots = slots_of(v_pad.astype(F32))
-        slots_a = slots_of(group_a)
-        x_slots = to_rows(edge_lat[0])
-        slots_b = slots_of(group_b)
-        g_slots = to_rows(grad_edge[0])
-        gn_pad = jnp.pad(grad_node[0], ((0, pad_nodes - nodes), (0, 0)))
-        gn_slots = slots_of(gn_pad.astype(F32))
-
-        mats_a = unpack_weights(slots_a, (0, 128, 256, 384))
-        mats_b = unpack_weights(slots_b, tuple(range(0, 1280, 128)))
-        ew, nw = [mats_a, mats_b[3:7]], [mats_b[:3], mats_b[7:]]
-        all_vec = jnp.stack([s[512:515].reshape(2, 2, 3, LANES) for s in slots_a], axis=3).reshape(2, 2, 3, width)
-        all_vec = jnp.pad(all_vec, ((0, 0), (0, 0), (0, 5), (0, 0)))
-        eb1 = [jnp.broadcast_to(edge_b1[l][None], (8, width)) for l in range(2)]
-        nb1 = [jnp.broadcast_to(node_b1[l][None], (8, width)) for l in range(2)]
-        nw1 = [jnp.stack(nw[l][:2]) for l in range(2)]
-
-        def chip_sum(pair_a, pair_b):
-            return pair_a + swap(pair_b, 1)
+        vecs = jnp.pad(vecs, ((0, 8 - len(vecs)), (0, 0)))
+        group_a = jnp.concatenate([pack(0, edge_w1, edge_w2).reshape(2, -1, width), jnp.stack([vecs, vecs])], axis=1)
+        group_b = jnp.concatenate([pack(0, node_w1, node_w2), pack(1, edge_w1, edge_w2), pack(1, node_w1, node_w2)])
+        v_slots = node_slots(node_lat[0])
+        slots_a = weight_slots(group_a)
+        x_slots = to_rows(edge_lat[0], IN_CUTS)
+        slots_b = weight_slots(group_b.reshape(2, -1, width))
+        g_slots = to_rows(grad_edge[0], GRAD_CUTS)
+        gn_slots = node_slots(grad_node[0])
+        snd, rcv = my_index(senders), my_index(receivers)
+
+        mats_a = unpack_weights(half_ref, slots_a, 2)
+        mats_b = unpack_weights(half_ref, slots_b, 5)
+        nv0, ns0, nt0, *edge_mats, nv1, ns1, nt1 = mats_b
+        own_a, near_a, far_a, _, cross_a, _ = slots_a
+        vec_rows = [s[2 * LANES:2 * LANES + 3].reshape(2, 2, 3, LANES) for s in (own_a[0], near_a[0], far_a, cross_a)]
+        (vec0, vec1), (nvec0, nvec1) = jnp.pad(jnp.concatenate(vec_rows, axis=-1), ((0, 0), (0, 0), (0, 5), (0, 0)))
+        (eb0, eb1), (nb0, nb1) = [jnp.broadcast_to(b[:, None], (2, 8, width)) for b in (edge_b1, node_b1)]
+        low = Layer(*mats_a, vec0, eb0, jnp.stack([nv0, ns0]), nt0, nvec0, nb0)
+        top = Layer(*edge_mats, vec1, eb1, jnp.stack([nv1, ns1]), nt1, nvec1, nb1)
 
         def all_sum(pair_a, pair_b):
-            chip = chip_sum(pair_a, pair_b)
+            chip = pair_a + swap(pair_b, 1)
             total = chip + swap(chip, 2)[::-1]
             return total, swap(total, 1)
 
         def own_sum(pair_a, pair_b):
-            chip = chip_sum(pair_a, pair_b)
+            chip = pair_a + swap(pair_b, 1)
             return chip[0] + swap(chip[1], 2)
 
-        v0, ps, pr = node_project(v_slots, ew[0][1], ew[0][2], eb1[0])
+        v0, ps, pr = node_project(v_slots, low.ws, low.wr, low.b1)
         hid0, nrm0, inv0, e1, sa, sb = edge_forward(
-            snd, rcv, x_slots, ps, pr, ew[0][0], ew[0][3], all_vec[0, 0], False, pad_nodes)
+            snd, rcv, x_slots, ps, pr, low.w1, low.w2t, low.vec, (), pad_nodes)
         sa, sb = all_sum(sa, sb)
         v1, s0, nhid, nnrm, ninv, ps, pr = node_forward(
-            v0, sa, sb, nw1[0], nw[0][2], all_vec[1, 0], nb1[0], ew[1][1], ew[1][2], eb1[1])
-        out1 = edge_forward(snd, rcv, [e1], ps, pr, ew[1][0], ew[1][3], all_vec[0, 1], True, pad_nodes)
-        hid1, nrm1, inv1 = out1[:3]
-        edge_out = to_columns(out1[3:7])
-        sa, sb = all_sum(*out1[7:])
-
-        v2, ds, dv, gn1, ndb1 = node_top(v1, sa, sb, [gn_pad] + list(gn_slots[1:]), nw1[1], nw[1][2], all_vec[1, 1], nb1[1])
+            v0, sa, sb, low.node_w1, low.node_w2t, low.node_vec, low.node_b1, top.ws, top.wr, top.b1)
+        hid1, nrm1, inv1, *parts, sa, sb = edge_forward(
+            snd, rcv, [e1], ps, pr, top.w1, top.w2t, top.vec, OUT_CUTS, pad_nodes)
+        edge_out = to_columns(parts, OUT_CUTS)
+        sa, sb = all_sum(sa, sb)
+
+        v2, ds, dv, gn1, ndb1 = node_top(
+            v1, sa, sb, gn_slots, top.node_w1, top.node_w2t, top.node_vec, top.node_b1)
         node_out = v2[:nodes][None]
 
         def mine_only(db1):
             lane = lax.broadcasted_iota(jnp.int32, db1.shape, 1)
             return jnp.broadcast_to(jnp.where(lane // LANES == me, db1, 0.0).sum(axis=0), db1.shape)
 
-        def edge_grad_sum(pair_a, pair_b):
-            own = own_sum(pair_a, pair_b)
-            return own + swap_dp(own)
-
         d_e1, dw1e, dw2t, small, ts, tr = edge_backward(
-            snd, rcv, g_slots, [e1], (hid1, nrm1, inv1), ds, ew[1][0], ew[1][3], all_vec[0, 1], True, pad_nodes)
-        da, db, ga1, gb1 = proj_backward(ts, tr, v1, ew[1][1], ew[1][2], dw1e, dw2t, small, mine_only(ndb1))
+            snd, rcv, g_slots, [e1], (hid1, nrm1, inv1), ds, top.w1, top.w2t, top.vec,
+            GRAD_CUTS, pad_nodes)
+        da, db, *ge1 = proj_backward(ts, tr, v1, top.ws, top.wr, dw1e, dw2t, small, mine_only(ndb1))
         da, db = all_sum(da, db)
         ds, dv_own, gn0, ndb1 = node_backward(
-            dv, da, db, v0, s0, (nhid, nnrm, ninv), nw1[0], nw[0][2], all_vec[1, 0])
+            dv, da, db, v0, s0, (nhid, nnrm, ninv), low.node_w1, low.node_w2t, low.node_vec)
         *d_slots, dw1e, dw2t, small, ts, tr = edge_backward(
-            snd, rcv, [d_e1], x_slots, (hid0, nrm0, inv0), ds, ew[0][0], ew[0][3], all_vec[0, 0], False, pad_nodes)
-        d_edge = to_columns(d_slots)
-        da, db, ga0, gb0 = proj_backward(ts, tr, v0, ew[0][1], ew[0][2], dw1e, dw2t, small, mine_only(ndb1))
+            snd, rcv, [d_e1], x_slots, (hid0, nrm0, inv0), ds, low.w1, low.w2t, low.vec,
+            (), pad_nodes)
+        d_edge = to_columns(d_slots, IN_CUTS)
+        da, db, *ge0 = proj_backward(ts, tr, v0, low.ws, low.wr, dw1e, dw2t, small, mine_only(ndb1))
         d_node = (dv_own + own_sum(da, db))[:nodes].astype(BF16)[None]
 
-        ge = [edge_grad_sum(ga0, gb0), edge_grad_sum(ga1, gb1)]
-        gn = [gn0 + swap_dp(gn0), gn1 + swap_dp(gn1)]
+        ge = [own_sum(*ge0), own_sum(*ge1)]
+        ge = [g + swap_dp(g) for g in ge]
+        gn = [g + swap_dp(g) for g in (gn0, gn1)]
         stack = lambda fn: jnp.stack([fn(l) for l in range(2)])
+        w1_rows, w2_rows, vec_wide = 3 * LANES, 4 * LANES, 3 * LANES
         return (node_out, edge_out, d_node, d_edge,
-                stack(lambda l: ge[l][:384].reshape(3, LANES, width)),
-                stack(lambda l: ge[l][513]),
-                stack(lambda l: ge[l][384:512].T),
-                stack(lambda l: ge[l][512, :384].reshape(3, LANES)),
-                stack(lambda l: gn[l][:256].reshape(2, LANES, width)),
-                stack(lambda l: ge[l][514]),
-                stack(lambda l: gn[l][256:384].T),
-                stack(lambda l: gn[l][384:, :384].sum(axis=0).reshape(3, LANES)))
+                stack(lambda l: ge[l][:w1_rows].reshape(3, LANES, width)),
+                stack(lambda l: ge[l][w2_rows + 1]),
+                stack(lambda l: ge[l][w1_rows:w2_rows].T),
+                stack(lambda l: ge[l][w2_rows, :vec_wide].reshape(3, LANES)),
+                stack(lambda l: gn[l][:2 * LANES].reshape(2, LANES, width)),
+                stack(lambda l: ge[l][w2_rows + 2]),
+                stack(lambda l: gn[l][2 * LANES:w1_rows].T),
+                stack(lambda l: gn[l][w1_rows:, :vec_wide].sum(axis=0).reshape(3, LANES)))
 
     return jax.shard_map(local_step, mesh=mesh, in_specs=in_specs, out_specs=out_specs, check_vma=False)

time: 1110 us -> 1120 us (level)
    ppermute x39 -> x47, waiting for transfers between devices: 636 us -> 605 us  [swap(): return lax.ppermute(val, 'tp', [(i, i ^ mask) for i in range(tp)])]
    ppermute x4 -> x6, waiting for transfers between devices: 40.6 us -> 70.8 us  [swap_dp(): return lax.ppermute(val, 'dp', [(0, 1), (1, 0)])]
    ppermute x39 -> x47, starting transfers between devices: 24.6 us -> 32.8 us  [swap(): return lax.ppermute(val, 'tp', [(i, i ^ mask) for i in range(tp)])]
  transfers between devices with their start and end apart: 43 -> 53, of which waited for: 21 -> 25; matrix products, arithmetic and copies ran while one was open for 5% -> 6% of each run, Pallas kernels for 14% -> 13%
where the time goes in v3:
time: 1120 us; the launch traced here: 1110 us
  waiting for transfers between devices  676 us (60%)
  Pallas kernels  303 us (27%)
  other arithmetic  49.4 us (4%)
  local copies, waits for them, and re-layouts  43.7 us (4%)
  starting transfers between devices  38.2 us (3%)
    ppermute x47, waiting for transfers between devices, swap(): return lax.ppermute(val, 'tp', [(i, i ^ mask) for i in range(tp)])  605 us
    pallas_call x2, Pallas kernels, edge_backward(): call(functools.partial(edge_bwd_body, len(xs), cuts, pad_nodes, copies),...  87.8 us
    pallas_call x2, Pallas kernels, edge_forward(): call(functools.partial(edge_fwd_body, len(xs), cuts, pad_nodes, copies),...  77.8 us
    ppermute x6, waiting for transfers between devices, swap_dp(): return lax.ppermute(val, 'dp', [(0, 1), (1, 0)])  70.8 us
    ppermute x47, starting transfers between devices, swap(): return lax.ppermute(val, 'tp', [(i, i ^ mask) for i in range(tp)])  32.8 us
    pallas_call x2, Pallas kernels, proj_backward(): call(proj_bwd_body, (nodes // NODE_BLK,), in_specs, out_specs, outs, scra...  31.5 us
    pallas_call x1, Pallas kernels, node_top(): call(node_top_body, (nodes // NODE_BLK,), in_specs, out_specs, outs, [])  23.2 us
  transfers between devices with their start and end apart: 53, of which 25 were waited for; matrix products, arithmetic and copies ran while one was open for 6% of the time, Pallas kernels for 13%

profile of v3, /device:TPU:0, one launch (start us, length us, event | category | flops | bytes accessed | tf_op | source)
XLA Modules:
  0.0 1110.8 jit_solution(15515886316956400568)
XLA Ops:
  8.1 3.3 collective-permute-start.4
  11.5 12.4 %collective-permute-done.4.refs_2_ = f32[264,512]{1,0:T(8,128)} collective-permute-done((f32[264,512]{1,0:T(8,128)S(1)}, f32[264,512]{1,0:T(8,128)}, u32[]{:S(2)}, u32[]{:S(2)}) %collective-permute-start.4) | collective-permute-done | bytes 540704 | tf_op jit(solution)/shard_map/ppermute | solution.py:633
  28.5 7.5 shard_map.231
  39.2 20.0 %collective-permute-done.1.v2_ref = f32[2576,128]{1,0:T(8,128)} collective-permute-done((f32[2576,128]{1,0:T(8,128)}, f32[2576,128]{1,0:T(8,128)}, u32[]{:S(2)}, u32[]{:S(2)}) %collective-permute-start.1) | collective-permute-done | bytes 1318944 | tf_op jit(solution)/shard_map/ppermute | solution.py:633
  66.8 3.8 shard_map.229
  71.9 10.6 shard_map.230
  82.6 32.8 %collective-permute-done.9.refs_2_.refs_3_ = f32[5120,128]{1,0:T(8,128)} collective-permute-done((f32[5120,128]{1,0:T(8,128)}, f32[5120,128]{1,0:T(8,128)}, u32[]{:S(2)}, u32[]{:S(2)}) %collective-permute-start.9) | collective-permute-done | bytes 2621472 | tf_op jit(solution)/shard_map/ppermute | solution.py:633
  115.3 52.9 %collective-permute-done.10.refs_3_.refs_4_ = f32[5120,128]{1,0:T(8,128)} collective-permute-done((f32[5120,128]{1,0:T(8,128)}, f32[5120,128]{1,0:T(8,128)}, u32[]{:S(2)}, u32[]{:S(2)}) %collective-permute-start.10) | collective-permute-done | bytes 2621472 | tf_op jit(solution)/shard_map/ppermute | solution.py:633
  168.3 40.7 %shard_map.232 = (f32[5120,512]{1,0:T(8,128)}, f32[5120,512]{1,0:T(8,128)}, f32[5120,128]{1,0:T(8,128)}, bf16[5120,512]{1,0:T(8,128)(2,1)}, f32[2,2576,128]{2,1,0:T(8,128)}, /*index=5*/f32[2,2576,128]{2,1,0:T(8,128)}) custom-call(s32[5120]{0:T(1024)} %get-tuple-element.232.snd_ref, s32[5120]{0:T(1024)} %get-tuple-element.233.rcv_ref, ...), custom_call_target="tpu_custom_call" | custom-call | flops 48000000000 | bytes 48000000 | tf_op jit(solution)/shard_map/pallas_call | solution.py:265
  209.8 4.8 collective-permute-done.11
  226.2 78.1 %collective-permute-done.15.refs_2_ = f32[640,512]{1,0:T(8,128)S(1)} collective-permute-done((f32[640,512]{1,0:T(8,128)S(1)}, f32[640,512]{1,0:T(8,128)S(1)}, u32[]{:S(2)}, u32[]{:S(2)}) %collective-permute-start.15) | collective-permute-done | bytes 1310752 | tf_op jit(solution)/shard_map/ppermute | solution.py:633
  304.9 3.5 reverse_add_fusion.2.sa_ref
  308.9 25.6 %collective-permute-done.16.refs_3_ = f32[640,512]{1,0:T(8,128)S(1)} collective-permute-done((f32[640,512]{1,0:T(8,128)S(1)}, f32[640,512]{1,0:T(8,128)S(1)}, u32[]{:S(2)}, u32[]{:S(2)}) %collective-permute-start.16) | collective-permute-done | bytes 1310752 | tf_op jit(solution)/shard_map/ppermute | solution.py:636
  337.7 7.3 shard_map.233
  345.0 2.3 pad_maximum_fusion.1.w1_ref
  349.2 16.1 %shard_map.234 = (bf16[2576,512]{1,0:T(8,128)(2,1)}, bf16[2576,512]{1,0:T(8,128)(2,1)}, f32[2576,512]{1,0:T(8,128)}, f32[2576,512]{1,0:T(8,128)}, f32[2576,128]{...) custom-call(bf16[2576,512]{1,0:T(8,128)(2,1)} %get-tuple-element.99.v_ref, ...), custom_call_target="tpu_custom_call" | custom-call | flops 4000000000 | bytes 4000000 | tf_op jit(solution)/shard_map/pallas_call | solution.py:439
  365.3 37.1 %shard_map.235 = (f32[5120,512]{1,0:T(8,128)}, f32[5120,512]{1,0:T(8,128)}, f32[5120,128]{1,0:T(8,128)}, bf16[5120,128]{1,0:T(8,128)(2,1)}, f32[5120,128]{1,0:T(...) custom-call(s32[5120]{0:T(1024)} %get-tuple-element.232.snd_ref, ...), custom_call_target="tpu_custom_call" | custom-call | flops 48000000000 | bytes 48000000 | tf_op jit(solution)/shard_map/pallas_call | solution.py:265
  402.9 4.8 collective-permute-done.19
  413.4 56.5 %collective-permute-done.20 = f32[2,2576,128]{2,1,0:T(8,128)S(1)} collective-permute-done((f32[2,2576,128]{2,1,0:T(8,128)S(1)}, f32[2,2576,128]{2,1,0:T(8,128)S(1)}, u32[]{:S(2)}, u32[]{:S(2)}) %collective-permute-start.20) | collective-permute-done | bytes 2637856 | tf_op jit(solution)/shard_map/ppermute | solution.py:633
  471.7 7.6 shard_map.238
  479.9 17.8 %collective-permute-done.23.g2_ref = f32[2576,128]{1,0:T(8,128)} collective-permute-done((f32[2576,128]{1,0:T(8,128)}, f32[2576,128]{1,0:T(8,128)}, u32[]{:S(2)}, u32[]{:S(2)}) %collective-permute-start.23) | collective-permute-done | bytes 1318944 | tf_op jit(solution)/shard_map/ppermute | solution.py:633
  499.3 13.1 %collective-permute-done.31.refs_2_ = f32[1024,128]{1,0:T(8,128)} collective-permute-done((f32[1024,128]{1,0:T(8,128)}, f32[1024,128]{1,0:T(8,128)}, u32[]{:S(2)}, u32[]{:S(2)}) %collective-permute-start.31) | collective-permute-done | bytes 524320 | tf_op jit(solution)/shard_map/ppermute | solution.py:633
  513.2 13.6 %collective-permute-done.34.refs_5_ = f32[1024,128]{1,0:T(8,128)} collective-permute-done((f32[1024,128]{1,0:T(8,128)}, f32[1024,128]{1,0:T(8,128)}, u32[]{:S(2)}, u32[]{:S(2)}) %collective-permute-start.34) | collective-permute-done | bytes 524320 | tf_op jit(solution)/shard_map/ppermute | solution.py:633
  531.4 2.3 pad_maximum_fusion.2.w1_ref
  534.3 23.2 %shard_map.236 = (bf16[2576,128]{1,0:T(8,128)(2,1)}, f32[10304,128]{1,0:T(8,128)}, f32[2576,512]{1,0:T(8,128)}, f32[392,512]{1,0:T(8,128)}, f32[8,512]{1,0:T(8,128)}) custom-call(bf16[2576,512]{1,0:T(8,128)(2,1)} %get-tuple-element.115.v_ref, f32[2,2576,128]{2,1,0:T(8,128)} %reverse_add_fusion.1.sa_ref, f32[2,2576,128]{2,1,0:T(8,128)} %collective-permute-done.21.sb_ref, ...), custom_call_target="tpu_custom_call" | custom-call | flops 4000000000 | bytes 4000000 | tf_op jit(solution)/shard_map/pallas_call | solution.py:478
  558.9 42.0 %collective-permute-done.32.refs_3_ = f32[1792,128]{1,0:T(8,128)} collective-permute-done((f32[1792,128]{1,0:T(8,128)}, f32[1792,128]{1,0:T(8,128)}, u32[]{:S(2)}, u32[]{:S(2)}) %collective-permute-start.32) | collective-permute-done | bytes 917536 | tf_op jit(solution)/shard_map/ppermute | solution.py:633
  600.9 18.0 %collective-permute-done.35.refs_6_ = f32[1792,128]{1,0:T(8,128)} collective-permute-done((f32[1792,128]{1,0:T(8,128)}, f32[1792,128]{1,0:T(8,128)}, u32[]{:S(2)}, u32[]{:S(2)}) %collective-permute-start.35) | collective-permute-done | bytes 917536 | tf_op jit(solution)/shard_map/ppermute | solution.py:633
  618.9 44.4 %shard_map.239 = (bf16[5120,512]{1,0:T(8,128)(2,1)}, f32[512,512]{1,0:T(8,128)}, f32[512,512]{1,0:T(8,128)}, f32[8,512]{1,0:T(8,128)}, bf16[2576,512]{1,0:T(8,128)(2,1)}, /*index=5*/bf16[2576,512]{1,0:T(8,128)(2,1)}) custom-call(s32[5120]{0:T(1024)} %get-tuple-element.232.snd_ref, s32[5120]{0:T(1024)} %get-tuple-element.233.rcv_ref, ...), custom_call_target="tpu_custom_call" | custom-call | flops 80000000000 | bytes 80000000 | tf_op jit(solution)/shard_map/pallas_call | solution.py:355
  664.5 15.8 %shard_map.240 = (f32[2,2576,128]{2,1,0:T(8,128)}, f32[2,2576,128]{2,1,0:T(8,128)}, f32[2,520,512]{2,1,0:T(8,128)}, f32[2,520,512]{2,1,0:T(8,128)}) custom-call(bf16[2576,512]{1,0:T(8,128)(2,1)} %get-tuple-element.146.ts_ref, bf16[2576,512]{1,0:T(8,128)(2,1)} %get-tuple-element.147.tr_ref, bf16[2576,512]{1,0:T(8,128)(2,1)} %get-tuple-element.115.v_ref, ...), custom_call_target="tpu_custom_call" | custom-call | flops 4000000000 | bytes 4000000 | tf_op jit(solution)/shard_map/pallas_call | solution.py:388
  681.0 4.8 collective-permute-done.37
  689.1 58.2 %collective-permute-done.38 = f32[2,2576,128]{2,1,0:T(8,128)S(1)} collective-permute-done((f32[2,2576,128]{2,1,0:T(8,128)S(1)}, f32[2,2576,128]{2,1,0:T(8,128)S(1)}, u32[]{:S(2)}, u32[]{:S(2)}) %collective-permute-start.38) | collective-permute-done | bytes 2637856 | tf_op jit(solution)/shard_map/ppermute | solution.py:633
  750.2 5.4 collective-permute-done.48
  761.2 17.8 %shard_map.241 = (f32[10304,128]{1,0:T(8,128)}, f32[2576,128]{1,0:T(8,128)}, f32[392,512]{1,0:T(8,128)}, f32[8,512]{1,0:T(8,128)}) custom-call(f32[2576,512]{1,0:T(8,128)} %get-tuple-element.133.dv_ref, f32[2,2576,128]{2,1,0:T(8,128)} %copy-done, f32[2,2576,128]{2,1,0:T(8,128)} %copy-done.5, bf16[2576,512]{1,0:T(8,128)(2,1)} %get-tuple-element.99.v_ref, ...), custom_call_target="tpu_custom_call" | custom-call | flops 4000000000 | bytes 4000000 | tf_op jit(solution)/shard_map/pallas_call | solution.py:499
  780.3 43.4 %shard_map.242 = (bf16[5120,128]{1,0:T(8,128)(2,1)}, f32[5120,128]{1,0:T(8,128)}, f32[5120,128]{1,0:T(8,128)}, f32[5120,128]{1,0:T(8,128)}, f32[512,512]{1,0:T(8...) custom-call(s32[5120]{0:T(1024)} %get-tuple-element.232.snd_ref, ...), custom_call_target="tpu_custom_call" | custom-call | flops 80000000000 | bytes 80000000 | tf_op jit(solution)/shard_map/pallas_call | solution.py:355
  825.1 15.7 %shard_map.243 = (f32[2,2576,128]{2,1,0:T(8,128)}, f32[2,2576,128]{2,1,0:T(8,128)}, f32[2,520,512]{2,1,0:T(8,128)}, f32[2,520,512]{2,1,0:T(8,128)}) custom-call(bf16[2576,512]{1,0:T(8,128)(2,1)} %get-tuple-element.164.ts_ref, bf16[2576,512]{1,0:T(8,128)(2,1)} %get-tuple-element.165.tr_ref, bf16[2576,512]{1,0:T(8,128)(2,1)} %get-tuple-element.99.v_ref, ...), custom_call_target="tpu_custom_call" | custom-call | flops 4000000000 | bytes 4000000 | tf_op jit(solution)/shard_map/pallas_call | solution.py:388
  840.8 22.4 %collective-permute-done.29.refs_5_ = f32[2048,128]{1,0:T(8,128)} collective-permute-done((f32[2048,128]{1,0:T(8,128)}, f32[2048,128]{1,0:T(8,128)}, u32[]{:S(2)}, u32[]{:S(2)}) %collective-permute-start.29) | collective-permute-done | bytes 1048608 | tf_op jit(solution)/shard_map/ppermute | solution.py:633
  864.2 22.1 %collective-permute-done.49 = f32[520,512]{1,0:T(8,128)} collective-permute-done((f32[520,512]{1,0:T(8,128)}, f32[520,512]{1,0:T(8,128)}, u32[]{:S(2)}, u32[]{:S(2)}) %collective-permute-start.49) | collective-permute-done | bytes 1064992 | tf_op jit(solution)/shard_map/ppermute | solution.py:633
  886.3 2.7 fusion.1
  891.1 5.8 shard_map.237
  899.4 10.7 collective-permute-done.52
  912.5 20.4 %collective-permute-done.50 = f32[520,512]{1,0:T(8,128)} collective-permute-done((f32[520,512]{1,0:T(8,128)}, f32[520,512]{1,0:T(8,128)}, u32[]{:S(2)}, u32[]{:S(2)}) %collective-permute-start.50) | collective-permute-done | bytes 1064992 | tf_op jit(solution)/shard_map/ppermute | solution.py:636
  936.0 13.5 %collective-permute-done.51 = f32[392,512]{1,0:T(8,128)S(1)} collective-permute-done((f32[392,512]{1,0:T(8,128)}, f32[392,512]{1,0:T(8,128)S(1)}, u32[]{:S(2)}, u32[]{:S(2)}) %collective-permute-start.51) | collective-permute-done | bytes 802848 | tf_op jit(solution)/shard_map/ppermute | solution.py:636
  953.1 2.2 add.86
  967.8 106.1 %collective-permute-done.46 = f32[520,512]{1,0:T(8,128)} collective-permute-done((f32[520,512]{1,0:T(8,128)}, f32[520,512]{1,0:T(8,128)}, u32[]{:S(2)}, u32[]{:S(2)}) %collective-permute-start.46) | collective-permute-done | bytes 1064992 | tf_op jit(solution)/shard_map/ppermute | solution.py:633
  1073.8 2.4 fusion.2
  1076.8 5.9 shard_map.244
  1082.7 18.9 %collective-permute-done.41 = f32[2576,128]{1,0:T(8,128)} collective-permute-done((f32[2576,128]{1,0:T(8,128)}, f32[2576,128]{1,0:T(8,128)}, u32[]{:S(2)}, u32[]{:S(2)}) %collective-permute-start.41) | collective-permute-done | bytes 1318944 | tf_op jit(solution)/shard_map/ppermute | solution.py:633
  1101.6 3.1 fusion.3
  (238 shorter events, 109.9 us)
Async XLA Ops:
  8.1 15.7 %collective-permute-start.4 = (f32[264,512]{1,0:T(8,128)S(1)}, f32[264,512]{1,0:T(8,128)}, u32[]{:S(2)}, u32[]{:S(2)}) collective-permute-start(f32[264,512]{1,0:T(8,128)S(1)} %dynamic-slice_bitcast_fusion.1), channel_id=1, source_target_pairs={{0,2},{1,3},{2,0},{3,1},{4,6},{5,7},{6,4},{7,5}} | collective-permute-start | bytes 1622024 | tf_op jit(solution)/shard_map/ppermute | solution.py:633
  11.5 25.1 %collective-permute-start.3 = (f32[2,264,512]{2,1,0:T(8,128)}, f32[2,264,512]{2,1,0:T(8,128)}, u32[]{:S(2)}, u32[]{:S(2)}) collective-permute-start(f32[2,264,512]{2,1,0:T(8,128)} %maximum_maximum_fusion.refs_0_), channel_id=1, source_target_pairs={{0,1},{1,0},{2,3},{3,2},{4,5},{5,4},{6,7},{7,6}} | collective-permute-start | bytes 3244040 | tf_op jit(solution)/shard_map/ppermute | solution.py:633
  23.9 13.8 %collective-permute-start.5 = (f32[264,512]{1,0:T(8,128)}, f32[264,512]{1,0:T(8,128)}, u32[]{:S(2)}, u32[]{:S(2)}) collective-permute-start(f32[264,512]{1,0:T(8,128)} %collective-permute-done.4.refs_2_), channel_id=1, source_target_pairs={{0,4},{4,0},{1,5},{5,1},{2,6},{6,2},{3,7},{7,3}} | collective-permute-start | bytes 1622024 | tf_op jit(solution)/shard_map/ppermute | solution.py:636
  27.0 32.1 %collective-permute-start.1 = (f32[2576,128]{1,0:T(8,128)}, f32[2576,128]{1,0:T(8,128)}, u32[]{:S(2)}, u32[]{:S(2)}) collective-permute-start(f32[2576,128]{1,0:T(8,128)} %get-tuple-element.216), channel_id=1, source_target_pairs={{0,2},{1,3},{2,0},{3,1},{4,6},{5,7},{6,4},{7,5}} | collective-permute-start | bytes 3956744 | tf_op jit(solution)/shard_map/ppermute | solution.py:633
  28.5 9.4 collective-permute-start.6
  36.0 46.5 %collective-permute-start.8 = (f32[5120,128]{1,0:T(8,128)}, f32[5120,128]{1,0:T(8,128)}, u32[]{:S(2)}, u32[]{:S(2)}) collective-permute-start(f32[5120,128]{1,0:T(8,128)} %get-tuple-element.101), channel_id=1, source_target_pairs={{0,1},{1,0},{2,3},{3,2},{4,5},{5,4},{6,7},{7,6}} | collective-permute-start | bytes 7864328 | tf_op jit(solution)/shard_map/ppermute | solution.py:633
  36.5 78.8 %collective-permute-start.9 = (f32[5120,128]{1,0:T(8,128)}, f32[5120,128]{1,0:T(8,128)}, u32[]{:S(2)}, u32[]{:S(2)}) collective-permute-start(f32[5120,128]{1,0:T(8,128)} %get-tuple-element.102), channel_id=1, source_target_pairs={{0,2},{1,3},{2,0},{3,1},{4,6},{5,7},{6,4},{7,5}} | collective-permute-start | bytes 7864328 | tf_op jit(solution)/shard_map/ppermute | solution.py:633
  37.6 130.7 %collective-permute-start.10 = (f32[5120,128]{1,0:T(8,128)}, f32[5120,128]{1,0:T(8,128)}, u32[]{:S(2)}, u32[]{:S(2)}) collective-permute-start(f32[5120,128]{1,0:T(8,128)} %get-tuple-element.103), channel_id=1, source_target_pairs={{0,3},{1,2},{2,1},{3,0},{4,7},{5,6},{6,5},{7,4}} | collective-permute-start | bytes 7864328 | tf_op jit(solution)/shard_map/ppermute | solution.py:633
  37.9 21.2 %collective-permute-start.7 = (f32[264,512]{1,0:T(8,128)}, f32[264,512]{1,0:T(8,128)S(1)}, u32[]{:S(2)}, u32[]{:S(2)}) collective-permute-start(f32[264,512]{1,0:T(8,128)} %collective-permute-done.5.refs_3_), channel_id=1, source_target_pairs={{0,1},{1,0},{2,3},{3,2},{4,5},{5,4},{6,7},{7,6}} | collective-permute-start | bytes 1622024 | tf_op jit(solution)/shard_map/ppermute | solution.py:633
  59.2 11.5 %collective-permute-start = (f32[2576,128]{1,0:T(8,128)}, f32[2576,128]{1,0:T(8,128)}, u32[]{:S(2)}, u32[]{:S(2)}) collective-permute-start(f32[2576,128]{1,0:T(8,128)} %get-tuple-element.216), channel_id=1, source_target_pairs={{0,1},{1,0},{2,3},{3,2},{4,5},{5,4},{6,7},{7,6}} | collective-permute-start | bytes 3956744 | tf_op jit(solution)/shard_map/ppermute | solution.py:633
  60.0 10.7 collective-permute-start.2
  216.7 88.1 %collective-permute-start.12 = (f32[2,2576,128]{2,1,0:T(8,128)S(1)}, f32[2,2576,128]{2,1,0:T(8,128)}, u32[]{:S(2)}, u32[]{:S(2)}) collective-permute-start(f32[2,2576,128]{2,1,0:T(8,128)S(1)} %add.77), channel_id=1, source_target_pairs={{0,2},{1,3},{2,0},{3,1},{4,6},{5,7},{6,4},{7,5}} | collective-permute-start | bytes 7913480 | tf_op jit(solution)/shard_map/ppermute | solution.py:633
  225.7 78.7 %collective-permute-start.15 = (f32[640,512]{1,0:T(8,128)S(1)}, f32[640,512]{1,0:T(8,128)S(1)}, u32[]{:S(2)}, u32[]{:S(2)}) collective-permute-start(f32[640,512]{1,0:T(8,128)S(1)} %dynamic-slice_bitcast_fusion), channel_id=1, source_target_pairs={{0,2},{1,3},{2,0},{3,1},{4,6},{5,7},{6,4},{7,5}} | collective-permute-start | bytes 3932168 | tf_op jit(solution)/shard_map/ppermute | solution.py:633
  226.2 109.0 %collective-permute-start.14 = (f32[2,640,512]{2,1,0:T(8,128)S(1)}, f32[2,640,512]{2,1,0:T(8,128)S(1)}, u32[]{:S(2)}, u32[]{:S(2)}) collective-permute-start(f32[2,640,512]{2,1,0:T(8,128)S(1)} %convert.7.refs_0_), channel_id=1, source_target_pairs={{0,1},{1,0},{2,3},{3,2},{4,5},{5,4},{6,7},{7,6}} | collective-permute-start | bytes 7864328 | tf_op jit(solution)/shard_map/ppermute | solution.py:633
  304.4 30.2 %collective-permute-start.16 = (f32[640,512]{1,0:T(8,128)S(1)}, f32[640,512]{1,0:T(8,128)S(1)}, u32[]{:S(2)}, u32[]{:S(2)}) collective-permute-start(f32[640,512]{1,0:T(8,128)S(1)} %collective-permute-done.15.refs_2_), channel_id=1, source_target_pairs={{0,4},{4,0},{1,5},{5,1},{2,6},{6,2},{3,7},{7,3}} | collective-permute-start | bytes 3932168 | tf_op jit(solution)/shard_map/ppermute | solution.py:636
  308.4 38.9 %collective-permute-start.13 = (f32[2,2576,128]{2,1,0:T(8,128)}, f32[2,2576,128]{2,1,0:T(8,128)}, u32[]{:S(2)}, u32[]{:S(2)}) collective-permute-start(f32[2,2576,128]{2,1,0:T(8,128)} %reverse_add_fusion.2.sa_ref), channel_id=1, source_target_pairs={{0,1},{1,0},{2,3},{3,2},{4,5},{5,4},{6,7},{7,6}} | collective-permute-start | bytes 7913480 | tf_op jit(solution)/shard_map/ppermute | solution.py:633
  308.4 28.3 %collective-permute-start.17 = (f32[640,512]{1,0:T(8,128)S(1)}, f32[640,512]{1,0:T(8,128)S(1)}, u32[]{:S(2)}, u32[]{:S(2)}) collective-permute-start(f32[640,512]{1,0:T(8,128)S(1)} %collective-permute-done.15.refs_2_), channel_id=1, source_target_pairs={{0,1},{1,0},{2,3},{3,2},{4,5},{5,4},{6,7},{7,6}} | collective-permute-start | bytes 3932168 | tf_op jit(solution)/shard_map/ppermute | solution.py:633
  409.8 60.1 %collective-permute-start.20 = (f32[2,2576,128]{2,1,0:T(8,128)S(1)}, f32[2,2576,128]{2,1,0:T(8,128)S(1)}, u32[]{:S(2)}, u32[]{:S(2)}) collective-permute-start(f32[2,2576,128]{2,1,0:T(8,128)S(1)} %add.79), channel_id=1, source_target_pairs={{0,2},{1,3},{2,0},{3,1},{4,6},{5,7},{6,4},{7,5}} | collective-permute-start | bytes 7913480 | tf_op jit(solution)/shard_map/ppermute | solution.py:633
  412.9 84.8 %collective-permute-start.23 = (f32[2576,128]{1,0:T(8,128)}, f32[2576,128]{1,0:T(8,128)}, u32[]{:S(2)}, u32[]{:S(2)}) collective-permute-start(f32[2576,128]{1,0:T(8,128)} %get-tuple-element.214), channel_id=1, source_target_pairs={{0,2},{1,3},{2,0},{3,1},{4,6},{5,7},{6,4},{7,5}} | collective-permute-start | bytes 3956744 | tf_op jit(solution)/shard_map/ppermute | solution.py:633
  471.7 57.9 %collective-permute-start.21 = (f32[2,2576,128]{2,1,0:T(8,128)}, f32[2,2576,128]{2,1,0:T(8,128)}, u32[]{:S(2)}, u32[]{:S(2)}) collective-permute-start(f32[2,2576,128]{2,1,0:T(8,128)} %reverse_add_fusion.1.sa_ref), channel_id=1, source_target_pairs={{0,1},{1,0},{2,3},{3,2},{4,5},{5,4},{6,7},{7,6}} | collective-permute-start | bytes 7913480 | tf_op jit(solution)/shard_map/ppermute | solution.py:633
  479.3 139.6 %collective-permute-start.30 = (f32[5120,128]{1,0:T(8,128)}, f32[5120,128]{1,0:T(8,128)}, u32[]{:S(2)}, u32[]{:S(2)}) collective-permute-start(f32[5120,128]{1,0:T(8,128)} %get-tuple-element.135), channel_id=1, source_target_pairs={{0,1},{1,0},{2,3},{3,2},{4,5},{5,4},{6,7},{7,6}} | collective-permute-start | bytes 7864328 | tf_op jit(solution)/shard_map/ppermute | solution.py:633
  479.8 48.4 %collective-permute-start.22 = (f32[2576,128]{1,0:T(8,128)}, f32[2576,128]{1,0:T(8,128)}, u32[]{:S(2)}, u32[]{:S(2)}) collective-permute-start(f32[2576,128]{1,0:T(8,128)} %get-tuple-element.214), channel_id=1, source_target_pairs={{0,1},{1,0},{2,3},{3,2},{4,5},{5,4},{6,7},{7,6}} | collective-permute-start | bytes 3956744 | tf_op jit(solution)/shard_map/ppermute | solution.py:633
  497.7 30.6 %collective-permute-start.24 = (f32[2576,128]{1,0:T(8,128)}, f32[2576,128]{1,0:T(8,128)}, u32[]{:S(2)}, u32[]{:S(2)}) collective-permute-start(f32[2576,128]{1,0:T(8,128)} %collective-permute-done.23.g2_ref), channel_id=1, source_target_pairs={{0,1},{1,0},{2,3},{3,2},{4,5},{5,4},{6,7},{7,6}} | collective-permute-start | bytes 3956744 | tf_op jit(solution)/shard_map/ppermute | solution.py:633
  497.7 14.7 %collective-permute-start.31 = (f32[1024,128]{1,0:T(8,128)}, f32[1024,128]{1,0:T(8,128)}, u32[]{:S(2)}, u32[]{:S(2)}) collective-permute-start(f32[1024,128]{1,0:T(8,128)} %get-tuple-element.136), channel_id=1, source_target_pairs={{0,2},{1,3},{2,0},{3,1},{4,6},{5,7},{6,4},{7,5}} | collective-permute-start | bytes 1572872 | tf_op jit(solution)/shard_map/ppermute | solution.py:633
  512.4 14.4 %collective-permute-start.34 = (f32[1024,128]{1,0:T(8,128)}, f32[1024,128]{1,0:T(8,128)}, u32[]{:S(2)}, u32[]{:S(2)}) collective-permute-start(f32[1024,128]{1,0:T(8,128)} %get-tuple-element.139), channel_id=1, source_target_pairs={{0,3},{1,2},{2,1},{3,0},{4,7},{5,6},{6,5},{7,4}} | collective-permute-start | bytes 1572872 | tf_op jit(solution)/shard_map/ppermute | solution.py:633
  526.8 92.1 %collective-permute-start.33 = (f32[2304,128]{1,0:T(8,128)}, f32[2304,128]{1,0:T(8,128)}, u32[]{:S(2)}, u32[]{:S(2)}) collective-permute-start(f32[2304,128]{1,0:T(8,128)} %get-tuple-element.138), channel_id=1, source_target_pairs={{0,2},{1,3},{2,0},{3,1},{4,6},{5,7},{6,4},{7,5}} | collective-permute-start | bytes 3538952 | tf_op jit(solution)/shard_map/ppermute | solution.py:633
  528.3 90.6 %collective-permute-start.36 = (f32[2304,128]{1,0:T(8,128)}, f32[2304,128]{1,0:T(8,128)}, u32[]{:S(2)}, u32[]{:S(2)}) collective-permute-start(f32[2304,128]{1,0:T(8,128)} %get-tuple-element.141), channel_id=1, source_target_pairs={{0,3},{1,2},{2,1},{3,0},{4,7},{5,6},{6,5},{7,4}} | collective-permute-start | bytes 3538952 | tf_op jit(solution)/shard_map/ppermute | solution.py:633
  528.3 72.6 %collective-permute-start.32 = (f32[1792,128]{1,0:T(8,128)}, f32[1792,128]{1,0:T(8,128)}, u32[]{:S(2)}, u32[]{:S(2)}) collective-permute-start(f32[1792,128]{1,0:T(8,128)} %get-tuple-element.137), channel_id=1, source_target_pairs={{0,2},{1,3},{2,0},{3,1},{4,6},{5,7},{6,4},{7,5}} | collective-permute-start | bytes 2752520 | tf_op jit(solution)/shard_map/ppermute | solution.py:633
  529.6 89.3 %collective-permute-start.35 = (f32[1792,128]{1,0:T(8,128)}, f32[1792,128]{1,0:T(8,128)}, u32[]{:S(2)}, u32[]{:S(2)}) collective-permute-start(f32[1792,128]{1,0:T(8,128)} %get-tuple-element.140), channel_id=1, source_target_pairs={{0,3},{1,2},{2,1},{3,0},{4,7},{5,6},{6,5},{7,4}} | collective-permute-start | bytes 2752520 | tf_op jit(solution)/shard_map/ppermute | solution.py:633
  687.8 59.5 %collective-permute-start.38 = (f32[2,2576,128]{2,1,0:T(8,128)S(1)}, f32[2,2576,128]{2,1,0:T(8,128)S(1)}, u32[]{:S(2)}, u32[]{:S(2)}) collective-permute-start(f32[2,2576,128]{2,1,0:T(8,128)S(1)} %add.81), channel_id=1, source_target_pairs={{0,2},{1,3},{2,0},{3,1},{4,6},{5,7},{6,4},{7,5}} | collective-permute-start | bytes 7913480 | tf_op jit(solution)/shard_map/ppermute | solution.py:633
  747.6 10.7 collective-permute-start.39
  748.2 30.9 %collective-permute-start.27 = (f32[2048,128]{1,0:T(8,128)}, f32[2048,128]{1,0:T(8,128)}, u32[]{:S(2)}, u32[]{:S(2)}) collective-permute-start(f32[2048,128]{1,0:T(8,128)} %get-tuple-element.130), channel_id=1, source_target_pairs={{0,2},{1,3},{2,0},{3,1},{4,6},{5,7},{6,4},{7,5}} | collective-permute-start | bytes 3145736 | tf_op jit(solution)/shard_map/ppermute | solution.py:633
  749.4 141.7 %collective-permute-start.25 = (f32[5120,128]{1,0:T(8,128)}, f32[5120,128]{1,0:T(8,128)}, u32[]{:S(2)}, u32[]{:S(2)}) collective-permute-start(f32[5120,128]{1,0:T(8,128)} %get-tuple-element.128), channel_id=1, source_target_pairs={{0,1},{1,0},{2,3},{3,2},{4,5},{5,4},{6,7},{7,6}} | collective-permute-start | bytes 7864328 | tf_op jit(solution)/shard_map/ppermute | solution.py:633
  749.4 139.6 %collective-permute-start.26 = (f32[3072,128]{1,0:T(8,128)}, f32[3072,128]{1,0:T(8,128)}, u32[]{:S(2)}, u32[]{:S(2)}) collective-permute-start(f32[3072,128]{1,0:T(8,128)} %get-tuple-element.129), channel_id=1, source_target_pairs={{0,2},{1,3},{2,0},{3,1},{4,6},{5,7},{6,4},{7,5}} | collective-permute-start | bytes 4718600 | tf_op jit(solution)/shard_map/ppermute | solution.py:633
  755.6 133.9 %collective-permute-start.28 = (f32[3072,128]{1,0:T(8,128)}, f32[3072,128]{1,0:T(8,128)}, u32[]{:S(2)}, u32[]{:S(2)}) collective-permute-start(f32[3072,128]{1,0:T(8,128)} %get-tuple-element.131), channel_id=1, source_target_pairs={{0,3},{1,2},{2,1},{3,0},{4,7},{5,6},{6,5},{7,4}} | collective-permute-start | bytes 4718600 | tf_op jit(solution)/shard_map/ppermute | solution.py:633
  760.5 102.7 %collective-permute-start.29 = (f32[2048,128]{1,0:T(8,128)}, f32[2048,128]{1,0:T(8,128)}, u32[]{:S(2)}, u32[]{:S(2)}) collective-permute-start(f32[2048,128]{1,0:T(8,128)} %get-tuple-element.132), channel_id=1, source_target_pairs={{0,3},{1,2},{2,1},{3,0},{4,7},{5,6},{6,5},{7,4}} | collective-permute-start | bytes 3145736 | tf_op jit(solution)/shard_map/ppermute | solution.py:633
  779.0 107.2 %collective-permute-start.49 = (f32[520,512]{1,0:T(8,128)}, f32[520,512]{1,0:T(8,128)}, u32[]{:S(2)}, u32[]{:S(2)}) collective-permute-start(f32[520,512]{1,0:T(8,128)} %slice_bitcast_fusion.2), channel_id=1, source_target_pairs={{0,2},{1,3},{2,0},{3,1},{4,6},{5,7},{6,4},{7,5}} | collective-permute-start | bytes 3194888 | tf_op jit(solution)/shard_map/ppermute | solution.py:633
  863.2 94.0 %collective-permute-start.40 = (f32[2,2576,128]{2,1,0:T(8,128)}, f32[2,2576,128]{2,1,0:T(8,128)}, u32[]{:S(2)}, u32[]{:S(2)}) collective-permute-start(f32[2,2576,128]{2,1,0:T(8,128)} %get-tuple-element.171), channel_id=1, source_target_pairs={{0,1},{1,0},{2,3},{3,2},{4,5},{5,4},{6,7},{7,6}} | collective-permute-start | bytes 7913480 | tf_op jit(solution)/shard_map/ppermute | solution.py:633
  886.3 66.8 %collective-permute-start.45 = (f32[2,520,512]{2,1,0:T(8,128)}, f32[2,520,512]{2,1,0:T(8,128)}, u32[]{:S(2)}, u32[]{:S(2)}) collective-permute-start(f32[2,520,512]{2,1,0:T(8,128)} %get-tuple-element.177), channel_id=1, source_target_pairs={{0,1},{1,0},{2,3},{3,2},{4,5},{5,4},{6,7},{7,6}} | collective-permute-start | bytes 6389768 | tf_op jit(solution)/shard_map/ppermute | solution.py:633
  889.0 21.1 %collective-permute-start.52 = (f32[392,512]{1,0:T(8,128)}, f32[392,512]{1,0:T(8,128)}, u32[]{:S(2)}, u32[]{:S(2)}) collective-permute-start(f32[392,512]{1,0:T(8,128)} %get-tuple-element.181), channel_id=1, source_target_pairs={{0,4},{4,0},{1,5},{5,1},{2,6},{6,2},{3,7},{7,3}} | collective-permute-start | bytes 2408456 | tf_op jit(solution)/shard_map/ppermute | solution.py:636
  889.6 43.4 %collective-permute-start.50 = (f32[520,512]{1,0:T(8,128)}, f32[520,512]{1,0:T(8,128)}, u32[]{:S(2)}, u32[]{:S(2)}) collective-permute-start(f32[520,512]{1,0:T(8,128)} %fusion.1), channel_id=1, source_target_pairs={{0,4},{4,0},{1,5},{5,1},{2,6},{6,2},{3,7},{7,3}} | collective-permute-start | bytes 3194888 | tf_op jit(solution)/shard_map/ppermute | solution.py:636
  896.9 52.7 %collective-permute-start.51 = (f32[392,512]{1,0:T(8,128)}, f32[392,512]{1,0:T(8,128)S(1)}, u32[]{:S(2)}, u32[]{:S(2)}) collective-permute-start(f32[392,512]{1,0:T(8,128)} %get-tuple-element.180), channel_id=1, source_target_pairs={{0,4},{4,0},{1,5},{5,1},{2,6},{6,2},{3,7},{7,3}} | collective-permute-start | bytes 2408456 | tf_op jit(solution)/shard_map/ppermute | solution.py:636
  934.7 142.1 %collective-permute-start.42 = (f32[5120,128]{1,0:T(8,128)}, f32[5120,128]{1,0:T(8,128)}, u32[]{:S(2)}, u32[]{:S(2)}) collective-permute-start(f32[5120,128]{1,0:T(8,128)} %get-tuple-element.173), channel_id=1, source_target_pairs={{0,1},{1,0},{2,3},{3,2},{4,5},{5,4},{6,7},{7,6}} | collective-permute-start | bytes 7864328 | tf_op jit(solution)/shard_map/ppermute | solution.py:633
  934.8 142.0 %collective-permute-start.43 = (f32[5120,128]{1,0:T(8,128)}, f32[5120,128]{1,0:T(8,128)}, u32[]{:S(2)}, u32[]{:S(2)}) collective-permute-start(f32[5120,128]{1,0:T(8,128)} %get-tuple-element.174), channel_id=1, source_target_pairs={{0,2},{1,3},{2,0},{3,1},{4,6},{5,7},{6,4},{7,5}} | collective-permute-start | bytes 7864328 | tf_op jit(solution)/shard_map/ppermute | solution.py:633
  949.6 127.2 %collective-permute-start.44 = (f32[5120,128]{1,0:T(8,128)}, f32[5120,128]{1,0:T(8,128)}, u32[]{:S(2)}, u32[]{:S(2)}) collective-permute-start(f32[5120,128]{1,0:T(8,128)} %get-tuple-element.175), channel_id=1, source_target_pairs={{0,3},{1,2},{2,1},{3,0},{4,7},{5,6},{6,5},{7,4}} | collective-permute-start | bytes 7864328 | tf_op jit(solution)/shard_map/ppermute | solution.py:633
  956.4 117.4 %collective-permute-start.46 = (f32[520,512]{1,0:T(8,128)}, f32[520,512]{1,0:T(8,128)}, u32[]{:S(2)}, u32[]{:S(2)}) collective-permute-start(f32[520,512]{1,0:T(8,128)} %slice_bitcast_fusion.4), channel_id=1, source_target_pairs={{0,2},{1,3},{2,0},{3,1},{4,6},{5,7},{6,4},{7,5}} | collective-permute-start | bytes 3194888 | tf_op jit(solution)/shard_map/ppermute | solution.py:633
  960.9 140.7 %collective-permute-start.41 = (f32[2576,128]{1,0:T(8,128)}, f32[2576,128]{1,0:T(8,128)}, u32[]{:S(2)}, u32[]{:S(2)}) collective-permute-start(f32[2576,128]{1,0:T(8,128)} %get-tuple-element.207), channel_id=1, source_target_pairs={{0,2},{1,3},{2,0},{3,1},{4,6},{5,7},{6,4},{7,5}} | collective-permute-start | bytes 3956744 | tf_op jit(solution)/shard_map/ppermute | solution.py:633
  1076.3 28.4 %collective-permute-start.47 = (f32[520,512]{1,0:T(8,128)}, f32[520,512]{1,0:T(8,128)}, u32[]{:S(2)}, u32[]{:S(2)}) collective-permute-start(f32[520,512]{1,0:T(8,128)} %fusion.2), channel_id=1, source_target_pairs={{0,4},{4,0},{1,5},{5,1},{2,6},{6,2},{3,7},{7,3}} | collective-permute-start | bytes 3194888 | tf_op jit(solution)/shard_map/ppermute | solution.py:636
  (38 other events, 575.8 us)

commit v4 on v3

--- a/solution.py
+++ b/solution.py
@@ -374,14 +374,14 @@
                 out[part * LANES:(part + 1) * LANES, :] = src[rows, :]
             vec_row = jnp.concatenate(
                 [small_ref[k:k + 1, rows] for k in range(3)] + [jnp.zeros((1, LANES), F32)], axis=-1)
-            out[512:520, :] = jnp.concatenate(
-                [vec_row, small_ref[3:4, :], node_b1_ref[0:1, :], jnp.zeros((5, wide(vec_row)), F32)], axis=0)
+            out[4 * LANES:, :] = jnp.concatenate(
+                [vec_row, small_ref[3:4, :], node_b1_ref[0:1, :], jnp.zeros((13, wide(vec_row)), F32)], axis=0)
 
 
 def proj_backward(ts, tr, v_full, w1s, w1r, dw1e, dw2t, small, node_b1):
     nodes, width = v_full.shape
     ins = [ts, tr, v_full, w1s, w1r, dw1e, dw2t, small, node_b1]
-    outs = [sds((2, nodes, LANES), F32)] * 2 + [sds((2, width + 8, width), F32)] * 2
+    outs = [sds((2, nodes, LANES), F32)] * 2 + [sds((2, width + 16, width), F32)] * 2
     in_specs = [rows_spec(NODE_BLK, width)] * 3 + [whole_spec(a.shape) for a in ins[3:]]
     out_specs = [pair_spec(NODE_BLK)] * 2 + [whole_spec(outs[2].shape)] * 2
     scratch = [pltpu.VMEM((width, width), F32)] * 2
@@ -603,8 +603,8 @@
 
 
 IN_CUTS = (20,)
-GRAD_CUTS = (4, 7, 9)
-OUT_CUTS = (12, 8)
+GRAD_CUTS = (4, 9, 7)
+OUT_CUTS = (11, 9)
 
 
 class Layer(NamedTuple):
@@ -739,8 +739,15 @@
         da, db, *ge0 = proj_backward(ts, tr, v0, low.ws, low.wr, dw1e, dw2t, small, mine_only(ndb1))
         d_node = (dv_own + own_sum(da, db))[:nodes].astype(BF16)[None]
 
-        ge = [own_sum(*ge0), own_sum(*ge1)]
-        ge = [g + swap_dp(g) for g in ge]
+        def grad_sum(pair_a, pair_b):
+            chip = (pair_a + swap(pair_b, 1)).reshape(2, 2, -1, width)
+            keep, give = [lax.dynamic_index_in_dim(chip, h, 1, keepdims=False) for h in (half, 1 - half)]
+            part = keep + swap_dp(give)
+            own = part[0] + swap(part[1], 2)
+            rest = swap_dp(own)
+            return jnp.concatenate([jnp.where(half == h, own, rest) for h in range(2)])
+
+        ge = [grad_sum(*ge0), grad_sum(*ge1)]
         gn = [g + swap_dp(g) for g in (gn0, gn1)]
         stack = lambda fn: jnp.stack([fn(l) for l in range(2)])
         w1_rows, w2_rows, vec_wide = 3 * LANES, 4 * LANES, 3 * LANES

time: 1120 us -> 1150 us (1.027)
  waiting for transfers between devices: 676 us -> 712 us
    ppermute x47, waiting for transfers between devices: 605 us -> 630 us  [swap(): return lax.ppermute(val, 'tp', [(i, i ^ mask) for i in range(tp)])]
    ppermute x6 -> x8, waiting for transfers between devices: 70.8 us -> 81.3 us  [swap_dp(): return lax.ppermute(val, 'dp', [(0, 1), (1, 0)])]
  transfers between devices with their start and end apart: 53 -> 55, of which waited for: 25 -> 28; matrix products, arithmetic and copies ran while one was open for 6% -> 5% of each run, Pallas kernels for 13% -> 13%
where the time goes in v4:
time: 1150 us; the launch traced here: 1140 us
  waiting for transfers between devices  712 us (62%)
  Pallas kernels  303 us (26%)
  local copies, waits for them, and re-layouts  44.5 us (4%)
  other arithmetic  43.7 us (4%)
  starting transfers between devices  39.1 us (3%)
    ppermute x47, waiting for transfers between devices, swap(): return lax.ppermute(val, 'tp', [(i, i ^ mask) for i in range(tp)])  630 us
    pallas_call x2, Pallas kernels, edge_backward(): call(functools.partial(edge_bwd_body, len(xs), cuts, pad_nodes, copies),...  87.8 us
    ppermute x8, waiting for transfers between devices, swap_dp(): return lax.ppermute(val, 'dp', [(0, 1), (1, 0)])  81.3 us
    pallas_call x2, Pallas kernels, edge_forward(): call(functools.partial(edge_fwd_body, len(xs), cuts, pad_nodes, copies),...  77.9 us
    pallas_call x2, Pallas kernels, proj_backward(): call(proj_bwd_body, (nodes // NODE_BLK,), in_specs, out_specs, outs, scra...  31.6 us
    ppermute x47, starting transfers between devices, swap(): return lax.ppermute(val, 'tp', [(i, i ^ mask) for i in range(tp)])  30.6 us
    pallas_call x1, Pallas kernels, node_top(): call(node_top_body, (nodes // NODE_BLK,), in_specs, out_specs, outs, [])  23.2 us
  transfers between devices with their start and end apart: 55, of which 28 were waited for; matrix products, arithmetic and copies ran while one was open for 5% of the time, Pallas kernels for 13%

profile of v4, /device:TPU:0, one launch (start us, length us, event | category | flops | bytes accessed | tf_op | source)
XLA Modules:
  0.0 1143.2 jit_solution(10341321897557284395)
XLA Ops:
  8.2 3.3 collective-permute-start.4
  11.5 12.4 %collective-permute-done.4.refs_2_ = f32[264,512]{1,0:T(8,128)} collective-permute-done((f32[264,512]{1,0:T(8,128)S(1)}, f32[264,512]{1,0:T(8,128)}, u32[]{:S(2)}, u32[]{:S(2)}) %collective-permute-start.4) | collective-permute-done | bytes 540704 | tf_op jit(solution)/shard_map/ppermute | solution.py:633
  28.6 7.5 shard_map.231
  39.2 20.0 %collective-permute-done.1.v2_ref = f32[2576,128]{1,0:T(8,128)} collective-permute-done((f32[2576,128]{1,0:T(8,128)}, f32[2576,128]{1,0:T(8,128)}, u32[]{:S(2)}, u32[]{:S(2)}) %collective-permute-start.1) | collective-permute-done | bytes 1318944 | tf_op jit(solution)/shard_map/ppermute | solution.py:633
  66.8 3.8 shard_map.229
  71.9 10.6 shard_map.230
  82.6 32.8 %collective-permute-done.9.refs_2_.refs_3_ = f32[5120,128]{1,0:T(8,128)} collective-permute-done((f32[5120,128]{1,0:T(8,128)}, f32[5120,128]{1,0:T(8,128)}, u32[]{:S(2)}, u32[]{:S(2)}) %collective-permute-start.9) | collective-permute-done | bytes 2621472 | tf_op jit(solution)/shard_map/ppermute | solution.py:633
  115.4 52.9 %collective-permute-done.10.refs_3_.refs_4_ = f32[5120,128]{1,0:T(8,128)} collective-permute-done((f32[5120,128]{1,0:T(8,128)}, f32[5120,128]{1,0:T(8,128)}, u32[]{:S(2)}, u32[]{:S(2)}) %collective-permute-start.10) | collective-permute-done | bytes 2621472 | tf_op jit(solution)/shard_map/ppermute | solution.py:633
  168.3 40.8 %shard_map.232 = (f32[5120,512]{1,0:T(8,128)}, f32[5120,512]{1,0:T(8,128)}, f32[5120,128]{1,0:T(8,128)}, bf16[5120,512]{1,0:T(8,128)(2,1)}, f32[2,2576,128]{2,1,0:T(8,128)}, /*index=5*/f32[2,2576,128]{2,1,0:T(8,128)}) custom-call(s32[5120]{0:T(1024)} %get-tuple-element.236.snd_ref, s32[5120]{0:T(1024)} %get-tuple-element.237.rcv_ref, ...), custom_call_target="tpu_custom_call" | custom-call | flops 48000000000 | bytes 48000000 | tf_op jit(solution)/shard_map/pallas_call | solution.py:265
  209.9 4.8 collective-permute-done.11
  226.3 78.1 %collective-permute-done.15.refs_2_ = f32[640,512]{1,0:T(8,128)S(1)} collective-permute-done((f32[640,512]{1,0:T(8,128)S(1)}, f32[640,512]{1,0:T(8,128)S(1)}, u32[]{:S(2)}, u32[]{:S(2)}) %collective-permute-start.15) | collective-permute-done | bytes 1310752 | tf_op jit(solution)/shard_map/ppermute | solution.py:633
  305.0 3.5 reverse_add_fusion.2.sa_ref
  309.0 25.6 %collective-permute-done.16.refs_3_ = f32[640,512]{1,0:T(8,128)S(1)} collective-permute-done((f32[640,512]{1,0:T(8,128)S(1)}, f32[640,512]{1,0:T(8,128)S(1)}, u32[]{:S(2)}, u32[]{:S(2)}) %collective-permute-start.16) | collective-permute-done | bytes 1310752 | tf_op jit(solution)/shard_map/ppermute | solution.py:636
  337.9 7.3 shard_map.233
  345.2 2.3 pad_maximum_fusion.1.w1_ref
  350.0 16.1 %shard_map.234 = (bf16[2576,512]{1,0:T(8,128)(2,1)}, bf16[2576,512]{1,0:T(8,128)(2,1)}, f32[2576,512]{1,0:T(8,128)}, f32[2576,512]{1,0:T(8,128)}, f32[2576,128]{...) custom-call(bf16[2576,512]{1,0:T(8,128)(2,1)} %get-tuple-element.99.v_ref, ...), custom_call_target="tpu_custom_call" | custom-call | flops 4000000000 | bytes 4000000 | tf_op jit(solution)/shard_map/pallas_call | solution.py:439
  366.2 37.1 %shard_map.235 = (f32[5120,512]{1,0:T(8,128)}, f32[5120,512]{1,0:T(8,128)}, f32[5120,128]{1,0:T(8,128)}, bf16[5120,128]{1,0:T(8,128)(2,1)}, f32[5120,128]{1,0:T(...) custom-call(s32[5120]{0:T(1024)} %get-tuple-element.236.snd_ref, ...), custom_call_target="tpu_custom_call" | custom-call | flops 48000000000 | bytes 48000000 | tf_op jit(solution)/shard_map/pallas_call | solution.py:265
  403.7 4.8 collective-permute-done.19
  414.1 56.6 %collective-permute-done.20 = f32[2,2576,128]{2,1,0:T(8,128)S(1)} collective-permute-done((f32[2,2576,128]{2,1,0:T(8,128)S(1)}, f32[2,2576,128]{2,1,0:T(8,128)S(1)}, u32[]{:S(2)}, u32[]{:S(2)}) %collective-permute-start.20) | collective-permute-done | bytes 2637856 | tf_op jit(solution)/shard_map/ppermute | solution.py:633
  472.5 7.6 shard_map.238
  480.7 17.9 %collective-permute-done.23.g2_ref = f32[2576,128]{1,0:T(8,128)} collective-permute-done((f32[2576,128]{1,0:T(8,128)}, f32[2576,128]{1,0:T(8,128)}, u32[]{:S(2)}, u32[]{:S(2)}) %collective-permute-start.23) | collective-permute-done | bytes 1318944 | tf_op jit(solution)/shard_map/ppermute | solution.py:633
  500.1 13.1 %collective-permute-done.31.refs_2_ = f32[1024,128]{1,0:T(8,128)} collective-permute-done((f32[1024,128]{1,0:T(8,128)}, f32[1024,128]{1,0:T(8,128)}, u32[]{:S(2)}, u32[]{:S(2)}) %collective-permute-start.31) | collective-permute-done | bytes 524320 | tf_op jit(solution)/shard_map/ppermute | solution.py:633
  514.0 13.6 %collective-permute-done.34.refs_5_ = f32[1024,128]{1,0:T(8,128)} collective-permute-done((f32[1024,128]{1,0:T(8,128)}, f32[1024,128]{1,0:T(8,128)}, u32[]{:S(2)}, u32[]{:S(2)}) %collective-permute-start.34) | collective-permute-done | bytes 524320 | tf_op jit(solution)/shard_map/ppermute | solution.py:633
  532.2 2.3 pad_maximum_fusion.2.w1_ref
  535.8 23.2 %shard_map.236 = (bf16[2576,128]{1,0:T(8,128)(2,1)}, f32[10304,128]{1,0:T(8,128)}, f32[2576,512]{1,0:T(8,128)}, f32[392,512]{1,0:T(8,128)}, f32[8,512]{1,0:T(8,128)}) custom-call(bf16[2576,512]{1,0:T(8,128)(2,1)} %get-tuple-element.115.v_ref, f32[2,2576,128]{2,1,0:T(8,128)} %reverse_add_fusion.1.sa_ref, f32[2,2576,128]{2,1,0:T(8,128)} %collective-permute-done.21.sb_ref, ...), custom_call_target="tpu_custom_call" | custom-call | flops 4000000000 | bytes 4000000 | tf_op jit(solution)/shard_map/pallas_call | solution.py:478
  560.3 41.4 %collective-permute-done.33.refs_4_ = f32[1792,128]{1,0:T(8,128)} collective-permute-done((f32[1792,128]{1,0:T(8,128)}, f32[1792,128]{1,0:T(8,128)}, u32[]{:S(2)}, u32[]{:S(2)}) %collective-permute-start.33) | collective-permute-done | bytes 917536 | tf_op jit(solution)/shard_map/ppermute | solution.py:633
  601.7 18.0 %collective-permute-done.36.refs_7_ = f32[1792,128]{1,0:T(8,128)} collective-permute-done((f32[1792,128]{1,0:T(8,128)}, f32[1792,128]{1,0:T(8,128)}, u32[]{:S(2)}, u32[]{:S(2)}) %collective-permute-start.36) | collective-permute-done | bytes 917536 | tf_op jit(solution)/shard_map/ppermute | solution.py:633
  619.6 44.4 %shard_map.239 = (bf16[5120,512]{1,0:T(8,128)(2,1)}, f32[512,512]{1,0:T(8,128)}, f32[512,512]{1,0:T(8,128)}, f32[8,512]{1,0:T(8,128)}, bf16[2576,512]{1,0:T(8,128)(2,1)}, /*index=5*/bf16[2576,512]{1,0:T(8,128)(2,1)}) custom-call(s32[5120]{0:T(1024)} %get-tuple-element.236.snd_ref, s32[5120]{0:T(1024)} %get-tuple-element.237.rcv_ref, ...), custom_call_target="tpu_custom_call" | custom-call | flops 80000000000 | bytes 80000000 | tf_op jit(solution)/shard_map/pallas_call | solution.py:355
  665.3 15.9 %shard_map.240 = (f32[2,2576,128]{2,1,0:T(8,128)}, f32[2,2576,128]{2,1,0:T(8,128)}, f32[2,528,512]{2,1,0:T(8,128)}, f32[2,528,512]{2,1,0:T(8,128)}) custom-call(bf16[2576,512]{1,0:T(8,128)(2,1)} %get-tuple-element.146.ts_ref, bf16[2576,512]{1,0:T(8,128)(2,1)} %get-tuple-element.147.tr_ref, bf16[2576,512]{1,0:T(8,128)(2,1)} %get-tuple-element.115.v_ref, ...), custom_call_target="tpu_custom_call" | custom-call | flops 4000000000 | bytes 4000000 | tf_op jit(solution)/shard_map/pallas_call | solution.py:388
  681.8 4.8 collective-permute-done.37
  692.4 56.5 %collective-permute-done.38 = f32[2,2576,128]{2,1,0:T(8,128)S(1)} collective-permute-done((f32[2,2576,128]{2,1,0:T(8,128)S(1)}, f32[2,2576,128]{2,1,0:T(8,128)S(1)}, u32[]{:S(2)}, u32[]{:S(2)}) %collective-permute-start.38) | collective-permute-done | bytes 2637856 | tf_op jit(solution)/shard_map/ppermute | solution.py:633
  750.8 23.5 %collective-permute-done.27.refs_3_ = f32[2304,128]{1,0:T(8,128)S(1)} collective-permute-done((f32[2304,128]{1,0:T(8,128)S(1)}, f32[2304,128]{1,0:T(8,128)S(1)}, u32[]{:S(2)}, u32[]{:S(2)}) %collective-permute-start.27) | collective-permute-done | bytes 1179680 | tf_op jit(solution)/shard_map/ppermute | solution.py:633
  780.3 18.2 %collective-permute-done.29.refs_5_ = f32[2304,128]{1,0:T(8,128)} collective-permute-done((f32[2304,128]{1,0:T(8,128)S(1)}, f32[2304,128]{1,0:T(8,128)}, u32[]{:S(2)}, u32[]{:S(2)}) %collective-permute-start.29) | collective-permute-done | bytes 1179680 | tf_op jit(solution)/shard_map/ppermute | solution.py:633
  799.0 31.5 %collective-permute-done.26.refs_2_ = f32[2816,128]{1,0:T(8,128)} collective-permute-done((f32[2816,128]{1,0:T(8,128)}, f32[2816,128]{1,0:T(8,128)}, u32[]{:S(2)}, u32[]{:S(2)}) %collective-permute-start.26) | collective-permute-done | bytes 1441824 | tf_op jit(solution)/shard_map/ppermute | solution.py:633
  830.5 29.7 %collective-permute-done.28.refs_4_ = f32[2816,128]{1,0:T(8,128)} collective-permute-done((f32[2816,128]{1,0:T(8,128)}, f32[2816,128]{1,0:T(8,128)}, u32[]{:S(2)}, u32[]{:S(2)}) %collective-permute-start.28) | collective-permute-done | bytes 1441824 | tf_op jit(solution)/shard_map/ppermute | solution.py:633
  860.2 5.8 shard_map.237
  871.5 17.8 %shard_map.241 = (f32[10304,128]{1,0:T(8,128)}, f32[2576,128]{1,0:T(8,128)}, f32[392,512]{1,0:T(8,128)}, f32[8,512]{1,0:T(8,128)}) custom-call(f32[2576,512]{1,0:T(8,128)} %get-tuple-element.133.dv_ref, f32[2,2576,128]{2,1,0:T(8,128)} %reverse_add_fusion.ta_ref, f32[2,2576,128]{2,1,0:T(8,128)} %collective-permute-done.39.tb_ref, ...), custom_call_target="tpu_custom_call" | custom-call | flops 4000000000 | bytes 4000000 | tf_op jit(solution)/shard_map/pallas_call | solution.py:499
  889.4 43.4 %shard_map.242 = (bf16[5120,128]{1,0:T(8,128)(2,1)}, f32[5120,128]{1,0:T(8,128)}, f32[5120,128]{1,0:T(8,128)}, f32[5120,128]{1,0:T(8,128)}, f32[512,512]{1,0:T(8...) custom-call(s32[5120]{0:T(1024)} %get-tuple-element.236.snd_ref, ...), custom_call_target="tpu_custom_call" | custom-call | flops 80000000000 | bytes 80000000 | tf_op jit(solution)/shard_map/pallas_call | solution.py:355
  934.1 15.7 %shard_map.243 = (f32[2,2576,128]{2,1,0:T(8,128)}, f32[2,2576,128]{2,1,0:T(8,128)}, f32[2,528,512]{2,1,0:T(8,128)}, f32[2,528,512]{2,1,0:T(8,128)}) custom-call(bf16[2576,512]{1,0:T(8,128)(2,1)} %get-tuple-element.164.ts_ref, bf16[2576,512]{1,0:T(8,128)(2,1)} %get-tuple-element.165.tr_ref, bf16[2576,512]{1,0:T(8,128)(2,1)} %get-tuple-element.99.v_ref, ...), custom_call_target="tpu_custom_call" | custom-call | flops 4000000000 | bytes 4000000 | tf_op jit(solution)/shard_map/pallas_call | solution.py:388
  956.8 9.6 collective-permute-done.52
  968.9 14.2 %collective-permute-done.53 = f32[392,512]{1,0:T(8,128)S(1)} collective-permute-done((f32[392,512]{1,0:T(8,128)S(1)}, f32[392,512]{1,0:T(8,128)S(1)}, u32[]{:S(2)}, u32[]{:S(2)}) %collective-permute-start.53) | collective-permute-done | bytes 802848 | tf_op jit(solution)/shard_map/ppermute | solution.py:636
  990.1 21.8 %collective-permute-done.46 = f32[2,264,512]{2,1,0:T(8,128)S(1)} collective-permute-done((f32[2,264,512]{2,1,0:T(8,128)S(1)}, f32[2,264,512]{2,1,0:T(8,128)S(1)}, u32[]{:S(2)}, u32[]{:S(2)}) %collective-permute-start.46) | collective-permute-done | bytes 1081376 | tf_op jit(solution)/shard_map/ppermute | solution.py:636
  1017.8 10.3 collective-permute-done.43.refs_2_
  1028.1 55.2 %collective-permute-done.44.refs_3_ = f32[5120,128]{1,0:T(8,128)} collective-permute-done((f32[5120,128]{1,0:T(8,128)}, f32[5120,128]{1,0:T(8,128)}, u32[]{:S(2)}, u32[]{:S(2)}) %collective-permute-start.44) | collective-permute-done | bytes 2621472 | tf_op jit(solution)/shard_map/ppermute | solution.py:633
  1083.4 5.9 shard_map.244
  1089.3 34.4 %collective-permute-done.47 = f32[264,512]{1,0:T(8,128)} collective-permute-done((f32[264,512]{1,0:T(8,128)}, f32[264,512]{1,0:T(8,128)}, u32[]{:S(2)}, u32[]{:S(2)}) %collective-permute-start.47) | collective-permute-done | bytes 540704 | tf_op jit(solution)/shard_map/ppermute | solution.py:633
  1126.5 2.7 fusion.1
  1129.3 9.6 collective-permute-done.48
  (251 shorter events, 113.8 us)
Async XLA Ops:
  8.2 15.7 %collective-permute-start.4 = (f32[264,512]{1,0:T(8,128)S(1)}, f32[264,512]{1,0:T(8,128)}, u32[]{:S(2)}, u32[]{:S(2)}) collective-permute-start(f32[264,512]{1,0:T(8,128)S(1)} %dynamic-slice_bitcast_fusion.3), channel_id=1, source_target_pairs={{0,2},{1,3},{2,0},{3,1},{4,6},{5,7},{6,4},{7,5}} | collective-permute-start | bytes 1622024 | tf_op jit(solution)/shard_map/ppermute | solution.py:633
  11.5 25.1 %collective-permute-start.3 = (f32[2,264,512]{2,1,0:T(8,128)}, f32[2,264,512]{2,1,0:T(8,128)}, u32[]{:S(2)}, u32[]{:S(2)}) collective-permute-start(f32[2,264,512]{2,1,0:T(8,128)} %maximum_maximum_fusion.refs_0_), channel_id=1, source_target_pairs={{0,1},{1,0},{2,3},{3,2},{4,5},{5,4},{6,7},{7,6}} | collective-permute-start | bytes 3244040 | tf_op jit(solution)/shard_map/ppermute | solution.py:633
  23.9 13.8 %collective-permute-start.5 = (f32[264,512]{1,0:T(8,128)}, f32[264,512]{1,0:T(8,128)}, u32[]{:S(2)}, u32[]{:S(2)}) collective-permute-start(f32[264,512]{1,0:T(8,128)} %collective-permute-done.4.refs_2_), channel_id=1, source_target_pairs={{0,4},{4,0},{1,5},{5,1},{2,6},{6,2},{3,7},{7,3}} | collective-permute-start | bytes 1622024 | tf_op jit(solution)/shard_map/ppermute | solution.py:636
  27.1 32.1 %collective-permute-start.1 = (f32[2576,128]{1,0:T(8,128)}, f32[2576,128]{1,0:T(8,128)}, u32[]{:S(2)}, u32[]{:S(2)}) collective-permute-start(f32[2576,128]{1,0:T(8,128)} %get-tuple-element.216), channel_id=1, source_target_pairs={{0,2},{1,3},{2,0},{3,1},{4,6},{5,7},{6,4},{7,5}} | collective-permute-start | bytes 3956744 | tf_op jit(solution)/shard_map/ppermute | solution.py:633
  36.1 46.5 %collective-permute-start.8 = (f32[5120,128]{1,0:T(8,128)}, f32[5120,128]{1,0:T(8,128)}, u32[]{:S(2)}, u32[]{:S(2)}) collective-permute-start(f32[5120,128]{1,0:T(8,128)} %get-tuple-element.101), channel_id=1, source_target_pairs={{0,1},{1,0},{2,3},{3,2},{4,5},{5,4},{6,7},{7,6}} | collective-permute-start | bytes 7864328 | tf_op jit(solution)/shard_map/ppermute | solution.py:633
  36.6 78.7 %collective-permute-start.9 = (f32[5120,128]{1,0:T(8,128)}, f32[5120,128]{1,0:T(8,128)}, u32[]{:S(2)}, u32[]{:S(2)}) collective-permute-start(f32[5120,128]{1,0:T(8,128)} %get-tuple-element.102), channel_id=1, source_target_pairs={{0,2},{1,3},{2,0},{3,1},{4,6},{5,7},{6,4},{7,5}} | collective-permute-start | bytes 7864328 | tf_op jit(solution)/shard_map/ppermute | solution.py:633
  37.6 130.7 %collective-permute-start.10 = (f32[5120,128]{1,0:T(8,128)}, f32[5120,128]{1,0:T(8,128)}, u32[]{:S(2)}, u32[]{:S(2)}) collective-permute-start(f32[5120,128]{1,0:T(8,128)} %get-tuple-element.103), channel_id=1, source_target_pairs={{0,3},{1,2},{2,1},{3,0},{4,7},{5,6},{6,5},{7,4}} | collective-permute-start | bytes 7864328 | tf_op jit(solution)/shard_map/ppermute | solution.py:633
  38.0 21.2 %collective-permute-start.7 = (f32[264,512]{1,0:T(8,128)}, f32[264,512]{1,0:T(8,128)S(1)}, u32[]{:S(2)}, u32[]{:S(2)}) collective-permute-start(f32[264,512]{1,0:T(8,128)} %collective-permute-done.5.refs_3_), channel_id=1, source_target_pairs={{0,1},{1,0},{2,3},{3,2},{4,5},{5,4},{6,7},{7,6}} | collective-permute-start | bytes 1622024 | tf_op jit(solution)/shard_map/ppermute | solution.py:633
  216.8 88.2 %collective-permute-start.12 = (f32[2,2576,128]{2,1,0:T(8,128)S(1)}, f32[2,2576,128]{2,1,0:T(8,128)}, u32[]{:S(2)}, u32[]{:S(2)}) collective-permute-start(f32[2,2576,128]{2,1,0:T(8,128)S(1)} %add.85), channel_id=1, source_target_pairs={{0,2},{1,3},{2,0},{3,1},{4,6},{5,7},{6,4},{7,5}} | collective-permute-start | bytes 7913480 | tf_op jit(solution)/shard_map/ppermute | solution.py:633
  225.8 78.7 %collective-permute-start.15 = (f32[640,512]{1,0:T(8,128)S(1)}, f32[640,512]{1,0:T(8,128)S(1)}, u32[]{:S(2)}, u32[]{:S(2)}) collective-permute-start(f32[640,512]{1,0:T(8,128)S(1)} %dynamic-slice_bitcast_fusion), channel_id=1, source_target_pairs={{0,2},{1,3},{2,0},{3,1},{4,6},{5,7},{6,4},{7,5}} | collective-permute-start | bytes 3932168 | tf_op jit(solution)/shard_map/ppermute | solution.py:633
  226.3 109.0 %collective-permute-start.14 = (f32[2,640,512]{2,1,0:T(8,128)S(1)}, f32[2,640,512]{2,1,0:T(8,128)S(1)}, u32[]{:S(2)}, u32[]{:S(2)}) collective-permute-start(f32[2,640,512]{2,1,0:T(8,128)S(1)} %convert.7.refs_0_), channel_id=1, source_target_pairs={{0,1},{1,0},{2,3},{3,2},{4,5},{5,4},{6,7},{7,6}} | collective-permute-start | bytes 7864328 | tf_op jit(solution)/shard_map/ppermute | solution.py:633
  304.4 30.2 %collective-permute-start.16 = (f32[640,512]{1,0:T(8,128)S(1)}, f32[640,512]{1,0:T(8,128)S(1)}, u32[]{:S(2)}, u32[]{:S(2)}) collective-permute-start(f32[640,512]{1,0:T(8,128)S(1)} %collective-permute-done.15.refs_2_), channel_id=1, source_target_pairs={{0,4},{4,0},{1,5},{5,1},{2,6},{6,2},{3,7},{7,3}} | collective-permute-start | bytes 3932168 | tf_op jit(solution)/shard_map/ppermute | solution.py:636
  308.5 39.0 %collective-permute-start.13 = (f32[2,2576,128]{2,1,0:T(8,128)}, f32[2,2576,128]{2,1,0:T(8,128)}, u32[]{:S(2)}, u32[]{:S(2)}) collective-permute-start(f32[2,2576,128]{2,1,0:T(8,128)} %reverse_add_fusion.2.sa_ref), channel_id=1, source_target_pairs={{0,1},{1,0},{2,3},{3,2},{4,5},{5,4},{6,7},{7,6}} | collective-permute-start | bytes 7913480 | tf_op jit(solution)/shard_map/ppermute | solution.py:633
  308.5 28.3 %collective-permute-start.17 = (f32[640,512]{1,0:T(8,128)S(1)}, f32[640,512]{1,0:T(8,128)S(1)}, u32[]{:S(2)}, u32[]{:S(2)}) collective-permute-start(f32[640,512]{1,0:T(8,128)S(1)} %collective-permute-done.15.refs_2_), channel_id=1, source_target_pairs={{0,1},{1,0},{2,3},{3,2},{4,5},{5,4},{6,7},{7,6}} | collective-permute-start | bytes 3932168 | tf_op jit(solution)/shard_map/ppermute | solution.py:633
  410.6 60.1 %collective-permute-start.20 = (f32[2,2576,128]{2,1,0:T(8,128)S(1)}, f32[2,2576,128]{2,1,0:T(8,128)S(1)}, u32[]{:S(2)}, u32[]{:S(2)}) collective-permute-start(f32[2,2576,128]{2,1,0:T(8,128)S(1)} %add.87), channel_id=1, source_target_pairs={{0,2},{1,3},{2,0},{3,1},{4,6},{5,7},{6,4},{7,5}} | collective-permute-start | bytes 7913480 | tf_op jit(solution)/shard_map/ppermute | solution.py:633
  413.7 84.8 %collective-permute-start.23 = (f32[2576,128]{1,0:T(8,128)}, f32[2576,128]{1,0:T(8,128)}, u32[]{:S(2)}, u32[]{:S(2)}) collective-permute-start(f32[2576,128]{1,0:T(8,128)} %get-tuple-element.214), channel_id=1, source_target_pairs={{0,2},{1,3},{2,0},{3,1},{4,6},{5,7},{6,4},{7,5}} | collective-permute-start | bytes 3956744 | tf_op jit(solution)/shard_map/ppermute | solution.py:633
  472.5 57.9 %collective-permute-start.21 = (f32[2,2576,128]{2,1,0:T(8,128)}, f32[2,2576,128]{2,1,0:T(8,128)}, u32[]{:S(2)}, u32[]{:S(2)}) collective-permute-start(f32[2,2576,128]{2,1,0:T(8,128)} %reverse_add_fusion.1.sa_ref), channel_id=1, source_target_pairs={{0,1},{1,0},{2,3},{3,2},{4,5},{5,4},{6,7},{7,6}} | collective-permute-start | bytes 7913480 | tf_op jit(solution)/shard_map/ppermute | solution.py:633
  480.1 139.6 %collective-permute-start.30 = (f32[5120,128]{1,0:T(8,128)}, f32[5120,128]{1,0:T(8,128)}, u32[]{:S(2)}, u32[]{:S(2)}) collective-permute-start(f32[5120,128]{1,0:T(8,128)} %get-tuple-element.135), channel_id=1, source_target_pairs={{0,1},{1,0},{2,3},{3,2},{4,5},{5,4},{6,7},{7,6}} | collective-permute-start | bytes 7864328 | tf_op jit(solution)/shard_map/ppermute | solution.py:633
  480.6 48.5 %collective-permute-start.22 = (f32[2576,128]{1,0:T(8,128)}, f32[2576,128]{1,0:T(8,128)}, u32[]{:S(2)}, u32[]{:S(2)}) collective-permute-start(f32[2576,128]{1,0:T(8,128)} %get-tuple-element.214), channel_id=1, source_target_pairs={{0,1},{1,0},{2,3},{3,2},{4,5},{5,4},{6,7},{7,6}} | collective-permute-start | bytes 3956744 | tf_op jit(solution)/shard_map/ppermute | solution.py:633
  498.5 30.6 %collective-permute-start.24 = (f32[2576,128]{1,0:T(8,128)}, f32[2576,128]{1,0:T(8,128)}, u32[]{:S(2)}, u32[]{:S(2)}) collective-permute-start(f32[2576,128]{1,0:T(8,128)} %collective-permute-done.23.g2_ref), channel_id=1, source_target_pairs={{0,1},{1,0},{2,3},{3,2},{4,5},{5,4},{6,7},{7,6}} | collective-permute-start | bytes 3956744 | tf_op jit(solution)/shard_map/ppermute | solution.py:633
  498.5 14.7 %collective-permute-start.31 = (f32[1024,128]{1,0:T(8,128)}, f32[1024,128]{1,0:T(8,128)}, u32[]{:S(2)}, u32[]{:S(2)}) collective-permute-start(f32[1024,128]{1,0:T(8,128)} %get-tuple-element.136), channel_id=1, source_target_pairs={{0,2},{1,3},{2,0},{3,1},{4,6},{5,7},{6,4},{7,5}} | collective-permute-start | bytes 1572872 | tf_op jit(solution)/shard_map/ppermute | solution.py:633
  513.2 14.4 %collective-permute-start.34 = (f32[1024,128]{1,0:T(8,128)}, f32[1024,128]{1,0:T(8,128)}, u32[]{:S(2)}, u32[]{:S(2)}) collective-permute-start(f32[1024,128]{1,0:T(8,128)} %get-tuple-element.139), channel_id=1, source_target_pairs={{0,3},{1,2},{2,1},{3,0},{4,7},{5,6},{6,5},{7,4}} | collective-permute-start | bytes 1572872 | tf_op jit(solution)/shard_map/ppermute | solution.py:633
  527.6 92.1 %collective-permute-start.32 = (f32[2304,128]{1,0:T(8,128)}, f32[2304,128]{1,0:T(8,128)}, u32[]{:S(2)}, u32[]{:S(2)}) collective-permute-start(f32[2304,128]{1,0:T(8,128)} %get-tuple-element.137), channel_id=1, source_target_pairs={{0,2},{1,3},{2,0},{3,1},{4,6},{5,7},{6,4},{7,5}} | collective-permute-start | bytes 3538952 | tf_op jit(solution)/shard_map/ppermute | solution.py:633
  529.1 90.5 %collective-permute-start.35 = (f32[2304,128]{1,0:T(8,128)}, f32[2304,128]{1,0:T(8,128)}, u32[]{:S(2)}, u32[]{:S(2)}) collective-permute-start(f32[2304,128]{1,0:T(8,128)} %get-tuple-element.140), channel_id=1, source_target_pairs={{0,3},{1,2},{2,1},{3,0},{4,7},{5,6},{6,5},{7,4}} | collective-permute-start | bytes 3538952 | tf_op jit(solution)/shard_map/ppermute | solution.py:633
  529.1 72.5 %collective-permute-start.33 = (f32[1792,128]{1,0:T(8,128)}, f32[1792,128]{1,0:T(8,128)}, u32[]{:S(2)}, u32[]{:S(2)}) collective-permute-start(f32[1792,128]{1,0:T(8,128)} %get-tuple-element.138), channel_id=1, source_target_pairs={{0,2},{1,3},{2,0},{3,1},{4,6},{5,7},{6,4},{7,5}} | collective-permute-start | bytes 2752520 | tf_op jit(solution)/shard_map/ppermute | solution.py:633
  530.4 89.2 %collective-permute-start.36 = (f32[1792,128]{1,0:T(8,128)}, f32[1792,128]{1,0:T(8,128)}, u32[]{:S(2)}, u32[]{:S(2)}) collective-permute-start(f32[1792,128]{1,0:T(8,128)} %get-tuple-element.141), channel_id=1, source_target_pairs={{0,3},{1,2},{2,1},{3,0},{4,7},{5,6},{6,5},{7,4}} | collective-permute-start | bytes 2752520 | tf_op jit(solution)/shard_map/ppermute | solution.py:633
  688.9 60.1 %collective-permute-start.38 = (f32[2,2576,128]{2,1,0:T(8,128)S(1)}, f32[2,2576,128]{2,1,0:T(8,128)S(1)}, u32[]{:S(2)}, u32[]{:S(2)}) collective-permute-start(f32[2,2576,128]{2,1,0:T(8,128)S(1)} %add.89), channel_id=1, source_target_pairs={{0,2},{1,3},{2,0},{3,1},{4,6},{5,7},{6,4},{7,5}} | collective-permute-start | bytes 7913480 | tf_op jit(solution)/shard_map/ppermute | solution.py:633
  690.2 85.4 %collective-permute-start.49 = (f32[2,528,512]{2,1,0:T(8,128)S(1)}, f32[2,528,512]{2,1,0:T(8,128)}, u32[]{:S(2)}, u32[]{:S(2)}) collective-permute-start(f32[2,528,512]{2,1,0:T(8,128)S(1)} %copy-done.26), channel_id=1, source_target_pairs={{0,1},{1,0},{2,3},{3,2},{4,5},{5,4},{6,7},{7,6}} | collective-permute-start | bytes 6488072 | tf_op jit(solution)/shard_map/ppermute | solution.py:633
  690.3 84.0 %collective-permute-start.27 = (f32[2304,128]{1,0:T(8,128)S(1)}, f32[2304,128]{1,0:T(8,128)S(1)}, u32[]{:S(2)}, u32[]{:S(2)}) collective-permute-start(f32[2304,128]{1,0:T(8,128)S(1)} %copy-done.31), channel_id=1, source_target_pairs={{0,2},{1,3},{2,0},{3,1},{4,6},{5,7},{6,4},{7,5}} | collective-permute-start | bytes 3538952 | tf_op jit(solution)/shard_map/ppermute | solution.py:633
  691.0 169.2 %collective-permute-start.25 = (f32[5120,128]{1,0:T(8,128)}, f32[5120,128]{1,0:T(8,128)}, u32[]{:S(2)}, u32[]{:S(2)}) collective-permute-start(f32[5120,128]{1,0:T(8,128)} %get-tuple-element.128), channel_id=1, source_target_pairs={{0,1},{1,0},{2,3},{3,2},{4,5},{5,4},{6,7},{7,6}} | collective-permute-start | bytes 7864328 | tf_op jit(solution)/shard_map/ppermute | solution.py:633
  691.2 107.3 %collective-permute-start.29 = (f32[2304,128]{1,0:T(8,128)S(1)}, f32[2304,128]{1,0:T(8,128)}, u32[]{:S(2)}, u32[]{:S(2)}) collective-permute-start(f32[2304,128]{1,0:T(8,128)S(1)} %copy-done.30), channel_id=1, source_target_pairs={{0,3},{1,2},{2,1},{3,0},{4,7},{5,6},{6,5},{7,4}} | collective-permute-start | bytes 3538952 | tf_op jit(solution)/shard_map/ppermute | solution.py:633
  750.8 120.8 %collective-permute-start.39 = (f32[2,2576,128]{2,1,0:T(8,128)}, f32[2,2576,128]{2,1,0:T(8,128)}, u32[]{:S(2)}, u32[]{:S(2)}) collective-permute-start(f32[2,2576,128]{2,1,0:T(8,128)} %reverse_add_fusion.ta_ref), channel_id=1, source_target_pairs={{0,1},{1,0},{2,3},{3,2},{4,5},{5,4},{6,7},{7,6}} | collective-permute-start | bytes 7913480 | tf_op jit(solution)/shard_map/ppermute | solution.py:633
  774.3 56.3 %collective-permute-start.26 = (f32[2816,128]{1,0:T(8,128)}, f32[2816,128]{1,0:T(8,128)}, u32[]{:S(2)}, u32[]{:S(2)}) collective-permute-start(f32[2816,128]{1,0:T(8,128)} %get-tuple-element.129), channel_id=1, source_target_pairs={{0,2},{1,3},{2,0},{3,1},{4,6},{5,7},{6,4},{7,5}} | collective-permute-start | bytes 4325384 | tf_op jit(solution)/shard_map/ppermute | solution.py:633
  775.6 84.7 %collective-permute-start.28 = (f32[2816,128]{1,0:T(8,128)}, f32[2816,128]{1,0:T(8,128)}, u32[]{:S(2)}, u32[]{:S(2)}) collective-permute-start(f32[2816,128]{1,0:T(8,128)} %get-tuple-element.131), channel_id=1, source_target_pairs={{0,3},{1,2},{2,1},{3,0},{4,7},{5,6},{6,5},{7,4}} | collective-permute-start | bytes 4325384 | tf_op jit(solution)/shard_map/ppermute | solution.py:633
  798.4 68.2 %collective-permute-start.50 = (f32[2,264,512]{2,1,0:T(8,128)}, f32[2,264,512]{2,1,0:T(8,128)}, u32[]{:S(2)}, u32[]{:S(2)}) collective-permute-start(f32[2,264,512]{2,1,0:T(8,128)} %dynamic-slice_bitcast_fusion.1), channel_id=1, source_target_pairs={{0,4},{4,0},{1,5},{5,1},{2,6},{6,2},{3,7},{7,3}} | collective-permute-start | bytes 3244040 | tf_op jit(solution)/shard_map/ppermute | solution.py:636
  866.1 88.8 %collective-permute-start.54 = (f32[392,512]{1,0:T(8,128)}, f32[392,512]{1,0:T(8,128)}, u32[]{:S(2)}, u32[]{:S(2)}) collective-permute-start(f32[392,512]{1,0:T(8,128)} %get-tuple-element.181), channel_id=1, source_target_pairs={{0,4},{4,0},{1,5},{5,1},{2,6},{6,2},{3,7},{7,3}} | collective-permute-start | bytes 2408456 | tf_op jit(solution)/shard_map/ppermute | solution.py:636
  870.3 79.6 %collective-permute-start.51 = (f32[264,512]{1,0:T(8,128)}, f32[264,512]{1,0:T(8,128)}, u32[]{:S(2)}, u32[]{:S(2)}) collective-permute-start(f32[264,512]{1,0:T(8,128)} %slice_bitcast_fusion.3), channel_id=1, source_target_pairs={{0,2},{1,3},{2,0},{3,1},{4,6},{5,7},{6,4},{7,5}} | collective-permute-start | bytes 1622024 | tf_op jit(solution)/shard_map/ppermute | solution.py:633
  949.9 34.8 %collective-permute-start.45 = (f32[2,528,512]{2,1,0:T(8,128)}, f32[2,528,512]{2,1,0:T(8,128)S(1)}, u32[]{:S(2)}, u32[]{:S(2)}) collective-permute-start(f32[2,528,512]{2,1,0:T(8,128)} %get-tuple-element.177), channel_id=1, source_target_pairs={{0,1},{1,0},{2,3},{3,2},{4,5},{5,4},{6,7},{7,6}} | collective-permute-start | bytes 6488072 | tf_op jit(solution)/shard_map/ppermute | solution.py:633
  951.3 15.2 %collective-permute-start.52 = (f32[264,512]{1,0:T(8,128)S(1)}, f32[264,512]{1,0:T(8,128)S(1)}, u32[]{:S(2)}, u32[]{:S(2)}) collective-permute-start(f32[264,512]{1,0:T(8,128)S(1)} %fusion.2), channel_id=1, source_target_pairs={{0,4},{4,0},{1,5},{5,1},{2,6},{6,2},{3,7},{7,3}} | collective-permute-start | bytes 1622024 | tf_op jit(solution)/shard_map/ppermute | solution.py:636
  952.8 34.0 %collective-permute-start.40 = (f32[2,2576,128]{2,1,0:T(8,128)}, f32[2,2576,128]{2,1,0:T(8,128)S(1)}, u32[]{:S(2)}, u32[]{:S(2)}) collective-permute-start(f32[2,2576,128]{2,1,0:T(8,128)} %get-tuple-element.171), channel_id=1, source_target_pairs={{0,1},{1,0},{2,3},{3,2},{4,5},{5,4},{6,7},{7,6}} | collective-permute-start | bytes 7913480 | tf_op jit(solution)/shard_map/ppermute | solution.py:633
  956.2 26.9 %collective-permute-start.53 = (f32[392,512]{1,0:T(8,128)S(1)}, f32[392,512]{1,0:T(8,128)S(1)}, u32[]{:S(2)}, u32[]{:S(2)}) collective-permute-start(f32[392,512]{1,0:T(8,128)S(1)} %copy-done.13), channel_id=1, source_target_pairs={{0,4},{4,0},{1,5},{5,1},{2,6},{6,2},{3,7},{7,3}} | collective-permute-start | bytes 2408456 | tf_op jit(solution)/shard_map/ppermute | solution.py:636
  968.1 49.8 %collective-permute-start.42 = (f32[5120,128]{1,0:T(8,128)}, f32[5120,128]{1,0:T(8,128)}, u32[]{:S(2)}, u32[]{:S(2)}) collective-permute-start(f32[5120,128]{1,0:T(8,128)} %get-tuple-element.173), channel_id=1, source_target_pairs={{0,1},{1,0},{2,3},{3,2},{4,5},{5,4},{6,7},{7,6}} | collective-permute-start | bytes 7864328 | tf_op jit(solution)/shard_map/ppermute | solution.py:633
  968.1 60.1 %collective-permute-start.43 = (f32[5120,128]{1,0:T(8,128)}, f32[5120,128]{1,0:T(8,128)}, u32[]{:S(2)}, u32[]{:S(2)}) collective-permute-start(f32[5120,128]{1,0:T(8,128)} %get-tuple-element.174), channel_id=1, source_target_pairs={{0,2},{1,3},{2,0},{3,1},{4,6},{5,7},{6,4},{7,5}} | collective-permute-start | bytes 7864328 | tf_op jit(solution)/shard_map/ppermute | solution.py:633
  983.1 100.3 %collective-permute-start.44 = (f32[5120,128]{1,0:T(8,128)}, f32[5120,128]{1,0:T(8,128)}, u32[]{:S(2)}, u32[]{:S(2)}) collective-permute-start(f32[5120,128]{1,0:T(8,128)} %get-tuple-element.175), channel_id=1, source_target_pairs={{0,3},{1,2},{2,1},{3,0},{4,7},{5,6},{6,5},{7,4}} | collective-permute-start | bytes 7864328 | tf_op jit(solution)/shard_map/ppermute | solution.py:633
  985.3 26.6 %collective-permute-start.46 = (f32[2,264,512]{2,1,0:T(8,128)S(1)}, f32[2,264,512]{2,1,0:T(8,128)S(1)}, u32[]{:S(2)}, u32[]{:S(2)}) collective-permute-start(f32[2,264,512]{2,1,0:T(8,128)S(1)} %dynamic-slice_bitcast_fusion.2), channel_id=1, source_target_pairs={{0,4},{4,0},{1,5},{5,1},{2,6},{6,2},{3,7},{7,3}} | collective-permute-start | bytes 3244040 | tf_op jit(solution)/shard_map/ppermute | solution.py:636
  988.9 137.7 %collective-permute-start.41 = (f32[2576,128]{1,0:T(8,128)}, f32[2576,128]{1,0:T(8,128)}, u32[]{:S(2)}, u32[]{:S(2)}) collective-permute-start(f32[2576,128]{1,0:T(8,128)} %get-tuple-element.207), channel_id=1, source_target_pairs={{0,2},{1,3},{2,0},{3,1},{4,6},{5,7},{6,4},{7,5}} | collective-permute-start | bytes 3956744 | tf_op jit(solution)/shard_map/ppermute | solution.py:633
  1013.9 109.7 %collective-permute-start.47 = (f32[264,512]{1,0:T(8,128)}, f32[264,512]{1,0:T(8,128)}, u32[]{:S(2)}, u32[]{:S(2)}) collective-permute-start(f32[264,512]{1,0:T(8,128)} %slice_bitcast_fusion.5), channel_id=1, source_target_pairs={{0,2},{1,3},{2,0},{3,1},{4,6},{5,7},{6,4},{7,5}} | collective-permute-start | bytes 1622024 | tf_op jit(solution)/shard_map/ppermute | solution.py:633
  1125.0 13.8 %collective-permute-start.48 = (f32[264,512]{1,0:T(8,128)S(1)}, f32[264,512]{1,0:T(8,128)S(1)}, u32[]{:S(2)}, u32[]{:S(2)}) collective-permute-start(f32[264,512]{1,0:T(8,128)S(1)} %fusion.3), channel_id=1, source_target_pairs={{0,4},{4,0},{1,5},{5,1},{2,6},{6,2},{3,7},{7,3}} | collective-permute-start | bytes 1622024 | tf_op jit(solution)/shard_map/ppermute | solution.py:636
  (42 other events, 506.0 us)
